TPU v7x, 32 devices: a whole 2x2x4 slice. The times are simulated.
32 devices in a mesh: dp: 8 (over z, x), mp: 4 (over y, core).
Axes of the slice: x: 2, y: 2, z: 4, core: 2. Of those that a mesh axis runs over, the one named last changes fastest.
Arguments:
- media: bfloat16 [64, 256, 1536], P('dp', None, 'mp'), may hold values from -6 to 6
- time_table: bfloat16 [8, 1536], P(None, 'mp'), may hold values from -4 to 4
- doc_images: int32 [16], P('dp'), may hold values from 0 to 8, as said below
- plan: int32 [8, 8], P('dp'), may hold values from -1 to 19, as said below
- latents: bfloat16 [64, 1536], replicated, may hold values from -6 to 6
- queries: bfloat16 [64, 1024], P(None, 'mp'), may hold values from -450 to 450
- key_weight: bfloat16 [1536, 1024], P(None, 'mp'), may hold values from -0.15625 to 0.15625
- value_weight: bfloat16 [1536, 1024], P(None, 'mp'), may hold values from -0.15625 to 0.15625
- out_weight: bfloat16 [1024, 1536], P('mp'), may hold values from -0.1875 to 0.1875
- cotangent: bfloat16 [32, 64, 1536], P('dp', None, 'mp'), may hold values from -6 to 6
Outputs:
- resampled: bfloat16 [32, 64, 1536], P('dp', None, 'mp')
- key_grad: float32 [1536, 1024], P('dp', 'mp')
- value_grad: float32 [1536, 1024], P('dp', 'mp')
Inputs may be any that keep to these rules, and one draw needn't show every extreme that they name: `doc_images`: A device's documents fill its image slots from slot 0 in document order and hold 8 images or fewer together; some document holds exactly 8. `plan`: entry s of device d's row is -1 exactly when slot s holds no image, else k * 4 + w with k from 0 to 4 and d + k a device of dp: the image goes to work slot w of device d + k. Each work slot receives at most one image; a device sends at most one image for each k from 1 to 4; some device sends one for every such k and fills its own 4 work slots.
All inputs are finite; a program needn't handle non-finite values.
Results may differ from a plain program's by a relative error of at most 0.0096.
Values may be sent and summed in bfloat16 or wider, within the bound.
No kernel may reach another device: no remote copies, remote signals or barrier semaphores. Data moves between devices by JAX's collectives and lax.ppermute only.
A program may use at most 64 MiB of HBM per device.

v0:
```python
import functools

import jax
import jax.numpy as jnp
from jax import lax
from jax.experimental import pallas as pl
from jax.experimental.pallas import tpu as pltpu
from jax.sharding import PartitionSpec as P


HEAD = 64
MARK_ROWS = 16
VMEM_BYTES = 67043328
norm_epsilon = 1e-05
f32 = jnp.float32
bf16 = jnp.bfloat16
VMEM = pl.BlockSpec(memory_space=pltpu.VMEM)
SMEM = pl.BlockSpec(memory_space=pltpu.SMEM)
HBM = pl.BlockSpec(memory_space=pltpu.HBM)


def from_behind(block, axis, distance):
    devices = range(lax.axis_size(axis))
    route = [(i - distance, i) for i in devices if i - distance in devices]
    return lax.ppermute(block, axis, route)


def flip(block, axis, bit):
    return lax.ppermute(block, axis, [(i, i ^ bit) for i in range(lax.axis_size(axis))])


class Chain:
    def __init__(self):
        self.token = None

    def call(
        self,
        body,
        outs,
        in_specs,
        out_specs,
        args,
        scratch=(),
        flops=0,
        moved=0,
        limit=8,
        aliases=None,
        full=False,
        spare=0,
    ):
        has = self.token is not None
        limit_bytes = limit << 20
        if full:
            held = sum(
                o.size * o.dtype.itemsize
                for o, spec in zip(outs, out_specs)
                if spec.memory_space == pltpu.VMEM
            )
            limit_bytes = VMEM_BYTES - held - spare

        def chained(*refs):
            inside = refs[has:]
            place = len(args) + len(outs)
            after = inside[place]
            after[0] = refs[0][0] if has else jnp.int32(0)
            body(*inside[:place], *inside[place + 1 :])

        *results, token = pl.pallas_call(
            chained,
            out_shape=[*outs, jax.ShapeDtypeStruct((1,), jnp.int32)],
            in_specs=[SMEM] * has + list(in_specs),
            out_specs=[*out_specs, SMEM],
            scratch_shapes=list(scratch),
            input_output_aliases={i + has: o for i, o in (aliases or {}).items()},
            cost_estimate=pl.CostEstimate(flops=flops, bytes_accessed=moved, transcendentals=0),
            compiler_params=pltpu.CompilerParams(vmem_limit_bytes=limit_bytes),
        )(*([self.token] * has), *args)
        self.token = token
        return results


def tn(a, b):
    return lax.dot_general(a, b, (((0,), (0,)), ((), ())), preferred_element_type=f32)


def nt(a, b):
    return lax.dot_general(a, b, (((1,), (1,)), ((), ())), preferred_element_type=f32)


def nn(a, b):
    return jnp.dot(a, b, preferred_element_type=f32)


def slot_position(doc_ref, slot):
    first = jnp.int32(0)
    start = jnp.int32(0)
    for j in range(doc_ref.shape[0]):
        start = jnp.where(first <= slot, jnp.maximum(start, first), start)
        first = first + doc_ref[j]
    return slot - start


def time_row(time_ref, position):
    table = time_ref[...].astype(f32)
    rows = lax.broadcasted_iota(jnp.int32, table.shape, 0)
    return jnp.sum(jnp.where(rows == position, table, 0.0), axis=0, keepdims=True)


def fetch(pairs, sems):
    copies = [pltpu.make_async_copy(src, dst, sems.at[i]) for i, (src, dst) in enumerate(pairs)]
    for copy in copies:
        copy.start()
    return copies


def prep_body(work, reach, plan_hbm, doc_hbm, time_hbm, media_ref, *rest):
    sends = rest[:reach]
    facts_ref, table_ref, held, plan_ref, doc_ref, sems, more = rest[reach:]
    slots, tokens, _ = media_ref.shape
    early = fetch([(plan_hbm, plan_ref), (doc_hbm, doc_ref), (time_hbm, table_ref)], more)
    for copy in early:
        copy.wait()
    chosen = []
    for k in range(1, reach + 1):
        slot = jnp.int32(0)
        mark = jnp.int32(0)
        for s in range(slots):
            code = plan_ref[0, s]
            hit = (code >= 0) & (code // work == k)
            slot = jnp.where(hit, s, slot)
            mark = jnp.where(hit, code % work + 1, mark)
        chosen.append((slot, mark))
    copies = fetch([(media_ref.at[slot], held.at[k]) for k, (slot, _) in enumerate(chosen)], sems)
    rank = jnp.int32(0)
    for w in range(work):
        facts_ref[w] = jnp.int32(0)
        facts_ref[work + w] = jnp.int32(0)
        facts_ref[2 * work + w] = jnp.int32(0)
    for s in range(slots):
        code = plan_ref[0, s]
        own = (code >= 0) & (code < work)

        @pl.when(own)
        def _():
            facts_ref[rank] = code
            facts_ref[work + rank] = jnp.int32(s)
            facts_ref[2 * work + rank] = slot_position(doc_ref, jnp.int32(s))

        rank = rank + own.astype(jnp.int32)
    facts_ref[3 * work] = rank
    for k in range(reach):
        slot, mark = chosen[k]
        row = time_row(table_ref, slot_position(doc_ref, slot))
        sends[k][pl.ds(tokens, MARK_ROWS), :] = jnp.full(
            (MARK_ROWS, row.shape[1]), mark.astype(f32), f32
        ).astype(bf16)
        copies[k].wait()
        sends[k][pl.ds(0, tokens), :] = (held[k].astype(f32) + row).astype(bf16)


def stage_body(work, facts_ref, table_ref, media_ref, out_ref, held, sems):
    copies = fetch(
        [(media_ref.at[facts_ref[work + w]], held.at[w]) for w in range(work)], sems
    )
    for w in range(work):
        row = time_row(table_ref, facts_ref[2 * work + w])
        copies[w].wait()
        out_ref[w] = (held[w].astype(f32) + row).astype(bf16)


def seen_at(work, reach, place):
    return min(max(reach - work + place + 1, 0), reach)


def select_body(work, reach, place, facts_ref, own_ref, *rest):
    seen = seen_at(work, reach, place)
    known = seen_at(work, reach, place - 1) if place else 0
    arrivals = rest[:seen]
    rest = rest[seen:]
    if place:
        state_in, rest = rest[0], rest[1:]
    out_ref, state_ref = rest
    tokens = out_ref.shape[0]
    own_count = facts_ref[3 * work]
    marks = [state_in[3 + k] for k in range(known)]
    for k in range(known, seen):
        mark = arrivals[k][pl.ds(tokens, MARK_ROWS), pl.ds(0, 128)].astype(f32)
        marks.append(jnp.max(mark).astype(jnp.int32))
    before = state_in[2] if place else jnp.int32(0)
    ready = own_count + sum([(m > 0).astype(jnp.int32) for m in marks], jnp.int32(0))
    alive = before < ready
    is_own = before < own_count
    index = jnp.minimum(before, work - 1)
    target = jnp.where(is_own, facts_ref[index], 0)
    source = jnp.int32(-1)
    rank = own_count
    for k in range(seen):
        live = marks[k] > 0
        hit = live & (rank == before)
        source = jnp.where(hit, k, source)
        target = jnp.where(hit, marks[k] - 1, target)
        rank = rank + live.astype(jnp.int32)
    state_ref[0] = target
    state_ref[1] = alive.astype(jnp.int32)
    state_ref[2] = before + alive.astype(jnp.int32)
    for k in range(reach):
        state_ref[3 + k] = marks[k] if k < seen else jnp.int32(0)

    @pl.when(is_own)
    def _():
        out_ref[...] = own_ref[index]

    for k in range(seen):

        @pl.when(source == k)
        def _():
            out_ref[...] = arrivals[k][pl.ds(0, tokens), :]

    @pl.when(jnp.logical_not(alive))
    def _():
        out_ref[...] = jnp.zeros(out_ref.shape, bf16)


def normalise(rows):
    average = jnp.mean(rows, axis=-1, keepdims=True)
    centred = rows - average
    spread = jnp.mean(centred * centred, axis=-1, keepdims=True)
    return centred * lax.rsqrt(spread + norm_epsilon)


def own_block(shape, row_size, col_size):
    rows = lax.broadcasted_iota(jnp.int32, shape, 0) // row_size
    cols = lax.broadcasted_iota(jnp.int32, shape, 1) // col_size
    return rows == cols


def spread_heads(rows):
    heads = rows.shape[1] // HEAD
    tall = jnp.concatenate([rows.astype(f32)] * heads, axis=0)
    return jnp.where(own_block(tall.shape, rows.shape[0], HEAD), tall, 0.0)


def latent_body(latents_ref, queries_ref, kw_ref, vw_ref, norm_ref, keys_ref, values_ref, qt_ref, q_ref):
    normed = normalise(latents_ref[...].astype(f32)).astype(bf16)
    norm_ref[...] = normed
    keys_ref[...] = nn(normed, kw_ref[...]).astype(bf16)
    values_ref[...] = nn(normed, vw_ref[...]).astype(bf16)
    tall = spread_heads(queries_ref[...])
    q_ref[...] = tall.astype(bf16)
    qt_ref[...] = tall.T.astype(bf16)


def assemble(dst, blocks, parts, width):
    me = lax.axis_index("mp")
    for b in range(parts):
        start = pl.multiple_of((me ^ b) * width, width)
        dst[:, pl.ds(start, width)] = blocks[b][...]


def grad_attended_body(parts, *refs):
    blocks = refs[:parts]
    ow_ref, out_ref, full = refs[parts:]
    width = blocks[0].shape[1]
    assemble(full, blocks, parts, width)
    out_ref[...] = nt(full[...], ow_ref[...]).astype(bf16)


def place_body(parts, first, last, scale, split, info_ref, *refs):
    blocks = refs[:parts]
    refs = refs[parts:]
    ga_ref, kw_ref, vw_ref, lk_ref, lv_ref, qt_ref, q_ref = refs[:7]
    refs = refs[7:]
    if not first:
        acc_in, lat_in = refs[:2]
        refs = refs[2:]
    if last:
        norm_ref = refs[0]
        *done, att_ref, full, keys, values, grads, late = refs[1:]
    else:
        acc_ref, lat_ref, att_ref, full, keys, values, grads = refs
    tokens, width = blocks[0].shape
    latents = lk_ref.shape[0]
    inner = kw_ref.shape[1]
    assemble(full, blocks, parts, width)
    x = full[...].astype(f32)
    full[...] = normalise(x).astype(bf16)
    keys[pl.ds(0, tokens), :] = nn(full[...], kw_ref[...]).astype(bf16)
    values[pl.ds(0, tokens), :] = nn(full[...], vw_ref[...]).astype(bf16)
    keys[pl.ds(tokens, latents), :] = lk_ref[...]
    values[pl.ds(tokens, latents), :] = lv_ref[...]
    scores = nn(keys[...], qt_ref[...]) * 0.125
    raised = jnp.exp(scores - jnp.max(scores, axis=0, keepdims=True))
    attention = raised / jnp.sum(raised, axis=0, keepdims=True)
    attention_b = attention.astype(bf16)
    crossed = tn(attention_b, values[...])
    crossed = jnp.where(own_block(crossed.shape, latents, HEAD), crossed, 0.0)
    heads = crossed.shape[0] // latents
    att_ref[...] = sum(crossed[h * latents : (h + 1) * latents] for h in range(heads)).astype(bf16)
    alive = info_ref[1].astype(f32)
    start = pl.multiple_of(info_ref[0] * latents, latents)
    ga = ga_ref[pl.ds(start, latents), :].astype(f32) * alive
    tall = spread_heads(ga)
    grad_weights = nn(values[...], tall.T.astype(bf16))
    row_dot = jnp.sum(attention * grad_weights, axis=0, keepdims=True)
    grad_scores = attention * (grad_weights - row_dot)
    high = grad_scores.astype(bf16)
    low = (grad_scores - high.astype(f32)).astype(bf16)
    grad_keys = ((nn(high, q_ref[...]) + nn(low, q_ref[...])) * 0.125).astype(bf16)
    grad_values = nn(attention_b, tall.astype(bf16)).astype(bf16)
    grads[:, pl.ds(0, inner)] = grad_keys[:tokens]
    grads[:, pl.ds(inner, inner)] = grad_values[:tokens]
    late_rows = [grad_keys[tokens:].astype(f32), grad_values[tokens:].astype(f32)]
    if not first:
        late_rows = [lat_in[:, i * inner : (i + 1) * inner] + late_rows[i] for i in range(2)]
    if not last:
        term = tn(full[...], grads[...])
        acc_ref[...] = term if first else acc_in[...] + term
        lat_ref[:, pl.ds(0, inner)] = late_rows[0]
        lat_ref[:, pl.ds(inner, inner)] = late_rows[1]
        return
    twice = jnp.concatenate([norm_ref[...]] * 2, axis=0)
    for i in range(2):
        columns = slice(i * inner, (i + 1) * inner)
        high = late_rows[i].astype(bf16)
        low = (late_rows[i] - high.astype(f32)).astype(bf16)
        total = tn(full[...], grads[:, columns]) + tn(twice, jnp.concatenate([high, low], axis=0))
        if not first:
            total = total + acc_in[:, columns]
        if split is None:
            done[i][...] = (total * scale).astype(bf16)
            continue
        rows, count, bits = split
        late[...] = total * scale
        bit = bits[i]
        mine = (lax.axis_index("dp") // bit) % 2
        for j in range(count // 2):
            for side in range(2):
                chosen = mine if side == 0 else 1 - mine
                block = (j // bit) * 2 * bit + chosen * bit + j % bit
                at = pl.multiple_of(block * rows, rows)
                done[2 * i + side][pl.ds(j * rows, rows), :] = late[pl.ds(at, rows), :].astype(bf16)


def out_body(work, parts, *refs):
    infos = refs[:work]
    atts = refs[work : 2 * work]
    latents_ref, ow_ref, out_ref, base_ref, rows = refs[2 * work :]
    latents = latents_ref.shape[0]
    width = base_ref.shape[2]
    for p in range(work):
        rows[pl.ds(p * latents, latents), :] = atts[p][...]
    me = lax.axis_index("mp")
    start = pl.multiple_of(me * width, width)
    mine = latents_ref[:, pl.ds(start, width)]
    for j in range(parts):
        part = nn(rows[...], ow_ref[:, j * width : (j + 1) * width])
        for w in range(work):
            value = jnp.zeros((latents, width), f32)
            for p in range(work):
                hit = (infos[p][0] == w) & (infos[p][1] > 0)
                value = value + part[p * latents : (p + 1) * latents] * hit.astype(f32)
            out_ref[j, pl.ds(w * latents, latents), :] = value.astype(bf16)
    for w in range(work):
        live = jnp.float32(0)
        for p in range(work):
            live = live + ((infos[p][0] == w) & (infos[p][1] > 0)).astype(f32)
        base_ref[w] = mine.astype(f32) * live


def gather_blocks(block, axis):
    size = lax.axis_size(axis)
    blocks = {0: block}
    bit = size // 2
    while bit >= 1:
        for key in list(blocks):
            blocks[key ^ bit] = flip(blocks[key], axis, bit)
        bit //= 2
    return [blocks[b] for b in range(size)]


def pick_side(value, axis, bit_axis, bit):
    mine = (lax.axis_index(axis) // bit) % 2
    keep = lax.dynamic_index_in_dim(value, mine, bit_axis, keepdims=True)
    send = lax.dynamic_index_in_dim(value, 1 - mine, bit_axis, keepdims=True)
    return keep, send


def exchange(keep, send, axis, bit, last):
    got = flip(send, axis, bit)
    total = keep.astype(f32) + got.astype(f32)
    return total if last else total.astype(bf16)


def powers(size):
    found = []
    while 2 ** len(found) < size:
        found.append(2 ** len(found))
    return found


def layer(
    media,
    time_table,
    doc_images,
    plan,
    latents,
    queries,
    key_weight,
    value_weight,
    out_weight,
    cotangent,
):
    slots, tokens, width = media.shape
    work, latent_count, _ = cotangent.shape
    reach = slots - work
    model_width = latents.shape[1]
    inner = queries.shape[1]
    heads = inner // HEAD
    cross = heads * latent_count
    parts = lax.axis_size("mp")
    dp = lax.axis_size("dp")
    bits = powers(dp)
    depth = len(bits)
    turned = bits[1:] + bits[:1]
    rows = model_width // dp
    shape = jax.ShapeDtypeStruct
    chain = Chain()

    *sends, facts, table = chain.call(
        functools.partial(prep_body, work, reach),
        [shape((tokens + MARK_ROWS, width), bf16)] * reach
        + [shape((3 * work + 1,), jnp.int32), shape(time_table.shape, bf16)],
        [HBM] * 4,
        [VMEM] * reach + [SMEM, VMEM],
        (plan, doc_images, time_table, media),
        [
            pltpu.VMEM((reach, tokens, width), bf16),
            pltpu.SMEM(plan.shape, jnp.int32),
            pltpu.SMEM(doc_images.shape, jnp.int32),
            pltpu.SemaphoreType.DMA((reach,)),
            pltpu.SemaphoreType.DMA((3,)),
        ],
        moved=reach * tokens * width * 4,
        full=True,
    )
    arrivals = []
    for k in range(1, reach + 1):
        arrivals.append(from_behind(sends[k - 1], "dp", k))
    cot_blocks = gather_blocks(cotangent.reshape(work * latent_count, width), "mp")
    (own,) = chain.call(
        functools.partial(stage_body, work),
        [shape((work, tokens, width), bf16)],
        [SMEM, VMEM, HBM],
        [VMEM],
        (facts, table, media),
        [
            pltpu.VMEM((work, tokens, width), bf16),
            pltpu.SemaphoreType.DMA((work,)),
        ],
        moved=work * tokens * width * 4,
        limit=4,
    )
    infos = []
    gathered = []
    attended = []
    carried = ()

    def select(p):
        seen = seen_at(work, reach, p)
        block, info = chain.call(
            functools.partial(select_body, work, reach, p),
            [shape((tokens, width), bf16), shape((3 + reach,), jnp.int32)],
            [SMEM] + [VMEM] * (seen + 1) + [SMEM] * (p > 0),
            [VMEM, SMEM],
            (facts, own, *arrivals[:seen], *infos[-1:]),
            moved=tokens * width * 4,
            limit=2,
        )
        infos.append(info)
        gathered.append(gather_blocks(block, "mp"))

    def place(p):
        nonlocal carried
        first, last = p == 0, p == work - 1
        count = 1 + parts + 7
        sums = [
            shape((model_width, 2 * inner), f32),
            shape((latent_count, 2 * inner), f32),
        ]
        split = None
        scratch = [
            pltpu.VMEM((tokens, model_width), bf16),
            pltpu.VMEM((tokens + latent_count, inner), bf16),
            pltpu.VMEM((tokens + latent_count, inner), bf16),
            pltpu.VMEM((tokens, 2 * inner), bf16),
        ]
        tail = ()
        if last:
            scratch.append(pltpu.VMEM((model_width, inner), f32))
            tail = (norm,)
            if rows % 16 == 0 and depth:
                split = (rows, dp, (bits[0], turned[0]))
                sums = [shape((model_width // 2, inner), bf16)] * 4
            else:
                sums = [shape((model_width, inner), bf16)] * 2
        *carried_new, att = chain.call(
            functools.partial(place_body, parts, first, last, 1.0 / (dp * work), split),
            [*sums, shape((latent_count, inner), bf16)],
            [SMEM] + [VMEM] * (count - 1 + len(carried) + len(tail)),
            [VMEM] * (len(sums) + 1),
            (
                infos[p],
                *gathered[p],
                grad_attended,
                key_weight,
                value_weight,
                late_keys,
                late_values,
                qt,
                q,
                *carried,
                *tail,
            ),
            scratch,
            flops=8 * tokens * model_width * inner + 14 * (tokens + latent_count) * inner * cross,
            limit=16,
            aliases={} if first or last else {count: 0, count + 1: 1},
        )
        carried = tuple(carried_new)
        attended.append(att)

    for p in range(work):
        select(p)
        if p == 0:
            norm, late_keys, late_values, qt, q = chain.call(
                latent_body,
                [
                    shape((latent_count, model_width), bf16),
                    shape((latent_count, inner), bf16),
                    shape((latent_count, inner), bf16),
                    shape((inner, cross), bf16),
                    shape((cross, inner), bf16),
                ],
                [VMEM] * 4,
                [VMEM] * 5,
                (latents, queries, key_weight, value_weight),
                flops=4 * latent_count * model_width * inner,
                limit=8,
            )
        if p == min(1, work - 1):
            (grad_attended,) = chain.call(
                functools.partial(grad_attended_body, parts),
                [shape((work * latent_count, inner), bf16)],
                [VMEM] * (parts + 1),
                [VMEM],
                (*cot_blocks, out_weight),
                [pltpu.VMEM((work * latent_count, model_width), bf16)],
                flops=2 * work * latent_count * inner * model_width,
                limit=8,
            )
        if p >= 2:
            place(p - 2)
    for p in range(max(work - 2, 0), work):
        place(p)

    grads = []
    for i, order in enumerate((bits, turned)):
        left = list(reversed(bits))
        if len(carried) == 4:
            keep, send = carried[2 * i : 2 * i + 2]
            left.remove(order[0])
            dims = (2,) * len(left) + (rows, inner)
            part = exchange(keep, send, "dp", order[0], depth == 1).reshape(dims)
            order = order[1:]
        else:
            part = carried[i].reshape((2,) * depth + (rows, inner))
        grads.append([part, left, order])
    for step in range(max((len(g[2]) for g in grads), default=0)):
        for g in grads:
            part, left, order = g
            bit = order[step]
            keep, send = pick_side(part, "dp", left.index(bit), bit)
            part = exchange(keep, send, "dp", bit, step == len(order) - 1)
            left.remove(bit)
            g[0] = part.reshape((2,) * len(left) + (rows, inner))
    key_grad, value_grad = [g[0].astype(f32) for g in grads]

    partial_out, base = chain.call(
        functools.partial(out_body, work, parts),
        [
            shape((parts, work * latent_count, width), bf16),
            shape((work, latent_count, width), f32),
        ],
        [SMEM] * work + [VMEM] * (work + 2),
        [VMEM] * 2,
        (*infos, *attended, latents, out_weight),
        [pltpu.VMEM((work * latent_count, inner), bf16)],
        flops=2 * work * latent_count * inner * model_width,
        limit=8,
    )
    out_bits = powers(parts)
    out = partial_out.reshape((2,) * len(out_bits) + partial_out.shape[1:])
    for step, bit in enumerate(out_bits):
        keep, send = pick_side(out, "mp", len(out_bits) - 1 - step, bit)
        out = exchange(keep, send, "mp", bit, step == len(out_bits) - 1)
    resampled = (base + out.reshape(base.shape)).astype(bf16)
    return (resampled, key_grad, value_grad)


def solution(mesh):
    return jax.shard_map(
        layer,
        mesh=mesh,
        in_specs=(
            P("dp", None, "mp"),
            P(None, "mp"),
            P("dp"),
            P("dp", None),
            P(),
            P(None, "mp"),
            P(None, "mp"),
            P(None, "mp"),
            P("mp", None),
            P("dp", None, "mp"),
        ),
        out_specs=(P("dp", None, "mp"), P("dp", "mp"), P("dp", "mp")),
        check_vma=False,
    )
```

profile of v0, /device:TPU:0, one launch (start us, length us, event | category | flops | bytes accessed | tf_op | source)
XLA Modules:
  0.0 108.1 jit_solution(790250650789310033)
XLA Ops:
  0.7 3.1 %shard_map.121 = (bf16[272,384]{1,0:T(8,128)(2,1)}, bf16[272,384]{1,0:T(8,128)(2,1)}, bf16[272,384]{1,0:T(8,128)(2,1)}, bf16[272,384]{1,0:T(8,128)(2,1)}, s32[13...) custom-call(s32[1,8]{1,0:T(1,128)} %refs_0_.1, s32[2]{0:T(128)} %refs_1_.2, bf16[8,384]{1,0:T(8,128)(2,1)} %refs_2_.2, ...), custom_call_target="tpu_custom_call" | custom-call | bytes 1572864 | tf_op jit(solution)/shard_map/pallas_call | solution.py:68
  3.8 4.9 %collective-permute-start = (bf16[272,384]{1,0:T(8,128)(2,1)}, bf16[272,384]{1,0:T(8,128)(2,1)S(1)}, u32[]{:S(2)}, u32[]{:S(2)}) collective-permute-start(bf16[272,384]{1,0:T(8,128)(2,1)} %get-tuple-element.57), channel_id=1, source_target_pairs={{0,4},{4,8},{8,12},{12,16},{16,20},{20,24},{24,28},{1,5},{5,9},{9,... | collective-permute-start | bytes 626696 | tf_op jit(solution)/shard_map/ppermute | solution.py:25
  8.7 1.6 %collective-permute-start.3 = (bf16[256,384]{1,0:T(8,128)(2,1)}, bf16[256,384]{1,0:T(8,128)(2,1)S(1)}, u32[]{:S(2)}, u32[]{:S(2)}) collective-permute-start(bf16[256,384]{1,0:T(8,128)(2,1)} %bitcast.21), channel_id=1, source_target_pairs={{0,2},{1,3},{2,0},{3,1},{4,6},{5,7},{6,4},{7,5},{8,10},{9,11},{10,... | collective-permute-start | bytes 589832 | tf_op jit(solution)/shard_map/ppermute | solution.py:29
  10.3 1.4 %copy-done.3 = bf16[8,256,384]{2,1,0:T(8,128)(2,1)S(1)} copy-done((bf16[8,256,384]{2,1,0:T(8,128)(2,1)S(1)}, bf16[8,256,384]{2,1,0:T(8,128)(2,1)}, u32[]{:S(2)}) %copy-start.3) | copy-done | bytes 1572888
  11.7 0.7 copy-done.9
  12.4 0.7 copy-done.11
  13.1 3.0 %shard_map.122 = (bf16[4,256,384]{2,1,0:T(8,128)(2,1)S(1)}, s32[1]{0:T(128)}) custom-call(s32[1]{0:T(128)} %get-tuple-element.52.refs_0_, s32[13]{0:T(128)S(1)} %copy-done.9, bf16[8,384]{1,0:T(8,128)(2,1)S(1)} %copy-done.11, bf16[8,256,384]{2,1,0:T(8,128)(2,1)S(1)} %copy-done.3), custom_call_target="tpu_custom_call" | custom-call | bytes 1572864 | tf_op jit(solution)/shard_map/pallas_call | solution.py:68
  16.1 2.0 %shard_map.123 = (bf16[256,384]{1,0:T(8,128)(2,1)S(1)}, s32[7]{0:T(128)S(1)}, s32[1]{0:T(128)}) custom-call(s32[1]{0:T(128)} %get-tuple-element.55.refs_0_, s32[13]{0:T(128)S(1)} %copy-done.9, bf16[4,256,384]{2,1,0:T(8,128)(2,1)S(1)} %get-tuple-element.56.refs_2_, bf16[272,384]{1,0:T(8,128)(2,1)S(1)} %collective-permute-done.refs_3_), custom_call_target="tpu_custom_call" | custom-call | bytes 393216 | tf_op jit(solution)/shard_map/pallas_call | solution.py:68
  18.1 0.6 collective-permute-start.7
  18.6 3.6 %collective-permute-start.1 = (bf16[272,384]{1,0:T(8,128)(2,1)}, bf16[272,384]{1,0:T(8,128)(2,1)S(1)}, u32[]{:S(2)}, u32[]{:S(2)}) collective-permute-start(bf16[272,384]{1,0:T(8,128)(2,1)} %get-tuple-element.60), channel_id=1, source_target_pairs={{0,8},{4,12},{8,16},{12,20},{16,24},{20,28},{1,9},{5,13},{9,17},{1... | collective-permute-start | bytes 626696 | tf_op jit(solution)/shard_map/ppermute | solution.py:25
  22.4 4.3 %collective-permute-start.5 = (bf16[272,384]{1,0:T(8,128)(2,1)}, bf16[272,384]{1,0:T(8,128)(2,1)S(1)}, u32[]{:S(2)}, u32[]{:S(2)}) collective-permute-start(bf16[272,384]{1,0:T(8,128)(2,1)} %get-tuple-element.64), channel_id=1, source_target_pairs={{0,12},{4,16},{8,20},{12,24},{16,28},{1,13},{5,17},{9,21},{13,25},... | collective-permute-start | bytes 626696 | tf_op jit(solution)/shard_map/ppermute | solution.py:25
  26.7 0.3 collective-permute-start.6
  27.0 0.3 collective-permute-start.8
  27.3 5.7 %collective-permute-start.9 = (bf16[272,384]{1,0:T(8,128)(2,1)}, bf16[272,384]{1,0:T(8,128)(2,1)S(1)}, u32[]{:S(2)}, u32[]{:S(2)}) collective-permute-start(bf16[272,384]{1,0:T(8,128)(2,1)} %get-tuple-element.74), channel_id=1, source_target_pairs={{0,16},{4,20},{8,24},{12,28},{1,17},{5,21},{9,25},{13,29},{2,18},{... | collective-permute-start | bytes 626696 | tf_op jit(solution)/shard_map/ppermute | solution.py:25
  33.0 1.1 %copy-done.1 = bf16[1536,256]{1,0:T(8,128)(2,1)S(1)} copy-done((bf16[1536,256]{1,0:T(8,128)(2,1)S(1)}, bf16[1536,256]{1,0:T(8,128)(2,1)}, u32[]{:S(2)}) %copy-start.1) | copy-done | bytes 786456
  34.1 0.9 copy-done.5
  35.1 1.2 %shard_map.124 = (bf16[64,1536]{1,0:T(8,128)(2,1)S(1)}, bf16[64,256]{1,0:T(8,128)(2,1)S(1)}, bf16[64,256]{1,0:T(8,128)(2,1)S(1)}, bf16[256,256]{1,0:T(8,128)(2,1...) custom-call(s32[1]{0:T(128)} %get-tuple-element.58.refs_0_, bf16[64,1536]{1,0:T(8,128)(2,1)S(1)} %copy-done.5, ...), custom_call_target="tpu_custom_call" | custom-call | flops 100663296 | tf_op jit(solution)/shard_map/pallas_call | solution.py:68
  36.3 1.9 %shard_map.125 = (bf16[256,384]{1,0:T(8,128)(2,1)S(1)}, s32[7]{0:T(128)S(1)}, s32[1]{0:T(128)}) custom-call(s32[1]{0:T(128)} %get-tuple-element.59.refs_0_, s32[13]{0:T(128)S(1)} %copy-done.10, bf16[4,256,384]{2,1,0:T(8,128)(2,1)S(1)} %get-tuple-element.56.refs_2_, bf16[272,384]{1,0:T(8,128)(2,1)S(1)} %collective-permute-done.refs_3_, ...), custom_call_target="tpu_custom_call" | custom-call | bytes 393216 | tf_op jit(solution)/shard_map/pallas_call | solution.py:68
  38.3 1.9 %collective-permute-start.11 = (bf16[256,384]{1,0:T(8,128)(2,1)S(1)}, bf16[256,384]{1,0:T(8,128)(2,1)S(1)}, u32[]{:S(2)}, u32[]{:S(2)}) collective-permute-start(bf16[256,384]{1,0:T(8,128)(2,1)S(1)} %get-tuple-element.77.refs_2_), channel_id=1, source_target_pairs={{0,2},{1,3},{2,0},{3,1},{4,6},{5,7},{6,4},{7,5},{8,10},{9,11},{10,... | collective-permute-start | bytes 589832 | tf_op jit(solution)/shard_map/ppermute | solution.py:29
  40.1 1.4 %shard_map.126 = (bf16[256,256]{1,0:T(8,128)(2,1)S(1)}, s32[1]{0:T(128)}) custom-call(s32[1]{0:T(128)} %get-tuple-element.62.refs_0_, bf16[256,384]{1,0:T(8,128)(2,1)S(1)} %bitcast.23, bf16[256,384]{1,0:T(8,128)(2,1)S(1)} %collective-permute-done.2.refs_2_, bf16[256,384]{1,0:T(8,128)(2,1)S(1)} %collective-permute-done.3.refs_3_, ...), custom_call_target="tpu_custom_call" | custom-call | flops 201326592 | tf_op jit(solution)/shard_map/pallas_call | solution.py:68
  41.6 1.9 %shard_map.127 = (bf16[256,384]{1,0:T(8,128)(2,1)S(1)}, s32[7]{0:T(128)S(1)}, s32[1]{0:T(128)}) custom-call(s32[1]{0:T(128)} %get-tuple-element.63.refs_0_, s32[13]{0:T(128)S(1)} %copy-done.10, bf16[4,256,384]{2,1,0:T(8,128)(2,1)S(1)} %get-tuple-element.56.refs_2_, bf16[272,384]{1,0:T(8,128)(2,1)S(1)} %collective-permute-done.refs_3_, ...), custom_call_target="tpu_custom_call" | custom-call | bytes 393216 | tf_op jit(solution)/shard_map/pallas_call | solution.py:68
  43.6 0.3 collective-permute-start.14
  43.9 3.5 %shard_map.128 = (f32[1536,512]{1,0:T(8,128)S(1)}, f32[64,512]{1,0:T(8,128)S(1)}, bf16[64,256]{1,0:T(8,128)(2,1)S(1)}, s32[1]{0:T(128)}) custom-call(s32[1]{0:T(128)} %get-tuple-element.66.refs_0_, s32[7]{0:T(128)S(1)} %get-tuple-element.61.refs_5_.refs_1_, bf16[256,384]{1,0:T(8,128)(2,1)S(1)} %get-tuple-element.67.refs_2_, ...), custom_call_target="tpu_custom_call" | custom-call | flops 1098907648 | tf_op jit(solution)/shard_map/pallas_call | solution.py:68
  47.4 2.1 %shard_map.129 = (bf16[256,384]{1,0:T(8,128)(2,1)S(1)}, s32[7]{0:T(128)S(1)}, s32[1]{0:T(128)}) custom-call(s32[1]{0:T(128)} %get-tuple-element.73.refs_0_, s32[13]{0:T(128)S(1)} %copy-done.10, bf16[4,256,384]{2,1,0:T(8,128)(2,1)S(1)} %get-tuple-element.56.refs_2_, bf16[272,384]{1,0:T(8,128)(2,1)S(1)} %collective-permute-done.refs_3_, ...), custom_call_target="tpu_custom_call" | custom-call | bytes 393216 | tf_op jit(solution)/shard_map/pallas_call | solution.py:68
  49.6 1.9 %collective-permute-start.17 = (bf16[256,384]{1,0:T(8,128)(2,1)S(1)}, bf16[256,384]{1,0:T(8,128)(2,1)S(1)}, u32[]{:S(2)}, u32[]{:S(2)}) collective-permute-start(bf16[256,384]{1,0:T(8,128)(2,1)S(1)} %get-tuple-element.86.refs_2_), channel_id=1, source_target_pairs={{0,2},{1,3},{2,0},{3,1},{4,6},{5,7},{6,4},{7,5},{8,10},{9,11},{10,... | collective-permute-start | bytes 589832 | tf_op jit(solution)/shard_map/ppermute | solution.py:29
  51.4 0.5 collective-permute-start.13
  52.0 0.5 collective-permute-start.16
  52.5 4.3 %collective-permute-done.17.refs_4_ = bf16[256,384]{1,0:T(8,128)(2,1)S(1)} collective-permute-done((bf16[256,384]{1,0:T(8,128)(2,1)S(1)}, bf16[256,384]{1,0:T(8,128)(2,1)S(1)}, u32[]{:S(2)}, u32[]{:S(2)}) %collective-permute-start.17) | collective-permute-done | bytes 196640 | tf_op jit(solution)/shard_map/ppermute | solution.py:29
  56.7 3.7 %shard_map.130 = (f32[1536,512]{1,0:T(8,128)S(1)}, f32[64,512]{1,0:T(8,128)S(1)}, bf16[64,256]{1,0:T(8,128)(2,1)S(1)}, s32[1]{0:T(128)}) custom-call(s32[1]{0:T(128)} %get-tuple-element.76.refs_0_, s32[7]{0:T(128)S(1)} %get-tuple-element.65.refs_6_.refs_1_.refs_2_, ...), custom_call_target="tpu_custom_call", output_to_operand_aliasing={{0}: (13, {}), {1}: (14, {})} | custom-call | flops 1098907648 | tf_op jit(solution)/shard_map/pallas_call | solution.py:68
  60.5 3.7 %shard_map.131 = (f32[1536,512]{1,0:T(8,128)S(1)}, f32[64,512]{1,0:T(8,128)S(1)}, bf16[64,256]{1,0:T(8,128)(2,1)S(1)}, s32[1]{0:T(128)}) custom-call(s32[1]{0:T(128)} %get-tuple-element.80.refs_0_, s32[7]{0:T(128)S(1)} %get-tuple-element.75.refs_7_.refs_1_.refs_3_, ...), custom_call_target="tpu_custom_call", output_to_operand_aliasing={{0}: (13, {}), {1}: (14, {})} | custom-call | flops 1098907648 | tf_op jit(solution)/shard_map/pallas_call | solution.py:68
  64.3 4.9 %shard_map.132 = (bf16[768,256]{1,0:T(8,128)(2,1)S(1)}, bf16[768,256]{1,0:T(8,128)(2,1)S(1)}, bf16[768,256]{1,0:T(8,128)(2,1)S(1)}, bf16[768,256]{1,0:T(8,128)(2...) custom-call(s32[1]{0:T(128)} %get-tuple-element.84.refs_0_, s32[7]{0:T(128)S(1)} %get-tuple-element.85.refs_1_.refs_4_, ...), custom_call_target="tpu_custom_call" | custom-call | flops 1098907648 | tf_op jit(solution)/shard_map/pallas_call | solution.py:68
  69.1 2.0 %collective-permute-start.24 = (bf16[768,256]{1,0:T(8,128)(2,1)S(1)}, bf16[768,256]{1,0:T(8,128)(2,1)S(1)}, u32[]{:S(2)}, u32[]{:S(2)}) collective-permute-start(bf16[768,256]{1,0:T(8,128)(2,1)S(1)} %get-tuple-element.100), channel_id=1, source_target_pairs={{0,8},{4,12},{8,0},{12,4},{16,24},{20,28},{24,16},{28,20},{1,9},{5... | collective-permute-start | bytes 1179656 | tf_op jit(solution)/shard_map/ppermute | solution.py:29
  71.1 6.7 %collective-permute-start.21 = (bf16[768,256]{1,0:T(8,128)(2,1)S(1)}, bf16[768,256]{1,0:T(8,128)(2,1)S(1)}, u32[]{:S(2)}, u32[]{:S(2)}) collective-permute-start(bf16[768,256]{1,0:T(8,128)(2,1)S(1)} %get-tuple-element.98), channel_id=1, source_target_pairs={{0,4},{4,0},{8,12},{12,8},{16,20},{20,16},{24,28},{28,24},{1,5},{5... | collective-permute-start | bytes 1179656 | tf_op jit(solution)/shard_map/ppermute | solution.py:29
  77.8 2.2 %shard_map.133 = (bf16[4,256,384]{2,1,0:T(8,128)(2,1)S(1)}, f32[4,64,384]{2,1,0:T(8,128)S(1)}, s32[1]{0:T(128)}) custom-call(s32[1]{0:T(128)} %get-tuple-element.90.refs_0_, s32[7]{0:T(128)S(1)} %get-tuple-element.61.refs_5_.refs_1_, s32[7]{0:T(128)S(1)} %get-tuple-element.65.refs_6_.refs_1_.refs_2_, s32[7]{0:T(128)S(1)} %get-tuple-element.75.refs_7_.refs_1_.refs_3_, ...), custom_call_target="tpu_custom_call" | custom-call | flops 201326592 | tf_op jit(solution)/shard_map/pallas_call | solution.py:68
  80.1 0.3 collective-permute-start.19
  80.4 0.5 collective-permute-done.24
  81.0 2.7 %collective-permute-start.25 = (bf16[1,2,192,256]{3,2,1,0:T(8,128)(2,1)S(1)}, bf16[1,2,192,256]{3,2,1,0:T(8,128)(2,1)S(1)}, u32[]{:S(2)}, u32[]{:S(2)}) collective-permute-start(bf16[1,2,192,256]{3,2,1,0:T(8,128)(2,1)S(1)} %constant_dynamic-slice_fusion), channel_id=1, source_target_pairs={{0,16},{4,20},{8,24},{12,28},{16,0},{20,4},{24,8},{28,12},{1,17},{... | collective-permute-start | bytes 589832 | tf_op jit(solution)/shard_map/ppermute | solution.py:29
  83.7 3.9 %collective-permute-done.21 = bf16[768,256]{1,0:T(8,128)(2,1)S(1)} collective-permute-done((bf16[768,256]{1,0:T(8,128)(2,1)S(1)}, bf16[768,256]{1,0:T(8,128)(2,1)S(1)}, u32[]{:S(2)}, u32[]{:S(2)}) %collective-permute-start.21) | collective-permute-done | bytes 393248 | tf_op jit(solution)/shard_map/ppermute | solution.py:29
  87.6 0.1 add_convert_fusion.1
  87.8 1.6 %collective-permute-start.22 = (bf16[2,1,192,256]{3,2,1,0:T(8,128)(2,1)S(1)}, bf16[2,1,192,256]{3,2,1,0:T(8,128)(2,1)S(1)}, u32[]{:S(2)}, u32[]{:S(2)}) collective-permute-start(bf16[2,1,192,256]{3,2,1,0:T(8,128)(2,1)S(1)} %constant_dynamic-slice_fusion.1), channel_id=1, source_target_pairs={{0,8},{4,12},{8,0},{12,4},{16,24},{20,28},{24,16},{28,20},{1,9},{5... | collective-permute-start | bytes 589832 | tf_op jit(solution)/shard_map/ppermute | solution.py:29
  89.3 0.1 add_convert_fusion.2
  89.5 1.6 %collective-permute-start.20 = (bf16[1,1,256,384]{3,2,1,0:T(8,128)(2,1)S(1)}, bf16[1,1,256,384]{3,2,1,0:T(8,128)(2,1)S(1)}, u32[]{:S(2)}, u32[]{:S(2)}) collective-permute-start(bf16[1,1,256,384]{3,2,1,0:T(8,128)(2,1)S(1)} %constant_dynamic-slice_fusion.2), channel_id=1, source_target_pairs={{0,2},{1,3},{2,0},{3,1},{4,6},{5,7},{6,4},{7,5},{8,10},{9,11},{10,... | collective-permute-start | bytes 589832 | tf_op jit(solution)/shard_map/ppermute | solution.py:29
  91.1 1.9 %collective-permute-done.25 = bf16[1,2,192,256]{3,2,1,0:T(8,128)(2,1)S(1)} collective-permute-done((bf16[1,2,192,256]{3,2,1,0:T(8,128)(2,1)S(1)}, bf16[1,2,192,256]{3,2,1,0:T(8,128)(2,1)S(1)}, u32[]{:S(2)}, u32[]{:S(2)}) %collective-permute-start.25) | collective-permute-done | bytes 196640 | tf_op jit(solution)/shard_map/ppermute | solution.py:29
  93.1 7.9 %collective-permute-start.26 = (bf16[1,192,256]{2,1,0:T(8,128)(2,1)S(1)}, bf16[1,192,256]{2,1,0:T(8,128)(2,1)S(1)}, u32[]{:S(2)}, u32[]{:S(2)}) collective-permute-start(bf16[1,192,256]{2,1,0:T(8,128)(2,1)S(1)} %dynamic-slice_bitcast_fusion), channel_id=1, source_target_pairs={{0,4},{4,0},{8,12},{12,8},{16,20},{20,16},{24,28},{28,24},{1,5},{5... | collective-permute-start | bytes 294920 | tf_op jit(solution)/shard_map/ppermute | solution.py:29
  101.3 0.7 add_convert_fusion.5
  102.0 4.7 %collective-permute-done.23 = bf16[1,192,256]{2,1,0:T(8,128)(2,1)S(1)} collective-permute-done((bf16[1,192,256]{2,1,0:T(8,128)(2,1)S(1)}, bf16[1,192,256]{2,1,0:T(8,128)(2,1)S(1)}, u32[]{:S(2)}, u32[]{:S(2)}) %collective-permute-start.23) | collective-permute-done | bytes 98336 | tf_op jit(solution)/shard_map/ppermute | solution.py:29
  106.7 0.7 fusion.1
  107.4 0.7 fusion
  (58 shorter events, 0.8 us)
Async XLA Ops:
  0.6 32.3 %copy-start.8 = (bf16[64,256]{1,0:T(8,128)(2,1)S(1)}, bf16[64,256]{1,0:T(8,128)(2,1)}, u32[]{:S(2)}) copy-start(bf16[64,256]{1,0:T(8,128)(2,1)} %refs_2_.3) | copy-start | bytes 98308
  0.6 32.3 %copy-start = (bf16[1536,256]{1,0:T(8,128)(2,1)S(1)}, bf16[1536,256]{1,0:T(8,128)(2,1)}, u32[]{:S(2)}) copy-start(bf16[1536,256]{1,0:T(8,128)(2,1)} %refs_7_.7) | copy-start | bytes 2359300
  3.8 32.5 %copy-start.10 = (s32[13]{0:T(128)S(1)}, s32[13]{0:T(128)}, u32[]{:S(2)}) copy-start(s32[13]{0:T(128)} %get-tuple-element.53.refs_1_) | copy-start | bytes 160
  3.8 12.2 %collective-permute-start = (bf16[272,384]{1,0:T(8,128)(2,1)}, bf16[272,384]{1,0:T(8,128)(2,1)S(1)}, u32[]{:S(2)}, u32[]{:S(2)}) collective-permute-start(bf16[272,384]{1,0:T(8,128)(2,1)} %get-tuple-element.57), channel_id=1, source_target_pairs={{0,4},{4,8},{8,12},{12,16},{16,20},{20,24},{24,28},{1,5},{5,9},{9,... | collective-permute-start | bytes 626696 | tf_op jit(solution)/shard_map/ppermute | solution.py:25
  8.7 13.6 %collective-permute-start.3 = (bf16[256,384]{1,0:T(8,128)(2,1)}, bf16[256,384]{1,0:T(8,128)(2,1)S(1)}, u32[]{:S(2)}, u32[]{:S(2)}) collective-permute-start(bf16[256,384]{1,0:T(8,128)(2,1)} %bitcast.21), channel_id=1, source_target_pairs={{0,2},{1,3},{2,0},{3,1},{4,6},{5,7},{6,4},{7,5},{8,10},{9,11},{10,... | collective-permute-start | bytes 589832 | tf_op jit(solution)/shard_map/ppermute | solution.py:29
  10.3 16.4 %collective-permute-start.2 = (bf16[256,384]{1,0:T(8,128)(2,1)}, bf16[256,384]{1,0:T(8,128)(2,1)S(1)}, u32[]{:S(2)}, u32[]{:S(2)}) collective-permute-start(bf16[256,384]{1,0:T(8,128)(2,1)} %bitcast.22), channel_id=1, source_target_pairs={{0,1},{1,0},{2,3},{3,2},{4,5},{5,4},{6,7},{7,6},{8,9},{9,8},{10,11... | collective-permute-start | bytes 589832 | tf_op jit(solution)/shard_map/ppermute | solution.py:29
  10.3 1.4 %copy-start.3 = (bf16[8,256,384]{2,1,0:T(8,128)(2,1)S(1)}, bf16[8,256,384]{2,1,0:T(8,128)(2,1)}, u32[]{:S(2)}) copy-start(bf16[8,256,384]{2,1,0:T(8,128)(2,1)} %refs_3_.4) | copy-start | bytes 4718596
  11.7 0.7 copy-start.9
  12.4 0.7 copy-start.11
  13.1 27.1 %copy-start.4 = (bf16[256,1536]{1,0:T(8,128)(2,1)S(1)}, bf16[256,1536]{1,0:T(8,128)(2,1)}, u32[]{:S(2)}) copy-start(bf16[256,1536]{1,0:T(8,128)(2,1)} %refs_10_.1) | copy-start | bytes 2359300
  13.1 27.1 %copy-start.7 = (bf16[4,64,384]{2,1,0:T(8,128)(2,1)S(1)}, bf16[4,64,384]{2,1,0:T(8,128)(2,1)}, u32[]{:S(2)}) copy-start(bf16[4,64,384]{2,1,0:T(8,128)(2,1)} %param.19) | copy-start | bytes 589828
  16.0 27.9 %copy-start.2 = (bf16[1536,256]{1,0:T(8,128)(2,1)S(1)}, bf16[1536,256]{1,0:T(8,128)(2,1)}, u32[]{:S(2)}) copy-start(bf16[1536,256]{1,0:T(8,128)(2,1)} %refs_8_.7) | copy-start | bytes 2359300
  18.1 8.9 %collective-permute-start.7 = (bf16[256,384]{1,0:T(8,128)(2,1)S(1)}, bf16[256,384]{1,0:T(8,128)(2,1)S(1)}, u32[]{:S(2)}, u32[]{:S(2)}) collective-permute-start(bf16[256,384]{1,0:T(8,128)(2,1)S(1)} %get-tuple-element.67.refs_2_), channel_id=1, source_target_pairs={{0,2},{1,3},{2,0},{3,1},{4,6},{5,7},{6,4},{7,5},{8,10},{9,11},{10,... | collective-permute-start | bytes 589832 | tf_op jit(solution)/shard_map/ppermute | solution.py:29
  18.6 8.6 %collective-permute-start.1 = (bf16[272,384]{1,0:T(8,128)(2,1)}, bf16[272,384]{1,0:T(8,128)(2,1)S(1)}, u32[]{:S(2)}, u32[]{:S(2)}) collective-permute-start(bf16[272,384]{1,0:T(8,128)(2,1)} %get-tuple-element.60), channel_id=1, source_target_pairs={{0,8},{4,12},{8,16},{12,20},{16,24},{20,28},{1,9},{5,13},{9,17},{1... | collective-permute-start | bytes 626696 | tf_op jit(solution)/shard_map/ppermute | solution.py:25
  22.3 16.0 %collective-permute-start.4 = (bf16[256,384]{1,0:T(8,128)(2,1)S(1)}, bf16[256,384]{1,0:T(8,128)(2,1)S(1)}, u32[]{:S(2)}, u32[]{:S(2)}) collective-permute-start(bf16[256,384]{1,0:T(8,128)(2,1)S(1)} %collective-permute-done.3.refs_3_), channel_id=1, source_target_pairs={{0,1},{1,0},{2,3},{3,2},{4,5},{5,4},{6,7},{7,6},{8,9},{9,8},{10,11... | collective-permute-start | bytes 589832 | tf_op jit(solution)/shard_map/ppermute | solution.py:29
  22.4 19.2 %collective-permute-start.5 = (bf16[272,384]{1,0:T(8,128)(2,1)}, bf16[272,384]{1,0:T(8,128)(2,1)S(1)}, u32[]{:S(2)}, u32[]{:S(2)}) collective-permute-start(bf16[272,384]{1,0:T(8,128)(2,1)} %get-tuple-element.64), channel_id=1, source_target_pairs={{0,12},{4,16},{8,20},{12,24},{16,28},{1,13},{5,17},{9,21},{13,25},... | collective-permute-start | bytes 626696 | tf_op jit(solution)/shard_map/ppermute | solution.py:25
  26.7 16.9 %collective-permute-start.6 = (bf16[256,384]{1,0:T(8,128)(2,1)S(1)}, bf16[256,384]{1,0:T(8,128)(2,1)S(1)}, u32[]{:S(2)}, u32[]{:S(2)}) collective-permute-start(bf16[256,384]{1,0:T(8,128)(2,1)S(1)} %get-tuple-element.67.refs_2_), channel_id=1, source_target_pairs={{0,1},{1,0},{2,3},{3,2},{4,5},{5,4},{6,7},{7,6},{8,9},{9,8},{10,11... | collective-permute-start | bytes 589832 | tf_op jit(solution)/shard_map/ppermute | solution.py:29
  27.0 16.9 %collective-permute-start.8 = (bf16[256,384]{1,0:T(8,128)(2,1)S(1)}, bf16[256,384]{1,0:T(8,128)(2,1)S(1)}, u32[]{:S(2)}, u32[]{:S(2)}) collective-permute-start(bf16[256,384]{1,0:T(8,128)(2,1)S(1)} %collective-permute-done.7.refs_4_), channel_id=1, source_target_pairs={{0,1},{1,0},{2,3},{3,2},{4,5},{5,4},{6,7},{7,6},{8,9},{9,8},{10,11... | collective-permute-start | bytes 589832 | tf_op jit(solution)/shard_map/ppermute | solution.py:29
  27.3 20.2 %collective-permute-start.9 = (bf16[272,384]{1,0:T(8,128)(2,1)}, bf16[272,384]{1,0:T(8,128)(2,1)S(1)}, u32[]{:S(2)}, u32[]{:S(2)}) collective-permute-start(bf16[272,384]{1,0:T(8,128)(2,1)} %get-tuple-element.74), channel_id=1, source_target_pairs={{0,16},{4,20},{8,24},{12,28},{1,17},{5,21},{9,25},{13,29},{2,18},{... | collective-permute-start | bytes 626696 | tf_op jit(solution)/shard_map/ppermute | solution.py:25
  33.0 1.1 %copy-start.1 = (bf16[1536,256]{1,0:T(8,128)(2,1)S(1)}, bf16[1536,256]{1,0:T(8,128)(2,1)}, u32[]{:S(2)}) copy-start(bf16[1536,256]{1,0:T(8,128)(2,1)} %refs_8_.7) | copy-start | bytes 2359300
  34.1 0.9 copy-start.5
  38.3 13.2 %collective-permute-start.11 = (bf16[256,384]{1,0:T(8,128)(2,1)S(1)}, bf16[256,384]{1,0:T(8,128)(2,1)S(1)}, u32[]{:S(2)}, u32[]{:S(2)}) collective-permute-start(bf16[256,384]{1,0:T(8,128)(2,1)S(1)} %get-tuple-element.77.refs_2_), channel_id=1, source_target_pairs={{0,2},{1,3},{2,0},{3,1},{4,6},{5,7},{6,4},{7,5},{8,10},{9,11},{10,... | collective-permute-start | bytes 589832 | tf_op jit(solution)/shard_map/ppermute | solution.py:29
  41.6 10.4 %collective-permute-start.10 = (bf16[256,384]{1,0:T(8,128)(2,1)S(1)}, bf16[256,384]{1,0:T(8,128)(2,1)S(1)}, u32[]{:S(2)}, u32[]{:S(2)}) collective-permute-start(bf16[256,384]{1,0:T(8,128)(2,1)S(1)} %get-tuple-element.77.refs_2_), channel_id=1, source_target_pairs={{0,1},{1,0},{2,3},{3,2},{4,5},{5,4},{6,7},{7,6},{8,9},{9,8},{10,11... | collective-permute-start | bytes 589832 | tf_op jit(solution)/shard_map/ppermute | solution.py:29
  43.6 8.4 %collective-permute-start.14 = (bf16[256,384]{1,0:T(8,128)(2,1)S(1)}, bf16[256,384]{1,0:T(8,128)(2,1)S(1)}, u32[]{:S(2)}, u32[]{:S(2)}) collective-permute-start(bf16[256,384]{1,0:T(8,128)(2,1)S(1)} %get-tuple-element.81.refs_2_), channel_id=1, source_target_pairs={{0,2},{1,3},{2,0},{3,1},{4,6},{5,7},{6,4},{7,5},{8,10},{9,11},{10,... | collective-permute-start | bytes 589832 | tf_op jit(solution)/shard_map/ppermute | solution.py:29
  49.6 7.2 %collective-permute-start.17 = (bf16[256,384]{1,0:T(8,128)(2,1)S(1)}, bf16[256,384]{1,0:T(8,128)(2,1)S(1)}, u32[]{:S(2)}, u32[]{:S(2)}) collective-permute-start(bf16[256,384]{1,0:T(8,128)(2,1)S(1)} %get-tuple-element.86.refs_2_), channel_id=1, source_target_pairs={{0,2},{1,3},{2,0},{3,1},{4,6},{5,7},{6,4},{7,5},{8,10},{9,11},{10,... | collective-permute-start | bytes 589832 | tf_op jit(solution)/shard_map/ppermute | solution.py:29
  51.4 5.3 %collective-permute-start.12 = (bf16[256,384]{1,0:T(8,128)(2,1)S(1)}, bf16[256,384]{1,0:T(8,128)(2,1)S(1)}, u32[]{:S(2)}, u32[]{:S(2)}) collective-permute-start(bf16[256,384]{1,0:T(8,128)(2,1)S(1)} %collective-permute-done.11.refs_4_), channel_id=1, source_target_pairs={{0,1},{1,0},{2,3},{3,2},{4,5},{5,4},{6,7},{7,6},{8,9},{9,8},{10,11... | collective-permute-start | bytes 589832 | tf_op jit(solution)/shard_map/ppermute | solution.py:29
  51.4 9.0 %collective-permute-start.13 = (bf16[256,384]{1,0:T(8,128)(2,1)S(1)}, bf16[256,384]{1,0:T(8,128)(2,1)S(1)}, u32[]{:S(2)}, u32[]{:S(2)}) collective-permute-start(bf16[256,384]{1,0:T(8,128)(2,1)S(1)} %get-tuple-element.81.refs_2_), channel_id=1, source_target_pairs={{0,1},{1,0},{2,3},{3,2},{4,5},{5,4},{6,7},{7,6},{8,9},{9,8},{10,11... | collective-permute-start | bytes 589832 | tf_op jit(solution)/shard_map/ppermute | solution.py:29
  52.0 8.5 %collective-permute-start.15 = (bf16[256,384]{1,0:T(8,128)(2,1)S(1)}, bf16[256,384]{1,0:T(8,128)(2,1)S(1)}, u32[]{:S(2)}, u32[]{:S(2)}) collective-permute-start(bf16[256,384]{1,0:T(8,128)(2,1)S(1)} %collective-permute-done.14.refs_4_), channel_id=1, source_target_pairs={{0,1},{1,0},{2,3},{3,2},{4,5},{5,4},{6,7},{7,6},{8,9},{9,8},{10,11... | collective-permute-start | bytes 589832 | tf_op jit(solution)/shard_map/ppermute | solution.py:29
  52.0 12.3 %collective-permute-start.16 = (bf16[256,384]{1,0:T(8,128)(2,1)S(1)}, bf16[256,384]{1,0:T(8,128)(2,1)S(1)}, u32[]{:S(2)}, u32[]{:S(2)}) collective-permute-start(bf16[256,384]{1,0:T(8,128)(2,1)S(1)} %get-tuple-element.86.refs_2_), channel_id=1, source_target_pairs={{0,1},{1,0},{2,3},{3,2},{4,5},{5,4},{6,7},{7,6},{8,9},{9,8},{10,11... | collective-permute-start | bytes 589832 | tf_op jit(solution)/shard_map/ppermute | solution.py:29
  56.7 7.5 %collective-permute-start.18 = (bf16[256,384]{1,0:T(8,128)(2,1)S(1)}, bf16[256,384]{1,0:T(8,128)(2,1)S(1)}, u32[]{:S(2)}, u32[]{:S(2)}) collective-permute-start(bf16[256,384]{1,0:T(8,128)(2,1)S(1)} %collective-permute-done.17.refs_4_), channel_id=1, source_target_pairs={{0,1},{1,0},{2,3},{3,2},{4,5},{5,4},{6,7},{7,6},{8,9},{9,8},{10,11... | collective-permute-start | bytes 589832 | tf_op jit(solution)/shard_map/ppermute | solution.py:29
  64.3 13.6 %copy-start.6 = (bf16[64,1536]{1,0:T(8,128)(2,1)S(1)}, bf16[64,1536]{1,0:T(8,128)(2,1)}, u32[]{:S(2)}) copy-start(bf16[64,1536]{1,0:T(8,128)(2,1)} %refs_9_.1) | copy-start | bytes 589828
  69.1 11.7 %collective-permute-start.24 = (bf16[768,256]{1,0:T(8,128)(2,1)S(1)}, bf16[768,256]{1,0:T(8,128)(2,1)S(1)}, u32[]{:S(2)}, u32[]{:S(2)}) collective-permute-start(bf16[768,256]{1,0:T(8,128)(2,1)S(1)} %get-tuple-element.100), channel_id=1, source_target_pairs={{0,8},{4,12},{8,0},{12,4},{16,24},{20,28},{24,16},{28,20},{1,9},{5... | collective-permute-start | bytes 1179656 | tf_op jit(solution)/shard_map/ppermute | solution.py:29
  71.1 16.5 %collective-permute-start.21 = (bf16[768,256]{1,0:T(8,128)(2,1)S(1)}, bf16[768,256]{1,0:T(8,128)(2,1)S(1)}, u32[]{:S(2)}, u32[]{:S(2)}) collective-permute-start(bf16[768,256]{1,0:T(8,128)(2,1)S(1)} %get-tuple-element.98), channel_id=1, source_target_pairs={{0,4},{4,0},{8,12},{12,8},{16,20},{20,16},{24,28},{28,24},{1,5},{5... | collective-permute-start | bytes 1179656 | tf_op jit(solution)/shard_map/ppermute | solution.py:29
  80.1 9.2 %collective-permute-start.19 = (bf16[2,1,256,384]{3,2,1,0:T(8,128)(2,1)S(1)}, bf16[2,1,256,384]{3,2,1,0:T(8,128)(2,1)S(1)}, u32[]{:S(2)}, u32[]{:S(2)}) collective-permute-start(bf16[2,1,256,384]{3,2,1,0:T(8,128)(2,1)S(1)} %constant_dynamic-slice_fusion.3), channel_id=1, source_target_pairs={{0,1},{1,0},{2,3},{3,2},{4,5},{5,4},{6,7},{7,6},{8,9},{9,8},{10,11... | collective-permute-start | bytes 1179656 | tf_op jit(solution)/shard_map/ppermute | solution.py:29
  81.0 12.0 %collective-permute-start.25 = (bf16[1,2,192,256]{3,2,1,0:T(8,128)(2,1)S(1)}, bf16[1,2,192,256]{3,2,1,0:T(8,128)(2,1)S(1)}, u32[]{:S(2)}, u32[]{:S(2)}) collective-permute-start(bf16[1,2,192,256]{3,2,1,0:T(8,128)(2,1)S(1)} %constant_dynamic-slice_fusion), channel_id=1, source_target_pairs={{0,16},{4,20},{8,24},{12,28},{16,0},{20,4},{24,8},{28,12},{1,17},{... | collective-permute-start | bytes 589832 | tf_op jit(solution)/shard_map/ppermute | solution.py:29
  87.8 13.3 %collective-permute-start.22 = (bf16[2,1,192,256]{3,2,1,0:T(8,128)(2,1)S(1)}, bf16[2,1,192,256]{3,2,1,0:T(8,128)(2,1)S(1)}, u32[]{:S(2)}, u32[]{:S(2)}) collective-permute-start(bf16[2,1,192,256]{3,2,1,0:T(8,128)(2,1)S(1)} %constant_dynamic-slice_fusion.1), channel_id=1, source_target_pairs={{0,8},{4,12},{8,0},{12,4},{16,24},{20,28},{24,16},{28,20},{1,9},{5... | collective-permute-start | bytes 589832 | tf_op jit(solution)/shard_map/ppermute | solution.py:29
  89.5 11.7 %collective-permute-start.20 = (bf16[1,1,256,384]{3,2,1,0:T(8,128)(2,1)S(1)}, bf16[1,1,256,384]{3,2,1,0:T(8,128)(2,1)S(1)}, u32[]{:S(2)}, u32[]{:S(2)}) collective-permute-start(bf16[1,1,256,384]{3,2,1,0:T(8,128)(2,1)S(1)} %constant_dynamic-slice_fusion.2), channel_id=1, source_target_pairs={{0,2},{1,3},{2,0},{3,1},{4,6},{5,7},{6,4},{7,5},{8,10},{9,11},{10,... | collective-permute-start | bytes 589832 | tf_op jit(solution)/shard_map/ppermute | solution.py:29
  93.1 14.3 %collective-permute-start.26 = (bf16[1,192,256]{2,1,0:T(8,128)(2,1)S(1)}, bf16[1,192,256]{2,1,0:T(8,128)(2,1)S(1)}, u32[]{:S(2)}, u32[]{:S(2)}) collective-permute-start(bf16[1,192,256]{2,1,0:T(8,128)(2,1)S(1)} %dynamic-slice_bitcast_fusion), channel_id=1, source_target_pairs={{0,4},{4,0},{8,12},{12,8},{16,20},{20,16},{24,28},{28,24},{1,5},{5... | collective-permute-start | bytes 294920 | tf_op jit(solution)/shard_map/ppermute | solution.py:29
  101.1 5.6 %collective-permute-start.23 = (bf16[1,192,256]{2,1,0:T(8,128)(2,1)S(1)}, bf16[1,192,256]{2,1,0:T(8,128)(2,1)S(1)}, u32[]{:S(2)}, u32[]{:S(2)}) collective-permute-start(bf16[1,192,256]{2,1,0:T(8,128)(2,1)S(1)} %dynamic-slice_bitcast_fusion.1), channel_id=1, source_target_pairs={{0,16},{4,20},{8,24},{12,28},{16,0},{20,4},{24,8},{28,12},{1,17},{... | collective-permute-start | bytes 294920 | tf_op jit(solution)/shard_map/ppermute | solution.py:29
where the time goes:
time: 109 us; the launch traced here: 108 us
  starting transfers between devices  49.3 us (45%)
  Pallas kernels  34.8 us (32%)
  waiting for transfers between devices  15.3 us (14%)
  local copies, waits for them, and re-layouts  5 us (5%)
  other arithmetic  2.6 us (2%)
    pallas_call x13, Pallas kernels, call(): pl.pallas_call(chained, out_shape=[*outs, jax.ShapeDtypeStruct((1,), jnp....  34.8 us
    ppermute x23, starting transfers between devices, flip(): lax.ppermute(block, axis, [(i, i ^ bit) for i in range(lax.axis_size(axis...  30.8 us
    ppermute x4, starting transfers between devices, from_behind(): return lax.ppermute(block, axis, route)  18.5 us
    ppermute x23, waiting for transfers between devices, flip(): lax.ppermute(block, axis, [(i, i ^ bit) for i in range(lax.axis_size(axis...  15.3 us
    unnamed x24, local copies, waits for them, and re-layouts  4.84 us
  transfers between devices with their start and end apart: 27, of which 5 were waited for; matrix products, arithmetic and copies ran while one was open for 2% of the time, Pallas kernels for 25%

commit v1 on v0

v1 whole, which is shorter than its diff:
```python
import functools

import jax
import jax.numpy as jnp
from jax import lax
from jax.experimental import pallas as pl
from jax.experimental.pallas import tpu as pltpu
from jax.sharding import PartitionSpec as P


HEAD = 64
MARK_ROWS = 16
VMEM_BYTES = 67043328
SPARE = 12000000
norm_epsilon = 1e-05
f32 = jnp.float32
bf16 = jnp.bfloat16
VMEM = pl.BlockSpec(memory_space=pltpu.VMEM)
HBM = pl.BlockSpec(memory_space=pltpu.HBM)


def from_behind(block, axis, distance):
    size = lax.axis_size(axis)
    return lax.ppermute(block, axis, [(i, (i + distance) % size) for i in range(size)])


def flip(block, axis, bit):
    return lax.ppermute(block, axis, [(i, i ^ bit) for i in range(lax.axis_size(axis))])


class Chain:
    def __init__(self):
        self.token = None

    def call(
        self,
        body,
        outs,
        in_specs,
        out_specs,
        args,
        scratch=(),
        flops=0,
        moved=0,
        limit=8,
        aliases=None,
        full=False,
        spare=0,
    ):
        has = self.token is not None
        limit_bytes = limit << 20
        if full:
            held = sum(
                o.size * o.dtype.itemsize
                for o, spec in zip(outs, out_specs)
                if spec.memory_space == pltpu.VMEM
            )
            limit_bytes = VMEM_BYTES - held - spare

        def chained(*refs):
            inside = refs[has:]
            place = len(args) + len(outs)
            inside[place][...] = jnp.zeros(inside[place].shape, f32)
            body(*inside[:place], *inside[place + 1 :])

        *results, token = pl.pallas_call(
            chained,
            out_shape=[*outs, jax.ShapeDtypeStruct((8, 128), f32)],
            in_specs=[VMEM] * has + list(in_specs),
            out_specs=[*out_specs, VMEM],
            scratch_shapes=list(scratch),
            input_output_aliases={i + has: o for i, o in (aliases or {}).items()},
            cost_estimate=pl.CostEstimate(flops=flops, bytes_accessed=moved, transcendentals=0),
            compiler_params=pltpu.CompilerParams(vmem_limit_bytes=limit_bytes),
        )(*([self.token] * has), *args)
        self.token = token
        return results


def tn(a, b):
    return lax.dot_general(a, b, (((0,), (0,)), ((), ())), preferred_element_type=f32)


def nt(a, b):
    return lax.dot_general(a, b, (((1,), (1,)), ((), ())), preferred_element_type=f32)


def nn(a, b):
    return jnp.dot(a, b, preferred_element_type=f32)


def slot_position(doc_ref, slot):
    first = jnp.int32(0)
    start = jnp.int32(0)
    for j in range(doc_ref.shape[0]):
        start = jnp.where(first <= slot, jnp.maximum(start, first), start)
        first = first + doc_ref[j]
    return slot - start


def time_row(time_ref, position):
    table = time_ref[...].astype(f32)
    rows = lax.broadcasted_iota(jnp.int32, table.shape, 0)
    return jnp.sum(jnp.where(rows == position, table, 0.0), axis=0, keepdims=True)


def fetch(pairs, sems):
    copies = [pltpu.make_async_copy(src, dst, sems.at[i]) for i, (src, dst) in enumerate(pairs)]
    for copy in copies:
        copy.start()
    return copies


def prep_body(work, reach, plan_hbm, doc_hbm, time_hbm, media_ref, *rest):
    sends = rest[:reach]
    own_ref, rows_ref, facts_ref, held, plan_ref, doc_ref, time_ref, sems, own_sems, more = rest[
        reach:
    ]
    slots, tokens, width = media_ref.shape
    early = fetch([(plan_hbm, plan_ref), (doc_hbm, doc_ref), (time_hbm, time_ref)], more)
    for copy in early:
        copy.wait()
    codes = [plan_ref[0, s] for s in range(slots)]
    chosen = []
    for k in range(1, reach + 1):
        slot = jnp.int32(0)
        mark = jnp.int32(0)
        for s in range(slots):
            hit = (codes[s] >= k * work) & (codes[s] < (k + 1) * work)
            slot = jnp.where(hit, s, slot)
            mark = jnp.where(hit, codes[s] - k * work + 1, mark)
        chosen.append((slot, mark))
    copies = fetch([(media_ref.at[slot], held.at[k]) for k, (slot, _) in enumerate(chosen)], sems)
    own_slots = [jnp.int32(0)] * work
    own_codes = [jnp.int32(0)] * work
    rank = jnp.int32(0)
    for s in range(slots):
        own = (codes[s] >= 0) & (codes[s] < work)
        for w in range(work):
            hit = own & (rank == w)
            own_slots[w] = jnp.where(hit, s, own_slots[w])
            own_codes[w] = jnp.where(hit, codes[s], own_codes[w])
        rank = rank + own.astype(jnp.int32)
    own_copies = fetch([(media_ref.at[own_slots[w]], own_ref.at[w]) for w in range(work)], own_sems)

    def splat(value):
        return jnp.full((1, width), value.astype(f32), f32)

    facts_ref[...] = jnp.zeros(facts_ref.shape, f32)
    facts_ref[pl.ds(work, 1), :] = splat(rank)
    for w in range(work):
        facts_ref[pl.ds(w, 1), :] = splat(own_codes[w])
        rows_ref[pl.ds(w, 1), :] = time_row(time_ref, slot_position(doc_ref, own_slots[w]))
    for k in range(reach):
        slot, mark = chosen[k]
        row = time_row(time_ref, slot_position(doc_ref, slot))
        sends[k][pl.ds(tokens, MARK_ROWS), :] = jnp.full(
            (MARK_ROWS, width), mark.astype(f32), f32
        ).astype(bf16)
        copies[k].wait()
        sends[k][pl.ds(0, tokens), :] = (held[k].astype(f32) + row).astype(bf16)
    for copy in own_copies:
        copy.wait()


def seen_at(work, reach, place):
    return min(max(reach - work + place + 1, 0), reach)


def select_body(work, reach, place, facts_ref, rows_ref, own_ref, *rest):
    seen = seen_at(work, reach, place)
    arrivals = rest[:seen]
    out_ref, info_ref = rest[seen:]
    tokens, width = out_ref.shape
    own_count = facts_ref[pl.ds(work, 1), :]
    marks = [ref[pl.ds(tokens, MARK_ROWS), :].astype(f32)[:1] for ref in arrivals]
    lives = [jnp.minimum(mark, 1.0) for mark in marks]
    taken = jnp.zeros((1, width), f32)
    for p in range(place + 1):
        ready = own_count
        for live in lives[: seen_at(work, reach, p)]:
            ready = ready + live
        before = taken
        taken = jnp.minimum(taken + 1.0, ready)
    alive = taken - before
    target = jnp.zeros((1, width), f32)
    row = jnp.zeros((1, width), f32)
    raw = jnp.zeros((tokens, width), bf16)
    for w in range(min(work, place + 1)):
        weight = jnp.where((before == w) & (own_count > w), 1.0, 0.0)
        target = target + weight * facts_ref[pl.ds(w, 1), :]
        row = row + weight * rows_ref[pl.ds(w, 1), :]
        raw = raw + own_ref[w] * weight.astype(bf16)
    block = (raw.astype(f32) + row).astype(bf16)
    rank = own_count
    for k in range(seen):
        weight = jnp.where(rank == before, lives[k], 0.0)
        target = target + weight * (marks[k] - 1.0)
        block = block + arrivals[k][pl.ds(0, tokens), :] * weight.astype(bf16)
        rank = rank + lives[k]
    out_ref[...] = block
    lanes = info_ref.shape[1]
    info_ref[...] = jnp.zeros(info_ref.shape, f32)
    info_ref[pl.ds(0, 1), :] = target[:, :lanes]
    info_ref[pl.ds(1, 1), :] = alive[:, :lanes]


def normalise(rows):
    average = jnp.mean(rows, axis=-1, keepdims=True)
    centred = rows - average
    spread = jnp.mean(centred * centred, axis=-1, keepdims=True)
    return centred * lax.rsqrt(spread + norm_epsilon)


def own_block(shape, row_size, col_size):
    rows = lax.broadcasted_iota(jnp.int32, shape, 0) // row_size
    cols = lax.broadcasted_iota(jnp.int32, shape, 1) // col_size
    return rows == cols


def spread_heads(rows):
    heads = rows.shape[1] // HEAD
    tall = jnp.concatenate([rows.astype(f32)] * heads, axis=0)
    return jnp.where(own_block(tall.shape, rows.shape[0], HEAD), tall, 0.0)


def assemble(dst, blocks, parts, width):
    me = lax.axis_index("mp")
    for b in range(parts):
        start = pl.multiple_of((me ^ b) * width, width)
        dst[pl.ds(0, blocks[b].shape[0]), pl.ds(start, width)] = blocks[b][...]


def slot_hit(info_ref, slot):
    target = info_ref[pl.ds(0, 1), pl.ds(0, 1)]
    return jnp.where(target == slot, info_ref[pl.ds(1, 1), pl.ds(0, 1)], 0.0)


def place_body(parts, first, last, scale, split, info_ref, *refs):
    blocks, refs = refs[:parts], refs[parts:]
    kw_ref, vw_ref, refs = refs[0], refs[1], refs[2:]
    if first:
        latents_ref, queries_ref, ow_ref, refs = *refs[:3], refs[3:]
        cots, refs = refs[:parts], refs[parts:]
        acc_ref, lat_ref, att_ref, ga_ref, lk_ref, lv_ref, qt_ref, q_ref, norm_ref, *refs = refs
        full, keys, values, grads, cot_full = refs
    else:
        acc_in, lat_in, ga_ref, lk_ref, lv_ref, qt_ref, q_ref, norm_ref, *refs = refs
        if last:
            *done, att_ref, full, keys, values, grads, late = refs
        else:
            acc_ref, lat_ref, att_ref, full, keys, values, grads = refs
    tokens, width = blocks[0].shape
    latents = lk_ref.shape[0]
    inner = kw_ref.shape[1]
    assemble(full, blocks, parts, width)
    chunk = tokens if tokens % 32 else 32
    for r in range(0, tokens, chunk):
        rows = full[pl.ds(r, chunk), :].astype(f32)
        full[pl.ds(r, chunk), :] = normalise(rows).astype(bf16)
    if first:
        assemble(cot_full, cots, parts, width)
        normed = normalise(latents_ref[...].astype(f32)).astype(bf16)
        norm_ref[...] = normed
        full[pl.ds(tokens, latents), :] = normed
        keys[...] = nn(full[...], kw_ref[...]).astype(bf16)
        values[...] = nn(full[...], vw_ref[...]).astype(bf16)
        lk_ref[...] = keys[pl.ds(tokens, latents), :]
        lv_ref[...] = values[pl.ds(tokens, latents), :]
        tall = spread_heads(queries_ref[...])
        q_ref[...] = tall.astype(bf16)
        qt_ref[...] = tall.T.astype(bf16)
        ga_ref[...] = nt(cot_full[...], ow_ref[...]).astype(bf16)
    else:
        keys[pl.ds(0, tokens), :] = nn(full[...], kw_ref[...]).astype(bf16)
        values[pl.ds(0, tokens), :] = nn(full[...], vw_ref[...]).astype(bf16)
        keys[pl.ds(tokens, latents), :] = lk_ref[...]
        values[pl.ds(tokens, latents), :] = lv_ref[...]
    scores = nn(keys[...], qt_ref[...]) * 0.125
    raised = jnp.exp(scores - jnp.max(scores, axis=0, keepdims=True))
    attention = raised / jnp.sum(raised, axis=0, keepdims=True)
    attention_b = attention.astype(bf16)
    crossed = tn(attention_b, values[...])
    crossed = jnp.where(own_block(crossed.shape, latents, HEAD), crossed, 0.0)
    heads = crossed.shape[0] // latents
    att_ref[...] = sum(crossed[h * latents : (h + 1) * latents] for h in range(heads)).astype(bf16)
    ga = jnp.zeros((latents, inner), f32)
    for w in range(ga_ref.shape[0] // latents):
        ga = ga + ga_ref[pl.ds(w * latents, latents), :].astype(f32) * slot_hit(info_ref, w)
    tall = spread_heads(ga)
    grad_weights = nn(values[...], tall.T.astype(bf16))
    row_dot = jnp.sum(attention * grad_weights, axis=0, keepdims=True)
    grad_scores = attention * (grad_weights - row_dot)
    high = grad_scores.astype(bf16)
    low = (grad_scores - high.astype(f32)).astype(bf16)
    grad_keys = ((nn(high, q_ref[...]) + nn(low, q_ref[...])) * 0.125).astype(bf16)
    grad_values = nn(attention_b, tall.astype(bf16)).astype(bf16)
    grads[:, pl.ds(0, inner)] = grad_keys[:tokens]
    grads[:, pl.ds(inner, inner)] = grad_values[:tokens]
    late_rows = [grad_keys[tokens:].astype(f32), grad_values[tokens:].astype(f32)]
    if not first:
        late_rows = [lat_in[:, i * inner : (i + 1) * inner] + late_rows[i] for i in range(2)]
    if not last:
        term = tn(full[pl.ds(0, tokens), :], grads[...])
        acc_ref[...] = term if first else acc_in[...] + term
        lat_ref[:, pl.ds(0, inner)] = late_rows[0]
        lat_ref[:, pl.ds(inner, inner)] = late_rows[1]
        return
    twice = jnp.concatenate([norm_ref[...]] * 2, axis=0)
    for i in range(2):
        columns = slice(i * inner, (i + 1) * inner)
        high = late_rows[i].astype(bf16)
        low = (late_rows[i] - high.astype(f32)).astype(bf16)
        total = tn(full[pl.ds(0, tokens), :], grads[:, columns]) + tn(twice, jnp.concatenate([high, low], axis=0))
        if not first:
            total = total + acc_in[:, columns]
        if split is None:
            done[i][...] = (total * scale).astype(bf16)
            continue
        rows, count, bits = split
        late[...] = total * scale
        bit = bits[i]
        mine = (lax.axis_index("dp") // bit) % 2
        for j in range(count // 2):
            for side in range(2):
                chosen = mine if side == 0 else 1 - mine
                block = (j // bit) * 2 * bit + chosen * bit + j % bit
                at = pl.multiple_of(block * rows, rows)
                done[2 * i + side][pl.ds(j * rows, rows), :] = late[pl.ds(at, rows), :].astype(bf16)


def out_body(work, parts, *refs):
    infos = refs[:work]
    atts = refs[work : 2 * work]
    latents_ref, ow_ref, out_ref, base_ref, rows = refs[2 * work :]
    latents = latents_ref.shape[0]
    width = base_ref.shape[2]
    for p in range(work):
        rows[pl.ds(p * latents, latents), :] = atts[p][...]
    me = lax.axis_index("mp")
    start = pl.multiple_of(me * width, width)
    mine = latents_ref[:, pl.ds(start, width)]
    for j in range(parts):
        part = nn(rows[...], ow_ref[:, j * width : (j + 1) * width])
        for w in range(work):
            value = jnp.zeros((latents, width), f32)
            for p in range(work):
                rows_p = part[p * latents : (p + 1) * latents]
                value = value + rows_p * slot_hit(infos[p], w)
            out_ref[j, pl.ds(w * latents, latents), :] = value.astype(bf16)
    for w in range(work):
        live = jnp.zeros((1, 1), f32)
        for p in range(work):
            live = live + slot_hit(infos[p], w)
        base_ref[w] = mine.astype(f32) * live


def gather_blocks(block, axis):
    size = lax.axis_size(axis)
    blocks = {0: block}
    bit = size // 2
    while bit >= 1:
        for key in list(blocks):
            blocks[key ^ bit] = flip(blocks[key], axis, bit)
        bit //= 2
    return [blocks[b] for b in range(size)]


def pick_side(value, axis, bit_axis, bit):
    mine = (lax.axis_index(axis) // bit) % 2
    keep = lax.dynamic_index_in_dim(value, mine, bit_axis, keepdims=True)
    send = lax.dynamic_index_in_dim(value, 1 - mine, bit_axis, keepdims=True)
    return keep, send


def exchange(keep, send, axis, bit, last):
    got = flip(send, axis, bit)
    total = keep.astype(f32) + got.astype(f32)
    return total if last else total.astype(bf16)


def powers(size):
    found = []
    while 2 ** len(found) < size:
        found.append(2 ** len(found))
    return found


def layer(
    media,
    time_table,
    doc_images,
    plan,
    latents,
    queries,
    key_weight,
    value_weight,
    out_weight,
    cotangent,
):
    slots, tokens, width = media.shape
    work, latent_count, _ = cotangent.shape
    reach = slots - work
    model_width = latents.shape[1]
    inner = queries.shape[1]
    heads = inner // HEAD
    cross = heads * latent_count
    parts = lax.axis_size("mp")
    dp = lax.axis_size("dp")
    bits = powers(dp)
    depth = len(bits)
    turned = bits[1:] + bits[:1]
    rows = model_width // dp
    shape = jax.ShapeDtypeStruct
    chain = Chain()

    fact_rows = -(-(work + 1) // 8) * 8
    *sends, own, own_rows, facts = chain.call(
        functools.partial(prep_body, work, reach),
        [shape((tokens + MARK_ROWS, width), bf16)] * reach
        + [
            shape((work, tokens, width), bf16),
            shape((fact_rows, width), f32),
            shape((fact_rows, width), f32),
        ],
        [HBM] * 4,
        [VMEM] * (reach + 3),
        (plan, doc_images, time_table, media),
        [
            pltpu.VMEM((reach, tokens, width), bf16),
            pltpu.SMEM(plan.shape, jnp.int32),
            pltpu.SMEM(doc_images.shape, jnp.int32),
            pltpu.VMEM(time_table.shape, bf16),
            pltpu.SemaphoreType.DMA((reach,)),
            pltpu.SemaphoreType.DMA((work,)),
            pltpu.SemaphoreType.DMA((3,)),
        ],
        moved=(reach + work) * tokens * width * 4,
        full=True,
        spare=SPARE,
    )
    arrivals = []
    for k in range(1, reach + 1):
        arrivals.append(from_behind(sends[k - 1], "dp", k))
    cot_blocks = gather_blocks(cotangent.reshape(work * latent_count, width), "mp")
    infos = []
    gathered = []
    attended = []
    sums = ()
    shared = ()

    def select(p):
        seen = seen_at(work, reach, p)
        block, info = chain.call(
            functools.partial(select_body, work, reach, p),
            [shape((tokens, width), bf16), shape((8, 128), f32)],
            [VMEM] * (seen + 3),
            [VMEM, VMEM],
            (facts, own_rows, own, *arrivals[:seen]),
            moved=tokens * width * 4,
            limit=2,
        )
        infos.append(info)
        gathered.append(gather_blocks(block, "mp"))

    def place(p):
        nonlocal sums, shared
        first, last = p == 0, p == work - 1
        held_rows = tokens + latent_count
        split = None
        new = [
            shape((model_width, 2 * inner), f32),
            shape((latent_count, 2 * inner), f32),
        ]
        if last:
            if rows % 16 == 0 and depth:
                split = (rows, dp, (bits[0], turned[0]))
                new = [shape((model_width // 2, inner), bf16)] * 4
            else:
                new = [shape((model_width, inner), bf16)] * 2
        scratch = [
            pltpu.VMEM((held_rows if first else tokens, model_width), bf16),
            pltpu.VMEM((held_rows, inner), bf16),
            pltpu.VMEM((held_rows, inner), bf16),
            pltpu.VMEM((tokens, 2 * inner), bf16),
        ]
        args = (infos[p], *gathered[p], key_weight, value_weight)
        extra = []
        if first:
            args += (latents, queries, out_weight, *cot_blocks)
            extra = [
                shape((work * latent_count, inner), bf16),
                shape((latent_count, inner), bf16),
                shape((latent_count, inner), bf16),
                shape((inner, cross), bf16),
                shape((cross, inner), bf16),
                shape((latent_count, model_width), bf16),
            ]
            scratch.append(pltpu.VMEM((work * latent_count, model_width), bf16))
        else:
            args += (*sums, *shared)
        if last:
            scratch.append(pltpu.VMEM((model_width, inner), f32))
        start = 3 + parts
        results = chain.call(
            functools.partial(place_body, parts, first, last, 1.0 / (dp * work), split),
            [*new, shape((latent_count, inner), bf16), *extra],
            [VMEM] * len(args),
            [VMEM] * (len(new) + 1 + len(extra)),
            args,
            scratch,
            flops=8 * tokens * model_width * inner + 14 * held_rows * inner * cross,
            limit=16,
            aliases={} if first or last else {start: 0, start + 1: 1},
        )
        sums = tuple(results[: len(new)])
        attended.append(results[len(new)])
        if first:
            shared = tuple(results[len(new) + 1 :])

    for p in range(work):
        if p >= 3:
            place(p - 3)
        select(p)
    for p in range(max(work - 3, 0), work):
        place(p)
    carried = sums

    grads = []
    for i, order in enumerate((bits, turned)):
        left = list(reversed(bits))
        if len(carried) == 4:
            keep, send = carried[2 * i : 2 * i + 2]
            left.remove(order[0])
            dims = (2,) * len(left) + (rows, inner)
            part = exchange(keep, send, "dp", order[0], depth == 1).reshape(dims)
            order = order[1:]
        else:
            part = carried[i].reshape((2,) * depth + (rows, inner))
        grads.append([part, left, order])
    for step in range(max((len(g[2]) for g in grads), default=0)):
        for g in grads:
            part, left, order = g
            bit = order[step]
            keep, send = pick_side(part, "dp", left.index(bit), bit)
            part = exchange(keep, send, "dp", bit, step == len(order) - 1)
            left.remove(bit)
            g[0] = part.reshape((2,) * len(left) + (rows, inner))
    key_grad, value_grad = [g[0].astype(f32) for g in grads]

    partial_out, base = chain.call(
        functools.partial(out_body, work, parts),
        [
            shape((parts, work * latent_count, width), bf16),
            shape((work, latent_count, width), f32),
        ],
        [VMEM] * (2 * work + 2),
        [VMEM] * 2,
        (*infos, *attended, latents, out_weight),
        [pltpu.VMEM((work * latent_count, inner), bf16)],
        flops=2 * work * latent_count * inner * model_width,
        limit=8,
    )
    out_bits = powers(parts)
    out = partial_out.reshape((2,) * len(out_bits) + partial_out.shape[1:])
    for step, bit in enumerate(out_bits):
        keep, send = pick_side(out, "mp", len(out_bits) - 1 - step, bit)
        out = exchange(keep, send, "mp", bit, step == len(out_bits) - 1)
    resampled = (base + out.reshape(base.shape)).astype(bf16)
    return (resampled, key_grad, value_grad)


def solution(mesh):
    return jax.shard_map(
        layer,
        mesh=mesh,
        in_specs=(
            P("dp", None, "mp"),
            P(None, "mp"),
            P("dp"),
            P("dp", None),
            P(),
            P(None, "mp"),
            P(None, "mp"),
            P(None, "mp"),
            P("mp", None),
            P("dp", None, "mp"),
        ),
        out_specs=(P("dp", None, "mp"), P("dp", "mp"), P("dp", "mp")),
        check_vma=False,
    )
```

time: 109 us -> 92.9 us (0.85)
  waiting for transfers between devices: 15.3 us -> 55.8 us
  starting transfers between devices: 49.3 us -> 14.9 us
  Pallas kernels: 34.8 us -> 16 us
  local copies, waits for them, and re-layouts: 5 us -> 2.3 us
    ppermute x4, waiting for transfers between devices: 0.01 us -> 21.6 us  [from_behind(): lax.ppermute(block, axis, [(i, (i + distance) % size) for i in range(size)])]
    ppermute x23, starting transfers between devices: 30.8 us -> 10.9 us  [flip(): lax.ppermute(block, axis, [(i, i ^ bit) for i in range(lax.axis_size(axis...]
    ppermute x23, waiting for transfers between devices: 15.3 us -> 34.3 us  [flip(): lax.ppermute(block, axis, [(i, i ^ bit) for i in range(lax.axis_size(axis...]
    pallas_call x13 -> x10, Pallas kernels: 34.8 us -> 16 us  [call(): pl.pallas_call(chained, out_shape=[*outs, jax.ShapeDtypeStruct((8, 128),...]
    ppermute x4, starting transfers between devices: 18.5 us -> 3.98 us  [from_behind(): lax.ppermute(block, axis, [(i, (i + distance) % size) for i in range(size)])]
    unnamed x24 -> x18, local copies, waits for them, and re-layouts: 4.84 us -> 2.16 us
  transfers between devices with their start and end apart: 27 -> 27, of which waited for: 5 -> 10; matrix products, arithmetic and copies ran while one was open for 2% -> 2% of each run, Pallas kernels for 25% -> 11%
where the time goes in v1:
time: 92.9 us; the launch traced here: 92.7 us
  waiting for transfers between devices  55.8 us (60%)
  Pallas kernels  16 us (17%)
  starting transfers between devices  14.9 us (16%)
  other arithmetic  2.61 us (3%)
  local copies, waits for them, and re-layouts  2.3 us (2%)
  between operations  1.09 us (1%)
    ppermute x23, waiting for transfers between devices, flip(): lax.ppermute(block, axis, [(i, i ^ bit) for i in range(lax.axis_size(axis...  34.3 us
    ppermute x4, waiting for transfers between devices, from_behind(): lax.ppermute(block, axis, [(i, (i + distance) % size) for i in range(size)])  21.6 us
    pallas_call x10, Pallas kernels, call(): pl.pallas_call(chained, out_shape=[*outs, jax.ShapeDtypeStruct((8, 128),...  16 us
    ppermute x23, starting transfers between devices, flip(): lax.ppermute(block, axis, [(i, i ^ bit) for i in range(lax.axis_size(axis...  10.9 us
    ppermute x4, starting transfers between devices, from_behind(): lax.ppermute(block, axis, [(i, (i + distance) % size) for i in range(size)])  3.98 us
    unnamed x18, local copies, waits for them, and re-layouts  2.16 us
  transfers between devices with their start and end apart: 27, of which 10 were waited for; matrix products, arithmetic and copies ran while one was open for 2% of the time, Pallas kernels for 11%

profile of v1, /device:TPU:0, one launch (start us, length us, event | category | flops | bytes accessed | tf_op | source)
XLA Modules:
  0.0 92.7 jit_solution(12985889409522160673)
XLA Ops:
  0.7 0.8 copy-done.6
  1.5 0.7 copy-done.7
  2.2 0.7 copy-done.8
  2.8 2.5 %shard_map.121 = (bf16[272,384]{1,0:T(8,128)(2,1)S(1)}, bf16[272,384]{1,0:T(8,128)(2,1)S(1)}, bf16[272,384]{1,0:T(8,128)(2,1)S(1)}, bf16[272,384]{1,0:T(8,128)(2...) custom-call(s32[1,8]{1,0:T(1,128)S(1)} %copy-done.7, ...), custom_call_target="tpu_custom_call" | custom-call | bytes 3145728 | tf_op jit(solution)/shard_map/pallas_call | solution.py:66
  5.4 2.7 %collective-permute-start = (bf16[272,384]{1,0:T(8,128)(2,1)S(1)}, bf16[272,384]{1,0:T(8,128)(2,1)S(1)}, u32[]{:S(2)}, u32[]{:S(2)}) collective-permute-start(bf16[272,384]{1,0:T(8,128)(2,1)S(1)} %get-tuple-element.53), channel_id=1, source_target_pairs={{0,4},{4,8},{8,12},{12,16},{16,20},{20,24},{24,28},{28,0},{1,5},{5... | collective-permute-start | bytes 626696 | tf_op jit(solution)/shard_map/ppermute | solution.py:24
  8.0 1.5 %collective-permute-start.7 = (bf16[256,384]{1,0:T(8,128)(2,1)}, bf16[256,384]{1,0:T(8,128)(2,1)S(1)}, u32[]{:S(2)}, u32[]{:S(2)}) collective-permute-start(bf16[256,384]{1,0:T(8,128)(2,1)} %bitcast.21), channel_id=1, source_target_pairs={{0,2},{1,3},{2,0},{3,1},{4,6},{5,7},{6,4},{7,5},{8,10},{9,11},{10,... | collective-permute-start | bytes 589832 | tf_op jit(solution)/shard_map/ppermute | solution.py:28
  9.6 7.0 %collective-permute-done.refs_4_ = bf16[272,384]{1,0:T(8,128)(2,1)S(1)} collective-permute-done((bf16[272,384]{1,0:T(8,128)(2,1)S(1)}, bf16[272,384]{1,0:T(8,128)(2,1)S(1)}, u32[]{:S(2)}, u32[]{:S(2)}) %collective-permute-start) | collective-permute-done | bytes 208928 | tf_op jit(solution)/shard_map/ppermute | solution.py:24
  16.6 0.1 shard_map.122
  16.7 1.6 %collective-permute-start.4 = (bf16[256,384]{1,0:T(8,128)(2,1)S(1)}, bf16[256,384]{1,0:T(8,128)(2,1)S(1)}, u32[]{:S(2)}, u32[]{:S(2)}) collective-permute-start(bf16[256,384]{1,0:T(8,128)(2,1)S(1)} %get-tuple-element.60.refs_2_), channel_id=1, source_target_pairs={{0,2},{1,3},{2,0},{3,1},{4,6},{5,7},{6,4},{7,5},{8,10},{9,11},{10,... | collective-permute-start | bytes 589832 | tf_op jit(solution)/shard_map/ppermute | solution.py:28
  18.3 1.3 %collective-permute-start.2 = (bf16[272,384]{1,0:T(8,128)(2,1)S(1)}, bf16[272,384]{1,0:T(8,128)(2,1)S(1)}, u32[]{:S(2)}, u32[]{:S(2)}) collective-permute-start(bf16[272,384]{1,0:T(8,128)(2,1)S(1)} %get-tuple-element.57), channel_id=1, source_target_pairs={{0,12},{4,16},{8,20},{12,24},{16,28},{20,0},{24,4},{28,8},{1,13},{... | collective-permute-start | bytes 626696 | tf_op jit(solution)/shard_map/ppermute | solution.py:24
  19.6 0.5 collective-permute-start.3
  20.1 2.7 %collective-permute-done.4.refs_4_ = bf16[256,384]{1,0:T(8,128)(2,1)S(1)} collective-permute-done((bf16[256,384]{1,0:T(8,128)(2,1)S(1)}, bf16[256,384]{1,0:T(8,128)(2,1)S(1)}, u32[]{:S(2)}, u32[]{:S(2)}) %collective-permute-start.4) | collective-permute-done | bytes 196640 | tf_op jit(solution)/shard_map/ppermute | solution.py:28
  22.8 5.4 %collective-permute-done.1.refs_5_ = bf16[272,384]{1,0:T(8,128)(2,1)S(1)} collective-permute-done((bf16[272,384]{1,0:T(8,128)(2,1)S(1)}, bf16[272,384]{1,0:T(8,128)(2,1)S(1)}, u32[]{:S(2)}, u32[]{:S(2)}) %collective-permute-start.1) | collective-permute-done | bytes 208928 | tf_op jit(solution)/shard_map/ppermute | solution.py:24
  28.2 0.2 shard_map.123
  28.3 9.2 %collective-permute-done.2.refs_6_ = bf16[272,384]{1,0:T(8,128)(2,1)S(1)} collective-permute-done((bf16[272,384]{1,0:T(8,128)(2,1)S(1)}, bf16[272,384]{1,0:T(8,128)(2,1)S(1)}, u32[]{:S(2)}, u32[]{:S(2)}) %collective-permute-start.2) | collective-permute-done | bytes 208928 | tf_op jit(solution)/shard_map/ppermute | solution.py:24
  37.6 0.5 collective-permute-start.11
  38.1 0.2 shard_map.124
  38.3 0.1 collective-permute-start.10
  38.4 1.6 %collective-permute-start.14 = (bf16[256,384]{1,0:T(8,128)(2,1)S(1)}, bf16[256,384]{1,0:T(8,128)(2,1)S(1)}, u32[]{:S(2)}, u32[]{:S(2)}) collective-permute-start(bf16[256,384]{1,0:T(8,128)(2,1)S(1)} %get-tuple-element.76.refs_2_), channel_id=1, source_target_pairs={{0,2},{1,3},{2,0},{3,1},{4,6},{5,7},{6,4},{7,5},{8,10},{9,11},{10,... | collective-permute-start | bytes 589832 | tf_op jit(solution)/shard_map/ppermute | solution.py:28
  40.0 2.9 %shard_map.125 = (f32[1536,512]{1,0:T(8,128)S(1)}, f32[64,512]{1,0:T(8,128)S(1)}, bf16[64,256]{1,0:T(8,128)(2,1)S(1)}, bf16[256,256]{1,0:T(8,128)(2,1)S(1)}, bf1...) custom-call(f32[8,128]{1,0:T(8,128)S(1)} %get-tuple-element.58.refs_, ...), custom_call_target="tpu_custom_call" | custom-call | flops 1098907648 | tf_op jit(solution)/shard_map/pallas_call | solution.py:66
  42.9 0.3 shard_map.126
  43.2 0.6 collective-permute-start.17
  43.7 1.6 %collective-permute-done.11.refs_4_ = bf16[256,384]{1,0:T(8,128)(2,1)S(1)} collective-permute-done((bf16[256,384]{1,0:T(8,128)(2,1)S(1)}, bf16[256,384]{1,0:T(8,128)(2,1)S(1)}, u32[]{:S(2)}, u32[]{:S(2)}) %collective-permute-start.11) | collective-permute-done | bytes 196640 | tf_op jit(solution)/shard_map/ppermute | solution.py:28
  45.3 0.5 collective-permute-start.13
  45.8 3.7 %collective-permute-done.14.refs_4_ = bf16[256,384]{1,0:T(8,128)(2,1)S(1)} collective-permute-done((bf16[256,384]{1,0:T(8,128)(2,1)S(1)}, bf16[256,384]{1,0:T(8,128)(2,1)S(1)}, u32[]{:S(2)}, u32[]{:S(2)}) %collective-permute-start.14) | collective-permute-done | bytes 196640 | tf_op jit(solution)/shard_map/ppermute | solution.py:28
  49.5 0.5 collective-permute-start.16
  50.1 2.7 %collective-permute-done.17.refs_4_ = bf16[256,384]{1,0:T(8,128)(2,1)S(1)} collective-permute-done((bf16[256,384]{1,0:T(8,128)(2,1)S(1)}, bf16[256,384]{1,0:T(8,128)(2,1)S(1)}, u32[]{:S(2)}, u32[]{:S(2)}) %collective-permute-start.17) | collective-permute-done | bytes 196640 | tf_op jit(solution)/shard_map/ppermute | solution.py:28
  52.7 2.5 %shard_map.127 = (f32[1536,512]{1,0:T(8,128)S(1)}, f32[64,512]{1,0:T(8,128)S(1)}, bf16[64,256]{1,0:T(8,128)(2,1)S(1)}, f32[8,128]{1,0:T(8,128)S(1)}) custom-call(f32[8,128]{1,0:T(8,128)S(1)} %get-tuple-element.63.refs_0_, f32[8,128]{1,0:T(8,128)S(1)} %get-tuple-element.64.refs_1_.refs_2_, ...), custom_call_target="tpu_custom_call", output_to_operand_aliasing={{0}: (8, {}), {1}: (9, {})} | custom-call | flops 1098907648 | tf_op jit(solution)/shard_map/pallas_call | solution.py:66
  55.3 2.5 %shard_map.128 = (f32[1536,512]{1,0:T(8,128)S(1)}, f32[64,512]{1,0:T(8,128)S(1)}, bf16[64,256]{1,0:T(8,128)(2,1)S(1)}, f32[8,128]{1,0:T(8,128)S(1)}) custom-call(f32[8,128]{1,0:T(8,128)S(1)} %get-tuple-element.74.refs_0_, f32[8,128]{1,0:T(8,128)S(1)} %get-tuple-element.75.refs_1_.refs_3_, ...), custom_call_target="tpu_custom_call", output_to_operand_aliasing={{0}: (8, {}), {1}: (9, {})} | custom-call | flops 1098907648 | tf_op jit(solution)/shard_map/pallas_call | solution.py:66
  57.8 3.5 %shard_map.129 = (bf16[768,256]{1,0:T(8,128)(2,1)S(1)}, bf16[768,256]{1,0:T(8,128)(2,1)S(1)}, bf16[768,256]{1,0:T(8,128)(2,1)S(1)}, bf16[768,256]{1,0:T(8,128)(2...) custom-call(f32[8,128]{1,0:T(8,128)S(1)} %get-tuple-element.79.refs_0_, ...), custom_call_target="tpu_custom_call" | custom-call | flops 1098907648 | tf_op jit(solution)/shard_map/pallas_call | solution.py:66
  61.3 0.1 collective-permute-start.24
  61.5 0.1 collective-permute-start.21
  61.6 1.4 %shard_map.130 = (bf16[4,256,384]{2,1,0:T(8,128)(2,1)S(1)}, f32[4,64,384]{2,1,0:T(8,128)S(1)}, f32[8,128]{1,0:T(8,128)}) custom-call(f32[8,128]{1,0:T(8,128)S(1)} %get-tuple-element.84.refs_0_, f32[8,128]{1,0:T(8,128)S(1)} %get-tuple-element.59.refs_1_, f32[8,128]{1,0:T(8,128)S(1)} %get-tuple-element.64.refs_1_.refs_2_, ...), custom_call_target="tpu_custom_call" | custom-call | flops 201326592 | tf_op jit(solution)/shard_map/pallas_call | solution.py:66
  63.0 0.6 collective-permute-start.19
  63.6 9.3 %collective-permute-done.24 = bf16[768,256]{1,0:T(8,128)(2,1)S(1)} collective-permute-done((bf16[768,256]{1,0:T(8,128)(2,1)S(1)}, bf16[768,256]{1,0:T(8,128)(2,1)S(1)}, u32[]{:S(2)}, u32[]{:S(2)}) %collective-permute-start.24) | collective-permute-done | bytes 393248 | tf_op jit(solution)/shard_map/ppermute | solution.py:28
  72.9 0.1 add_convert_fusion
  73.0 0.1 collective-permute-start.25
  73.1 0.1 add_convert_fusion.1
  73.3 1.6 %collective-permute-start.22 = (bf16[2,1,192,256]{3,2,1,0:T(8,128)(2,1)S(1)}, bf16[2,1,192,256]{3,2,1,0:T(8,128)(2,1)S(1)}, u32[]{:S(2)}, u32[]{:S(2)}) collective-permute-start(bf16[2,1,192,256]{3,2,1,0:T(8,128)(2,1)S(1)} %constant_dynamic-slice_fusion.1), channel_id=1, source_target_pairs={{0,8},{4,12},{8,0},{12,4},{16,24},{20,28},{24,16},{28,20},{1,9},{5... | collective-permute-start | bytes 589832 | tf_op jit(solution)/shard_map/ppermute | solution.py:28
  74.8 0.1 add_convert_fusion.2
  75.0 0.6 collective-permute-start.20
  75.5 9.1 %collective-permute-done.25 = bf16[1,2,192,256]{3,2,1,0:T(8,128)(2,1)S(1)} collective-permute-done((bf16[1,2,192,256]{3,2,1,0:T(8,128)(2,1)S(1)}, bf16[1,2,192,256]{3,2,1,0:T(8,128)(2,1)S(1)}, u32[]{:S(2)}, u32[]{:S(2)}) %collective-permute-start.25) | collective-permute-done | bytes 196640 | tf_op jit(solution)/shard_map/ppermute | solution.py:28
  84.7 0.1 collective-permute-start.26
  84.9 0.5 collective-permute-start.23
  85.5 0.7 add_convert_fusion.5
  86.2 5.1 %collective-permute-done.23 = bf16[1,192,256]{2,1,0:T(8,128)(2,1)S(1)} collective-permute-done((bf16[1,192,256]{2,1,0:T(8,128)(2,1)S(1)}, bf16[1,192,256]{2,1,0:T(8,128)(2,1)S(1)}, u32[]{:S(2)}, u32[]{:S(2)}) %collective-permute-start.23) | collective-permute-done | bytes 98336 | tf_op jit(solution)/shard_map/ppermute | solution.py:28
  91.3 0.7 fusion.1
  92.0 0.7 fusion
  (49 shorter events, 0.4 us)
Async XLA Ops:
  0.6 39.3 %copy-start.4 = (bf16[4,64,384]{2,1,0:T(8,128)(2,1)S(1)}, bf16[4,64,384]{2,1,0:T(8,128)(2,1)}, u32[]{:S(2)}) copy-start(bf16[4,64,384]{2,1,0:T(8,128)(2,1)} %param.19) | copy-start | bytes 589828
  0.6 39.3 %copy-start.3 = (bf16[64,1536]{1,0:T(8,128)(2,1)S(1)}, bf16[64,1536]{1,0:T(8,128)(2,1)}, u32[]{:S(2)}) copy-start(bf16[64,1536]{1,0:T(8,128)(2,1)} %refs_9_.3) | copy-start | bytes 589828
  0.7 39.3 %copy-start.5 = (bf16[64,256]{1,0:T(8,128)(2,1)S(1)}, bf16[64,256]{1,0:T(8,128)(2,1)}, u32[]{:S(2)}) copy-start(bf16[64,256]{1,0:T(8,128)(2,1)} %refs_9_.2) | copy-start | bytes 98308
  0.7 39.3 %copy-start = (bf16[1536,256]{1,0:T(8,128)(2,1)S(1)}, bf16[1536,256]{1,0:T(8,128)(2,1)}, u32[]{:S(2)}) copy-start(bf16[1536,256]{1,0:T(8,128)(2,1)} %refs_6_.7) | copy-start | bytes 2359300
  0.7 39.3 %copy-start.1 = (bf16[1536,256]{1,0:T(8,128)(2,1)S(1)}, bf16[1536,256]{1,0:T(8,128)(2,1)}, u32[]{:S(2)}) copy-start(bf16[1536,256]{1,0:T(8,128)(2,1)} %refs_7_.7) | copy-start | bytes 2359300
  0.7 0.8 copy-start.6
  1.5 0.7 copy-start.7
  2.2 0.7 copy-start.8
  2.8 37.2 %copy-start.2 = (bf16[256,1536]{1,0:T(8,128)(2,1)S(1)}, bf16[256,1536]{1,0:T(8,128)(2,1)}, u32[]{:S(2)}) copy-start(bf16[256,1536]{1,0:T(8,128)(2,1)} %refs_10_.3) | copy-start | bytes 2359300
  5.4 11.2 %collective-permute-start = (bf16[272,384]{1,0:T(8,128)(2,1)S(1)}, bf16[272,384]{1,0:T(8,128)(2,1)S(1)}, u32[]{:S(2)}, u32[]{:S(2)}) collective-permute-start(bf16[272,384]{1,0:T(8,128)(2,1)S(1)} %get-tuple-element.53), channel_id=1, source_target_pairs={{0,4},{4,8},{8,12},{12,16},{16,20},{20,24},{24,28},{28,0},{1,5},{5... | collective-permute-start | bytes 626696 | tf_op jit(solution)/shard_map/ppermute | solution.py:24
  8.0 11.5 %collective-permute-start.7 = (bf16[256,384]{1,0:T(8,128)(2,1)}, bf16[256,384]{1,0:T(8,128)(2,1)S(1)}, u32[]{:S(2)}, u32[]{:S(2)}) collective-permute-start(bf16[256,384]{1,0:T(8,128)(2,1)} %bitcast.21), channel_id=1, source_target_pairs={{0,2},{1,3},{2,0},{3,1},{4,6},{5,7},{6,4},{7,5},{8,10},{9,11},{10,... | collective-permute-start | bytes 589832 | tf_op jit(solution)/shard_map/ppermute | solution.py:28
  9.6 10.0 %collective-permute-start.6 = (bf16[256,384]{1,0:T(8,128)(2,1)}, bf16[256,384]{1,0:T(8,128)(2,1)S(1)}, u32[]{:S(2)}, u32[]{:S(2)}) collective-permute-start(bf16[256,384]{1,0:T(8,128)(2,1)} %bitcast.22), channel_id=1, source_target_pairs={{0,1},{1,0},{2,3},{3,2},{4,5},{5,4},{6,7},{7,6},{8,9},{9,8},{10,11... | collective-permute-start | bytes 589832 | tf_op jit(solution)/shard_map/ppermute | solution.py:28
  16.7 6.1 %collective-permute-start.4 = (bf16[256,384]{1,0:T(8,128)(2,1)S(1)}, bf16[256,384]{1,0:T(8,128)(2,1)S(1)}, u32[]{:S(2)}, u32[]{:S(2)}) collective-permute-start(bf16[256,384]{1,0:T(8,128)(2,1)S(1)} %get-tuple-element.60.refs_2_), channel_id=1, source_target_pairs={{0,2},{1,3},{2,0},{3,1},{4,6},{5,7},{6,4},{7,5},{8,10},{9,11},{10,... | collective-permute-start | bytes 589832 | tf_op jit(solution)/shard_map/ppermute | solution.py:28
  18.3 9.9 %collective-permute-start.1 = (bf16[272,384]{1,0:T(8,128)(2,1)S(1)}, bf16[272,384]{1,0:T(8,128)(2,1)S(1)}, u32[]{:S(2)}, u32[]{:S(2)}) collective-permute-start(bf16[272,384]{1,0:T(8,128)(2,1)S(1)} %get-tuple-element.55), channel_id=1, source_target_pairs={{0,8},{4,12},{8,16},{12,20},{16,24},{20,28},{24,0},{28,4},{1,9},{5... | collective-permute-start | bytes 626696 | tf_op jit(solution)/shard_map/ppermute | solution.py:24
  18.3 19.3 %collective-permute-start.2 = (bf16[272,384]{1,0:T(8,128)(2,1)S(1)}, bf16[272,384]{1,0:T(8,128)(2,1)S(1)}, u32[]{:S(2)}, u32[]{:S(2)}) collective-permute-start(bf16[272,384]{1,0:T(8,128)(2,1)S(1)} %get-tuple-element.57), channel_id=1, source_target_pairs={{0,12},{4,16},{8,20},{12,24},{16,28},{20,0},{24,4},{28,8},{1,13},{... | collective-permute-start | bytes 626696 | tf_op jit(solution)/shard_map/ppermute | solution.py:24
  19.6 18.7 %collective-permute-start.8 = (bf16[256,384]{1,0:T(8,128)(2,1)S(1)}, bf16[256,384]{1,0:T(8,128)(2,1)S(1)}, u32[]{:S(2)}, u32[]{:S(2)}) collective-permute-start(bf16[256,384]{1,0:T(8,128)(2,1)S(1)} %collective-permute-done.7.refs_13_), channel_id=1, source_target_pairs={{0,1},{1,0},{2,3},{3,2},{4,5},{5,4},{6,7},{7,6},{8,9},{9,8},{10,11... | collective-permute-start | bytes 589832 | tf_op jit(solution)/shard_map/ppermute | solution.py:28
  19.6 18.8 %collective-permute-start.3 = (bf16[256,384]{1,0:T(8,128)(2,1)S(1)}, bf16[256,384]{1,0:T(8,128)(2,1)S(1)}, u32[]{:S(2)}, u32[]{:S(2)}) collective-permute-start(bf16[256,384]{1,0:T(8,128)(2,1)S(1)} %get-tuple-element.60.refs_2_), channel_id=1, source_target_pairs={{0,1},{1,0},{2,3},{3,2},{4,5},{5,4},{6,7},{7,6},{8,9},{9,8},{10,11... | collective-permute-start | bytes 589832 | tf_op jit(solution)/shard_map/ppermute | solution.py:28
  22.8 17.1 %collective-permute-start.5 = (bf16[256,384]{1,0:T(8,128)(2,1)S(1)}, bf16[256,384]{1,0:T(8,128)(2,1)S(1)}, u32[]{:S(2)}, u32[]{:S(2)}) collective-permute-start(bf16[256,384]{1,0:T(8,128)(2,1)S(1)} %collective-permute-done.4.refs_4_), channel_id=1, source_target_pairs={{0,1},{1,0},{2,3},{3,2},{4,5},{5,4},{6,7},{7,6},{8,9},{9,8},{10,11... | collective-permute-start | bytes 589832 | tf_op jit(solution)/shard_map/ppermute | solution.py:28
  28.2 14.7 %collective-permute-start.9 = (bf16[272,384]{1,0:T(8,128)(2,1)S(1)}, bf16[272,384]{1,0:T(8,128)(2,1)S(1)}, u32[]{:S(2)}, u32[]{:S(2)}) collective-permute-start(bf16[272,384]{1,0:T(8,128)(2,1)S(1)} %get-tuple-element.62), channel_id=1, source_target_pairs={{0,16},{4,20},{8,24},{12,28},{16,0},{20,4},{24,8},{28,12},{1,17},{... | collective-permute-start | bytes 626696 | tf_op jit(solution)/shard_map/ppermute | solution.py:24
  37.6 7.8 %collective-permute-start.11 = (bf16[256,384]{1,0:T(8,128)(2,1)S(1)}, bf16[256,384]{1,0:T(8,128)(2,1)S(1)}, u32[]{:S(2)}, u32[]{:S(2)}) collective-permute-start(bf16[256,384]{1,0:T(8,128)(2,1)S(1)} %get-tuple-element.65.refs_2_), channel_id=1, source_target_pairs={{0,2},{1,3},{2,0},{3,1},{4,6},{5,7},{6,4},{7,5},{8,10},{9,11},{10,... | collective-permute-start | bytes 589832 | tf_op jit(solution)/shard_map/ppermute | solution.py:28
  38.3 11.3 %collective-permute-start.10 = (bf16[256,384]{1,0:T(8,128)(2,1)S(1)}, bf16[256,384]{1,0:T(8,128)(2,1)S(1)}, u32[]{:S(2)}, u32[]{:S(2)}) collective-permute-start(bf16[256,384]{1,0:T(8,128)(2,1)S(1)} %get-tuple-element.65.refs_2_), channel_id=1, source_target_pairs={{0,1},{1,0},{2,3},{3,2},{4,5},{5,4},{6,7},{7,6},{8,9},{9,8},{10,11... | collective-permute-start | bytes 589832 | tf_op jit(solution)/shard_map/ppermute | solution.py:28
  38.4 11.2 %collective-permute-start.14 = (bf16[256,384]{1,0:T(8,128)(2,1)S(1)}, bf16[256,384]{1,0:T(8,128)(2,1)S(1)}, u32[]{:S(2)}, u32[]{:S(2)}) collective-permute-start(bf16[256,384]{1,0:T(8,128)(2,1)S(1)} %get-tuple-element.76.refs_2_), channel_id=1, source_target_pairs={{0,2},{1,3},{2,0},{3,1},{4,6},{5,7},{6,4},{7,5},{8,10},{9,11},{10,... | collective-permute-start | bytes 589832 | tf_op jit(solution)/shard_map/ppermute | solution.py:28
  43.2 9.5 %collective-permute-start.17 = (bf16[256,384]{1,0:T(8,128)(2,1)S(1)}, bf16[256,384]{1,0:T(8,128)(2,1)S(1)}, u32[]{:S(2)}, u32[]{:S(2)}) collective-permute-start(bf16[256,384]{1,0:T(8,128)(2,1)S(1)} %get-tuple-element.81.refs_2_), channel_id=1, source_target_pairs={{0,2},{1,3},{2,0},{3,1},{4,6},{5,7},{6,4},{7,5},{8,10},{9,11},{10,... | collective-permute-start | bytes 589832 | tf_op jit(solution)/shard_map/ppermute | solution.py:28
  45.3 7.4 %collective-permute-start.12 = (bf16[256,384]{1,0:T(8,128)(2,1)S(1)}, bf16[256,384]{1,0:T(8,128)(2,1)S(1)}, u32[]{:S(2)}, u32[]{:S(2)}) collective-permute-start(bf16[256,384]{1,0:T(8,128)(2,1)S(1)} %collective-permute-done.11.refs_4_), channel_id=1, source_target_pairs={{0,1},{1,0},{2,3},{3,2},{4,5},{5,4},{6,7},{7,6},{8,9},{9,8},{10,11... | collective-permute-start | bytes 589832 | tf_op jit(solution)/shard_map/ppermute | solution.py:28
  45.3 9.9 %collective-permute-start.13 = (bf16[256,384]{1,0:T(8,128)(2,1)S(1)}, bf16[256,384]{1,0:T(8,128)(2,1)S(1)}, u32[]{:S(2)}, u32[]{:S(2)}) collective-permute-start(bf16[256,384]{1,0:T(8,128)(2,1)S(1)} %get-tuple-element.76.refs_2_), channel_id=1, source_target_pairs={{0,1},{1,0},{2,3},{3,2},{4,5},{5,4},{6,7},{7,6},{8,9},{9,8},{10,11... | collective-permute-start | bytes 589832 | tf_op jit(solution)/shard_map/ppermute | solution.py:28
  49.5 5.7 %collective-permute-start.15 = (bf16[256,384]{1,0:T(8,128)(2,1)S(1)}, bf16[256,384]{1,0:T(8,128)(2,1)S(1)}, u32[]{:S(2)}, u32[]{:S(2)}) collective-permute-start(bf16[256,384]{1,0:T(8,128)(2,1)S(1)} %collective-permute-done.14.refs_4_), channel_id=1, source_target_pairs={{0,1},{1,0},{2,3},{3,2},{4,5},{5,4},{6,7},{7,6},{8,9},{9,8},{10,11... | collective-permute-start | bytes 589832 | tf_op jit(solution)/shard_map/ppermute | solution.py:28
  49.5 8.2 %collective-permute-start.16 = (bf16[256,384]{1,0:T(8,128)(2,1)S(1)}, bf16[256,384]{1,0:T(8,128)(2,1)S(1)}, u32[]{:S(2)}, u32[]{:S(2)}) collective-permute-start(bf16[256,384]{1,0:T(8,128)(2,1)S(1)} %get-tuple-element.81.refs_2_), channel_id=1, source_target_pairs={{0,1},{1,0},{2,3},{3,2},{4,5},{5,4},{6,7},{7,6},{8,9},{9,8},{10,11... | collective-permute-start | bytes 589832 | tf_op jit(solution)/shard_map/ppermute | solution.py:28
  52.7 5.1 %collective-permute-start.18 = (bf16[256,384]{1,0:T(8,128)(2,1)S(1)}, bf16[256,384]{1,0:T(8,128)(2,1)S(1)}, u32[]{:S(2)}, u32[]{:S(2)}) collective-permute-start(bf16[256,384]{1,0:T(8,128)(2,1)S(1)} %collective-permute-done.17.refs_4_), channel_id=1, source_target_pairs={{0,1},{1,0},{2,3},{3,2},{4,5},{5,4},{6,7},{7,6},{8,9},{9,8},{10,11... | collective-permute-start | bytes 589832 | tf_op jit(solution)/shard_map/ppermute | solution.py:28
  61.3 11.6 %collective-permute-start.24 = (bf16[768,256]{1,0:T(8,128)(2,1)S(1)}, bf16[768,256]{1,0:T(8,128)(2,1)S(1)}, u32[]{:S(2)}, u32[]{:S(2)}) collective-permute-start(bf16[768,256]{1,0:T(8,128)(2,1)S(1)} %get-tuple-element.94), channel_id=1, source_target_pairs={{0,8},{4,12},{8,0},{12,4},{16,24},{20,28},{24,16},{28,20},{1,9},{5... | collective-permute-start | bytes 1179656 | tf_op jit(solution)/shard_map/ppermute | solution.py:28
  61.5 11.6 %collective-permute-start.21 = (bf16[768,256]{1,0:T(8,128)(2,1)S(1)}, bf16[768,256]{1,0:T(8,128)(2,1)S(1)}, u32[]{:S(2)}, u32[]{:S(2)}) collective-permute-start(bf16[768,256]{1,0:T(8,128)(2,1)S(1)} %get-tuple-element.92), channel_id=1, source_target_pairs={{0,4},{4,0},{8,12},{12,8},{16,20},{20,16},{24,28},{28,24},{1,5},{5... | collective-permute-start | bytes 1179656 | tf_op jit(solution)/shard_map/ppermute | solution.py:28
  63.0 11.8 %collective-permute-start.19 = (bf16[2,1,256,384]{3,2,1,0:T(8,128)(2,1)S(1)}, bf16[2,1,256,384]{3,2,1,0:T(8,128)(2,1)S(1)}, u32[]{:S(2)}, u32[]{:S(2)}) collective-permute-start(bf16[2,1,256,384]{3,2,1,0:T(8,128)(2,1)S(1)} %constant_dynamic-slice_fusion.3), channel_id=1, source_target_pairs={{0,1},{1,0},{2,3},{3,2},{4,5},{5,4},{6,7},{7,6},{8,9},{9,8},{10,11... | collective-permute-start | bytes 1179656 | tf_op jit(solution)/shard_map/ppermute | solution.py:28
  73.0 11.6 %collective-permute-start.25 = (bf16[1,2,192,256]{3,2,1,0:T(8,128)(2,1)S(1)}, bf16[1,2,192,256]{3,2,1,0:T(8,128)(2,1)S(1)}, u32[]{:S(2)}, u32[]{:S(2)}) collective-permute-start(bf16[1,2,192,256]{3,2,1,0:T(8,128)(2,1)S(1)} %constant_dynamic-slice_fusion), channel_id=1, source_target_pairs={{0,16},{4,20},{8,24},{12,28},{16,0},{20,4},{24,8},{28,12},{1,17},{... | collective-permute-start | bytes 589832 | tf_op jit(solution)/shard_map/ppermute | solution.py:28
  73.3 11.6 %collective-permute-start.22 = (bf16[2,1,192,256]{3,2,1,0:T(8,128)(2,1)S(1)}, bf16[2,1,192,256]{3,2,1,0:T(8,128)(2,1)S(1)}, u32[]{:S(2)}, u32[]{:S(2)}) collective-permute-start(bf16[2,1,192,256]{3,2,1,0:T(8,128)(2,1)S(1)} %constant_dynamic-slice_fusion.1), channel_id=1, source_target_pairs={{0,8},{4,12},{8,0},{12,4},{16,24},{20,28},{24,16},{28,20},{1,9},{5... | collective-permute-start | bytes 589832 | tf_op jit(solution)/shard_map/ppermute | solution.py:28
  75.0 10.4 %collective-permute-start.20 = (bf16[1,1,256,384]{3,2,1,0:T(8,128)(2,1)S(1)}, bf16[1,1,256,384]{3,2,1,0:T(8,128)(2,1)S(1)}, u32[]{:S(2)}, u32[]{:S(2)}) collective-permute-start(bf16[1,1,256,384]{3,2,1,0:T(8,128)(2,1)S(1)} %constant_dynamic-slice_fusion.2), channel_id=1, source_target_pairs={{0,2},{1,3},{2,0},{3,1},{4,6},{5,7},{6,4},{7,5},{8,10},{9,11},{10,... | collective-permute-start | bytes 589832 | tf_op jit(solution)/shard_map/ppermute | solution.py:28
  84.7 7.3 %collective-permute-start.26 = (bf16[1,192,256]{2,1,0:T(8,128)(2,1)S(1)}, bf16[1,192,256]{2,1,0:T(8,128)(2,1)S(1)}, u32[]{:S(2)}, u32[]{:S(2)}) collective-permute-start(bf16[1,192,256]{2,1,0:T(8,128)(2,1)S(1)} %dynamic-slice_bitcast_fusion), channel_id=1, source_target_pairs={{0,4},{4,0},{8,12},{12,8},{16,20},{20,16},{24,28},{28,24},{1,5},{5... | collective-permute-start | bytes 294920 | tf_op jit(solution)/shard_map/ppermute | solution.py:28
  84.9 6.4 %collective-permute-start.23 = (bf16[1,192,256]{2,1,0:T(8,128)(2,1)S(1)}, bf16[1,192,256]{2,1,0:T(8,128)(2,1)S(1)}, u32[]{:S(2)}, u32[]{:S(2)}) collective-permute-start(bf16[1,192,256]{2,1,0:T(8,128)(2,1)S(1)} %dynamic-slice_bitcast_fusion.1), channel_id=1, source_target_pairs={{0,16},{4,20},{8,24},{12,28},{16,0},{20,4},{24,8},{28,12},{1,17},{... | collective-permute-start | bytes 294920 | tf_op jit(solution)/shard_map/ppermute | solution.py:28

commit v2 on v1

--- a/solution.py
+++ b/solution.py
@@ -9,7 +9,7 @@
 
 
 HEAD = 64
-MARK_ROWS = 16
+MARK_ROWS = 8
 VMEM_BYTES = 67043328
 SPARE = 12000000
 norm_epsilon = 1e-05
@@ -21,7 +21,10 @@
 
 def from_behind(block, axis, distance):
     size = lax.axis_size(axis)
-    return lax.ppermute(block, axis, [(i, (i + distance) % size) for i in range(size)])
+    route = [(i, (i + distance) % size) for i in range(size)]
+    if distance >= 3:
+        route = [(i, j) for i, j in route if j > i]
+    return lax.ppermute(block, axis, route)
 
 
 def flip(block, axis, bit):
@@ -98,12 +101,6 @@
     return slot - start
 
 
-def time_row(time_ref, position):
-    table = time_ref[...].astype(f32)
-    rows = lax.broadcasted_iota(jnp.int32, table.shape, 0)
-    return jnp.sum(jnp.where(rows == position, table, 0.0), axis=0, keepdims=True)
-
-
 def fetch(pairs, sems):
     copies = [pltpu.make_async_copy(src, dst, sems.at[i]) for i, (src, dst) in enumerate(pairs)]
     for copy in copies:
@@ -111,13 +108,11 @@
     return copies
 
 
-def prep_body(work, reach, plan_hbm, doc_hbm, time_hbm, media_ref, *rest):
+def prep_body(work, reach, plan_hbm, doc_hbm, media_ref, *rest):
     sends = rest[:reach]
-    own_ref, rows_ref, facts_ref, held, plan_ref, doc_ref, time_ref, sems, own_sems, more = rest[
-        reach:
-    ]
+    own_ref, facts_ref, plan_ref, doc_ref, sems, own_sems, more = rest[reach:]
     slots, tokens, width = media_ref.shape
-    early = fetch([(plan_hbm, plan_ref), (doc_hbm, doc_ref), (time_hbm, time_ref)], more)
+    early = fetch([(plan_hbm, plan_ref), (doc_hbm, doc_ref)], more)
     for copy in early:
         copy.wait()
     codes = [plan_ref[0, s] for s in range(slots)]
@@ -130,7 +125,10 @@
             slot = jnp.where(hit, s, slot)
             mark = jnp.where(hit, codes[s] - k * work + 1, mark)
         chosen.append((slot, mark))
-    copies = fetch([(media_ref.at[slot], held.at[k]) for k, (slot, _) in enumerate(chosen)], sems)
+    copies = fetch(
+        [(media_ref.at[slot], sends[k].at[pl.ds(0, tokens)]) for k, (slot, _) in enumerate(chosen)],
+        sems,
+    )
     own_slots = [jnp.int32(0)] * work
     own_codes = [jnp.int32(0)] * work
     rank = jnp.int32(0)
@@ -143,37 +141,42 @@
         rank = rank + own.astype(jnp.int32)
     own_copies = fetch([(media_ref.at[own_slots[w]], own_ref.at[w]) for w in range(work)], own_sems)
 
-    def splat(value):
-        return jnp.full((1, width), value.astype(f32), f32)
+    def splat(value, height=1):
+        return jnp.full((height, width), value.astype(f32), f32)
 
     facts_ref[...] = jnp.zeros(facts_ref.shape, f32)
-    facts_ref[pl.ds(work, 1), :] = splat(rank)
+    facts_ref[pl.ds(2 * work, 1), :] = splat(rank)
     for w in range(work):
         facts_ref[pl.ds(w, 1), :] = splat(own_codes[w])
-        rows_ref[pl.ds(w, 1), :] = time_row(time_ref, slot_position(doc_ref, own_slots[w]))
+        facts_ref[pl.ds(work + w, 1), :] = splat(slot_position(doc_ref, own_slots[w]))
     for k in range(reach):
         slot, mark = chosen[k]
-        row = time_row(time_ref, slot_position(doc_ref, slot))
-        sends[k][pl.ds(tokens, MARK_ROWS), :] = jnp.full(
-            (MARK_ROWS, width), mark.astype(f32), f32
-        ).astype(bf16)
-        copies[k].wait()
-        sends[k][pl.ds(0, tokens), :] = (held[k].astype(f32) + row).astype(bf16)
-    for copy in own_copies:
+        row = lax.broadcasted_iota(jnp.int32, (MARK_ROWS, width), 0)
+        place = splat(slot_position(doc_ref, slot), MARK_ROWS)
+        signs = jnp.where(row == 0, splat(mark, MARK_ROWS), place)
+        sends[k][pl.ds(tokens, MARK_ROWS), :] = signs.astype(bf16)
+    for copy in copies + own_copies:
         copy.wait()
+
+
+def table_body(time_hbm, out_ref, held, sems):
+    (copy,) = fetch([(time_hbm, held)], sems)
+    copy.wait()
+    out_ref[...] = held[...].astype(f32)
 
 
 def seen_at(work, reach, place):
     return min(max(reach - work + place + 1, 0), reach)
 
 
-def select_body(work, reach, place, facts_ref, rows_ref, own_ref, *rest):
+def select_body(work, reach, place, facts_ref, time_ref, own_ref, *rest):
     seen = seen_at(work, reach, place)
     arrivals = rest[:seen]
     out_ref, info_ref = rest[seen:]
     tokens, width = out_ref.shape
-    own_count = facts_ref[pl.ds(work, 1), :]
-    marks = [ref[pl.ds(tokens, MARK_ROWS), :].astype(f32)[:1] for ref in arrivals]
+    own_count = facts_ref[pl.ds(2 * work, 1), :]
+    signs = [ref[pl.ds(tokens, MARK_ROWS), :].astype(f32) for ref in arrivals]
+    marks = [sign[0:1] for sign in signs]
     lives = [jnp.minimum(mark, 1.0) for mark in marks]
     taken = jnp.zeros((1, width), f32)
     for p in range(place + 1):
@@ -184,21 +187,24 @@
         taken = jnp.minimum(taken + 1.0, ready)
     alive = taken - before
     target = jnp.zeros((1, width), f32)
-    row = jnp.zeros((1, width), f32)
+    position = jnp.zeros((1, width), f32)
     raw = jnp.zeros((tokens, width), bf16)
     for w in range(min(work, place + 1)):
         weight = jnp.where((before == w) & (own_count > w), 1.0, 0.0)
         target = target + weight * facts_ref[pl.ds(w, 1), :]
-        row = row + weight * rows_ref[pl.ds(w, 1), :]
+        position = position + weight * facts_ref[pl.ds(work + w, 1), :]
         raw = raw + own_ref[w] * weight.astype(bf16)
-    block = (raw.astype(f32) + row).astype(bf16)
     rank = own_count
     for k in range(seen):
         weight = jnp.where(rank == before, lives[k], 0.0)
         target = target + weight * (marks[k] - 1.0)
-        block = block + arrivals[k][pl.ds(0, tokens), :] * weight.astype(bf16)
+        position = position + weight * signs[k][1:2]
+        raw = raw + arrivals[k][pl.ds(0, tokens), :] * weight.astype(bf16)
         rank = rank + lives[k]
-    out_ref[...] = block
+    table = time_ref[...]
+    rows = lax.broadcasted_iota(jnp.int32, table.shape, 0).astype(f32)
+    row = jnp.sum(jnp.where(rows == position, table, 0.0), axis=0, keepdims=True) * alive
+    out_ref[...] = (raw.astype(f32) + row).astype(bf16)
     lanes = info_ref.shape[1]
     info_ref[...] = jnp.zeros(info_ref.shape, f32)
     info_ref[pl.ds(0, 1), :] = target[:, :lanes]
@@ -414,35 +420,44 @@
     shape = jax.ShapeDtypeStruct
     chain = Chain()
 
-    fact_rows = -(-(work + 1) // 8) * 8
-    *sends, own, own_rows, facts = chain.call(
+    fact_rows = -(-(2 * work + 1) // 8) * 8
+    *sends, own, facts = chain.call(
         functools.partial(prep_body, work, reach),
         [shape((tokens + MARK_ROWS, width), bf16)] * reach
-        + [
-            shape((work, tokens, width), bf16),
-            shape((fact_rows, width), f32),
-            shape((fact_rows, width), f32),
-        ],
-        [HBM] * 4,
-        [VMEM] * (reach + 3),
-        (plan, doc_images, time_table, media),
+        + [shape((work, tokens, width), bf16), shape((fact_rows, width), f32)],
+        [HBM] * 3,
+        [VMEM] * (reach + 2),
+        (plan, doc_images, media),
         [
-            pltpu.VMEM((reach, tokens, width), bf16),
             pltpu.SMEM(plan.shape, jnp.int32),
             pltpu.SMEM(doc_images.shape, jnp.int32),
-            pltpu.VMEM(time_table.shape, bf16),
             pltpu.SemaphoreType.DMA((reach,)),
             pltpu.SemaphoreType.DMA((work,)),
-            pltpu.SemaphoreType.DMA((3,)),
+            pltpu.SemaphoreType.DMA((2,)),
         ],
         moved=(reach + work) * tokens * width * 4,
         full=True,
         spare=SPARE,
     )
     arrivals = []
-    for k in range(1, reach + 1):
+    for k in range(2, reach + 1):
         arrivals.append(from_behind(sends[k - 1], "dp", k))
+    if dp % 2 == 0:
+        near = flip(sends[0], "dp", 1)
+        route = [(i, i if i % 2 else (i + 2) % dp) for i in range(dp)]
+        arrivals.append(lax.ppermute(near, "dp", route))
+    else:
+        arrivals.append(from_behind(sends[0], "dp", 1))
     cot_blocks = gather_blocks(cotangent.reshape(work * latent_count, width), "mp")
+    (table,) = chain.call(
+        table_body,
+        [shape(time_table.shape, f32)],
+        [HBM],
+        [VMEM],
+        (time_table,),
+        [pltpu.VMEM(time_table.shape, bf16), pltpu.SemaphoreType.DMA((1,))],
+        limit=1,
+    )
     infos = []
     gathered = []
     attended = []
@@ -456,7 +471,7 @@
             [shape((tokens, width), bf16), shape((8, 128), f32)],
             [VMEM] * (seen + 3),
             [VMEM, VMEM],
-            (facts, own_rows, own, *arrivals[:seen]),
+            (facts, table, own, *arrivals[:seen]),
             moved=tokens * width * 4,
             limit=2,
         )
@@ -519,10 +534,10 @@
             shared = tuple(results[len(new) + 1 :])
 
     for p in range(work):
-        if p >= 3:
-            place(p - 3)
+        if p == 2:
+            place(0)
         select(p)
-    for p in range(max(work - 3, 0), work):
+    for p in range(int(work > 2), work):
         place(p)
     carried = sums
 

time: 92.9 us -> 93.9 us (1.011)
  starting transfers between devices: 14.9 us -> 35.4 us
  waiting for transfers between devices: 55.8 us -> 36.3 us
    ppermute x4, starting transfers between devices: 3.98 us -> 21.3 us  [the longest x3 11.8 us: from_behind(): return lax.ppermute(block, axis, route)]
    ppermute x4, waiting for transfers between devices: 21.6 us -> 5.47 us  [the longest x3 5.47 us: from_behind(): return lax.ppermute(block, axis, route)]
    ppermute x23 -> x24, waiting for transfers between devices: 34.3 us -> 30.8 us  [flip(): lax.ppermute(block, axis, [(i, i ^ bit) for i in range(lax.axis_size(axis...]
    ppermute x23 -> x24, starting transfers between devices: 10.9 us -> 14.1 us  [flip(): lax.ppermute(block, axis, [(i, i ^ bit) for i in range(lax.axis_size(axis...]
    pallas_call x10 -> x11, Pallas kernels: 16 us -> 16 us  [call(): pl.pallas_call(chained, out_shape=[*outs, jax.ShapeDtypeStruct((8, 128),...]
  transfers between devices with their start and end apart: 27 -> 28, of which waited for: 10 -> 9; matrix products, arithmetic and copies ran while one was open for 2% -> 2% of each run, Pallas kernels for 11% -> 11%
where the time goes in v2:
time: 93.9 us; the launch traced here: 93.6 us
  waiting for transfers between devices  36.3 us (39%)
  starting transfers between devices  35.4 us (38%)
  Pallas kernels  16 us (17%)
  other arithmetic  2.61 us (3%)
  local copies, waits for them, and re-layouts  2.31 us (2%)
  between operations  0.95 us (1%)
    ppermute x24, waiting for transfers between devices, flip(): lax.ppermute(block, axis, [(i, i ^ bit) for i in range(lax.axis_size(axis...  30.8 us
    pallas_call x11, Pallas kernels, call(): pl.pallas_call(chained, out_shape=[*outs, jax.ShapeDtypeStruct((8, 128),...  16 us
    ppermute x24, starting transfers between devices, flip(): lax.ppermute(block, axis, [(i, i ^ bit) for i in range(lax.axis_size(axis...  14.1 us
    ppermute x3, starting transfers between devices, from_behind(): return lax.ppermute(block, axis, route)  11.8 us
    ppermute x1, starting transfers between devices, layer(): arrivals.append(lax.ppermute(near, 'dp', route))  9.53 us
    ppermute x3, waiting for transfers between devices, from_behind(): return lax.ppermute(block, axis, route)  5.47 us
    unnamed x18, local copies, waits for them, and re-layouts  2.16 us
  transfers between devices with their start and end apart: 28, of which 9 were waited for; matrix products, arithmetic and copies ran while one was open for 2% of the time, Pallas kernels for 11%

profile of v2, /device:TPU:0, one launch (start us, length us, event | category | flops | bytes accessed | tf_op | source)
XLA Modules:
  0.0 93.6 jit_solution(17015817553028572143)
XLA Ops:
  0.7 0.8 copy-done.7
  1.5 0.7 copy-done.8
  2.1 2.5 %shard_map.121 = (bf16[264,384]{1,0:T(8,128)(2,1)S(1)}, bf16[264,384]{1,0:T(8,128)(2,1)S(1)}, bf16[264,384]{1,0:T(8,128)(2,1)S(1)}, bf16[264,384]{1,0:T(8,128)(2...) custom-call(s32[1,8]{1,0:T(1,128)S(1)} %copy-done.7, s32[2]{0:T(128)S(1)} %copy-done.8, ...), custom_call_target="tpu_custom_call" | custom-call | bytes 3145728 | tf_op jit(solution)/shard_map/pallas_call | solution.py:69
  4.6 2.8 %collective-permute-start = (bf16[264,384]{1,0:T(8,128)(2,1)S(1)}, bf16[264,384]{1,0:T(8,128)(2,1)S(1)}, u32[]{:S(2)}, u32[]{:S(2)}) collective-permute-start(bf16[264,384]{1,0:T(8,128)(2,1)S(1)} %get-tuple-element.55), channel_id=1, source_target_pairs={{0,8},{4,12},{8,16},{12,20},{16,24},{20,28},{24,0},{28,4},{1,9},{5... | collective-permute-start | bytes 608264 | tf_op jit(solution)/shard_map/ppermute | solution.py:27
  7.5 1.5 %collective-permute-start.6 = (bf16[256,384]{1,0:T(8,128)(2,1)}, bf16[256,384]{1,0:T(8,128)(2,1)S(1)}, u32[]{:S(2)}, u32[]{:S(2)}) collective-permute-start(bf16[256,384]{1,0:T(8,128)(2,1)} %bitcast.21), channel_id=1, source_target_pairs={{0,2},{1,3},{2,0},{3,1},{4,6},{5,7},{6,4},{7,5},{8,10},{9,11},{10,... | collective-permute-start | bytes 589832 | tf_op jit(solution)/shard_map/ppermute | solution.py:31
  9.0 0.7 copy-done.6
  9.7 4.8 %collective-permute-done.refs_4_ = bf16[264,384]{1,0:T(8,128)(2,1)S(1)} collective-permute-done((bf16[264,384]{1,0:T(8,128)(2,1)S(1)}, bf16[264,384]{1,0:T(8,128)(2,1)S(1)}, u32[]{:S(2)}, u32[]{:S(2)}) %collective-permute-start) | collective-permute-done | bytes 202784 | tf_op jit(solution)/shard_map/ppermute | solution.py:27
  14.5 0.1 shard_map.123
  14.6 1.8 %collective-permute-start.3 = (bf16[256,384]{1,0:T(8,128)(2,1)S(1)}, bf16[256,384]{1,0:T(8,128)(2,1)S(1)}, u32[]{:S(2)}, u32[]{:S(2)}) collective-permute-start(bf16[256,384]{1,0:T(8,128)(2,1)S(1)} %get-tuple-element.60.refs_2_), channel_id=1, source_target_pairs={{0,2},{1,3},{2,0},{3,1},{4,6},{5,7},{6,4},{7,5},{8,10},{9,11},{10,... | collective-permute-start | bytes 589832 | tf_op jit(solution)/shard_map/ppermute | solution.py:31
  16.4 2.2 %collective-permute-start.1 = (bf16[264,384]{1,0:T(8,128)(2,1)S(1)}, bf16[264,384]{1,0:T(8,128)(2,1)S(1)}, u32[]{:S(2)}, u32[]{:S(2)}) collective-permute-start(bf16[264,384]{1,0:T(8,128)(2,1)S(1)} %get-tuple-element.57), channel_id=1, source_target_pairs={{0,12},{4,16},{8,20},{12,24},{16,28},{1,13},{5,17},{9,21},{13,25},... | collective-permute-start | bytes 608264 | tf_op jit(solution)/shard_map/ppermute | solution.py:27
  18.7 2.0 %collective-permute-start.9 = (bf16[264,384]{1,0:T(8,128)(2,1)S(1)}, bf16[264,384]{1,0:T(8,128)(2,1)S(1)}, u32[]{:S(2)}, u32[]{:S(2)}) collective-permute-start(bf16[264,384]{1,0:T(8,128)(2,1)S(1)} %get-tuple-element.64), channel_id=1, source_target_pairs={{0,4},{4,0},{8,12},{12,8},{16,20},{20,16},{24,28},{28,24},{1,5},{5... | collective-permute-start | bytes 608264 | tf_op jit(solution)/shard_map/ppermute | solution.py:31
  20.7 0.5 collective-permute-start.2
  21.2 0.1 collective-permute-start.4
  21.3 0.7 collective-permute-done.1.refs_5_
  21.9 6.7 %collective-permute-start.8 = (bf16[264,384]{1,0:T(8,128)(2,1)S(1)}, bf16[264,384]{1,0:T(8,128)(2,1)S(1)}, u32[]{:S(2)}, u32[]{:S(2)}) collective-permute-start(bf16[264,384]{1,0:T(8,128)(2,1)S(1)} %get-tuple-element.62), channel_id=1, source_target_pairs={{0,16},{4,20},{8,24},{12,28},{1,17},{5,21},{9,25},{13,29},{2,18},{... | collective-permute-start | bytes 608264 | tf_op jit(solution)/shard_map/ppermute | solution.py:27
  28.7 9.5 %collective-permute-start.10 = (bf16[264,384]{1,0:T(8,128)(2,1)S(1)}, bf16[264,384]{1,0:T(8,128)(2,1)S(1)}, u32[]{:S(2)}, u32[]{:S(2)}) collective-permute-start(bf16[264,384]{1,0:T(8,128)(2,1)S(1)} %collective-permute-done.9), channel_id=1, source_target_pairs={{0,8},{4,4},{8,16},{12,12},{16,24},{20,20},{24,0},{28,28},{1,9},{5... | collective-permute-start | bytes 608264 | tf_op jit(solution)/shard_map/ppermute | solution.py:448
  38.2 0.2 shard_map.124
  38.4 0.6 collective-permute-start.12
  39.0 2.9 %shard_map.125 = (f32[1536,512]{1,0:T(8,128)S(1)}, f32[64,512]{1,0:T(8,128)S(1)}, bf16[64,256]{1,0:T(8,128)(2,1)S(1)}, bf16[256,256]{1,0:T(8,128)(2,1)S(1)}, bf1...) custom-call(f32[8,128]{1,0:T(8,128)S(1)} %get-tuple-element.58.refs_, ...), custom_call_target="tpu_custom_call" | custom-call | flops 1098907648 | tf_op jit(solution)/shard_map/pallas_call | solution.py:69
  41.9 0.2 shard_map.126
  42.1 1.6 %collective-permute-start.15 = (bf16[256,384]{1,0:T(8,128)(2,1)S(1)}, bf16[256,384]{1,0:T(8,128)(2,1)S(1)}, u32[]{:S(2)}, u32[]{:S(2)}) collective-permute-start(bf16[256,384]{1,0:T(8,128)(2,1)S(1)} %get-tuple-element.78.refs_2_), channel_id=1, source_target_pairs={{0,2},{1,3},{2,0},{3,1},{4,6},{5,7},{6,4},{7,5},{8,10},{9,11},{10,... | collective-permute-start | bytes 589832 | tf_op jit(solution)/shard_map/ppermute | solution.py:31
  43.7 0.3 shard_map.127
  44.0 0.6 collective-permute-start.18
  44.6 0.7 collective-permute-done.12.refs_4_
  45.3 0.5 collective-permute-start.14
  45.8 4.2 %collective-permute-done.15.refs_4_ = bf16[256,384]{1,0:T(8,128)(2,1)S(1)} collective-permute-done((bf16[256,384]{1,0:T(8,128)(2,1)S(1)}, bf16[256,384]{1,0:T(8,128)(2,1)S(1)}, u32[]{:S(2)}, u32[]{:S(2)}) %collective-permute-start.15) | collective-permute-done | bytes 196640 | tf_op jit(solution)/shard_map/ppermute | solution.py:31
  50.0 0.5 collective-permute-start.17
  50.5 2.5 %collective-permute-done.18.refs_4_ = bf16[256,384]{1,0:T(8,128)(2,1)S(1)} collective-permute-done((bf16[256,384]{1,0:T(8,128)(2,1)S(1)}, bf16[256,384]{1,0:T(8,128)(2,1)S(1)}, u32[]{:S(2)}, u32[]{:S(2)}) %collective-permute-start.18) | collective-permute-done | bytes 196640 | tf_op jit(solution)/shard_map/ppermute | solution.py:31
  53.0 2.5 %shard_map.128 = (f32[1536,512]{1,0:T(8,128)S(1)}, f32[64,512]{1,0:T(8,128)S(1)}, bf16[64,256]{1,0:T(8,128)(2,1)S(1)}, f32[8,128]{1,0:T(8,128)S(1)}) custom-call(f32[8,128]{1,0:T(8,128)S(1)} %get-tuple-element.65.refs_0_, f32[8,128]{1,0:T(8,128)S(1)} %get-tuple-element.66.refs_1_.refs_2_, ...), custom_call_target="tpu_custom_call", output_to_operand_aliasing={{0}: (8, {}), {1}: (9, {})} | custom-call | flops 1098907648 | tf_op jit(solution)/shard_map/pallas_call | solution.py:69
  55.5 2.5 %shard_map.129 = (f32[1536,512]{1,0:T(8,128)S(1)}, f32[64,512]{1,0:T(8,128)S(1)}, bf16[64,256]{1,0:T(8,128)(2,1)S(1)}, f32[8,128]{1,0:T(8,128)S(1)}) custom-call(f32[8,128]{1,0:T(8,128)S(1)} %get-tuple-element.76.refs_0_, f32[8,128]{1,0:T(8,128)S(1)} %get-tuple-element.77.refs_1_.refs_3_, ...), custom_call_target="tpu_custom_call", output_to_operand_aliasing={{0}: (8, {}), {1}: (9, {})} | custom-call | flops 1098907648 | tf_op jit(solution)/shard_map/pallas_call | solution.py:69
  58.0 3.5 %shard_map.130 = (bf16[768,256]{1,0:T(8,128)(2,1)S(1)}, bf16[768,256]{1,0:T(8,128)(2,1)S(1)}, bf16[768,256]{1,0:T(8,128)(2,1)S(1)}, bf16[768,256]{1,0:T(8,128)(2...) custom-call(f32[8,128]{1,0:T(8,128)S(1)} %get-tuple-element.81.refs_0_, ...), custom_call_target="tpu_custom_call" | custom-call | flops 1098907648 | tf_op jit(solution)/shard_map/pallas_call | solution.py:69
  61.5 0.4 collective-permute-start.25
  61.9 1.4 %shard_map.131 = (bf16[4,256,384]{2,1,0:T(8,128)(2,1)S(1)}, f32[4,64,384]{2,1,0:T(8,128)S(1)}, f32[8,128]{1,0:T(8,128)}) custom-call(f32[8,128]{1,0:T(8,128)S(1)} %get-tuple-element.86.refs_0_, f32[8,128]{1,0:T(8,128)S(1)} %get-tuple-element.59.refs_1_, f32[8,128]{1,0:T(8,128)S(1)} %get-tuple-element.66.refs_1_.refs_2_, ...), custom_call_target="tpu_custom_call" | custom-call | flops 201326592 | tf_op jit(solution)/shard_map/pallas_call | solution.py:69
  63.3 0.5 collective-permute-start.20
  63.8 9.3 %collective-permute-done.25 = bf16[768,256]{1,0:T(8,128)(2,1)S(1)} collective-permute-done((bf16[768,256]{1,0:T(8,128)(2,1)S(1)}, bf16[768,256]{1,0:T(8,128)(2,1)S(1)}, u32[]{:S(2)}, u32[]{:S(2)}) %collective-permute-start.25) | collective-permute-done | bytes 393248 | tf_op jit(solution)/shard_map/ppermute | solution.py:31
  73.1 0.1 add_convert_fusion
  73.3 0.8 collective-permute-start.26
  74.1 0.1 add_convert_fusion.1
  74.2 1.8 %collective-permute-start.23 = (bf16[2,1,192,256]{3,2,1,0:T(8,128)(2,1)S(1)}, bf16[2,1,192,256]{3,2,1,0:T(8,128)(2,1)S(1)}, u32[]{:S(2)}, u32[]{:S(2)}) collective-permute-start(bf16[2,1,192,256]{3,2,1,0:T(8,128)(2,1)S(1)} %constant_dynamic-slice_fusion.1), channel_id=1, source_target_pairs={{0,8},{4,12},{8,0},{12,4},{16,24},{20,28},{24,16},{28,20},{1,9},{5... | collective-permute-start | bytes 589832 | tf_op jit(solution)/shard_map/ppermute | solution.py:31
  76.0 0.1 add_convert_fusion.2
  76.2 0.6 collective-permute-start.21
  76.7 8.0 %collective-permute-done.26 = bf16[1,2,192,256]{3,2,1,0:T(8,128)(2,1)S(1)} collective-permute-done((bf16[1,2,192,256]{3,2,1,0:T(8,128)(2,1)S(1)}, bf16[1,2,192,256]{3,2,1,0:T(8,128)(2,1)S(1)}, u32[]{:S(2)}, u32[]{:S(2)}) %collective-permute-start.26) | collective-permute-done | bytes 196640 | tf_op jit(solution)/shard_map/ppermute | solution.py:31
  84.8 0.1 collective-permute-start.27
  85.0 0.3 collective-permute-start.24
  85.4 0.7 add_convert_fusion.5
  86.2 6.1 %collective-permute-done.24 = bf16[1,192,256]{2,1,0:T(8,128)(2,1)S(1)} collective-permute-done((bf16[1,192,256]{2,1,0:T(8,128)(2,1)S(1)}, bf16[1,192,256]{2,1,0:T(8,128)(2,1)S(1)}, u32[]{:S(2)}, u32[]{:S(2)}) %collective-permute-start.24) | collective-permute-done | bytes 98336 | tf_op jit(solution)/shard_map/ppermute | solution.py:31
  92.2 0.7 fusion.1
  92.9 0.7 fusion
  (52 shorter events, 0.5 us)
Async XLA Ops:
  0.6 38.3 %copy-start.4 = (bf16[4,64,384]{2,1,0:T(8,128)(2,1)S(1)}, bf16[4,64,384]{2,1,0:T(8,128)(2,1)}, u32[]{:S(2)}) copy-start(bf16[4,64,384]{2,1,0:T(8,128)(2,1)} %param.19) | copy-start | bytes 589828
  0.6 38.3 %copy-start.3 = (bf16[64,1536]{1,0:T(8,128)(2,1)S(1)}, bf16[64,1536]{1,0:T(8,128)(2,1)}, u32[]{:S(2)}) copy-start(bf16[64,1536]{1,0:T(8,128)(2,1)} %refs_9_.3) | copy-start | bytes 589828
  0.7 38.3 %copy-start.5 = (bf16[64,256]{1,0:T(8,128)(2,1)S(1)}, bf16[64,256]{1,0:T(8,128)(2,1)}, u32[]{:S(2)}) copy-start(bf16[64,256]{1,0:T(8,128)(2,1)} %refs_9_.2) | copy-start | bytes 98308
  0.7 38.3 %copy-start = (bf16[1536,256]{1,0:T(8,128)(2,1)S(1)}, bf16[1536,256]{1,0:T(8,128)(2,1)}, u32[]{:S(2)}) copy-start(bf16[1536,256]{1,0:T(8,128)(2,1)} %refs_6_.7) | copy-start | bytes 2359300
  0.7 38.3 %copy-start.1 = (bf16[1536,256]{1,0:T(8,128)(2,1)S(1)}, bf16[1536,256]{1,0:T(8,128)(2,1)}, u32[]{:S(2)}) copy-start(bf16[1536,256]{1,0:T(8,128)(2,1)} %refs_7_.7) | copy-start | bytes 2359300
  0.7 0.8 copy-start.7
  1.5 0.7 copy-start.8
  2.1 36.9 %copy-start.2 = (bf16[256,1536]{1,0:T(8,128)(2,1)S(1)}, bf16[256,1536]{1,0:T(8,128)(2,1)}, u32[]{:S(2)}) copy-start(bf16[256,1536]{1,0:T(8,128)(2,1)} %refs_10_.3) | copy-start | bytes 2359300
  4.6 9.9 %collective-permute-start = (bf16[264,384]{1,0:T(8,128)(2,1)S(1)}, bf16[264,384]{1,0:T(8,128)(2,1)S(1)}, u32[]{:S(2)}, u32[]{:S(2)}) collective-permute-start(bf16[264,384]{1,0:T(8,128)(2,1)S(1)} %get-tuple-element.55), channel_id=1, source_target_pairs={{0,8},{4,12},{8,16},{12,20},{16,24},{20,28},{24,0},{28,4},{1,9},{5... | collective-permute-start | bytes 608264 | tf_op jit(solution)/shard_map/ppermute | solution.py:27
  7.5 13.2 %collective-permute-start.6 = (bf16[256,384]{1,0:T(8,128)(2,1)}, bf16[256,384]{1,0:T(8,128)(2,1)S(1)}, u32[]{:S(2)}, u32[]{:S(2)}) collective-permute-start(bf16[256,384]{1,0:T(8,128)(2,1)} %bitcast.21), channel_id=1, source_target_pairs={{0,2},{1,3},{2,0},{3,1},{4,6},{5,7},{6,4},{7,5},{8,10},{9,11},{10,... | collective-permute-start | bytes 589832 | tf_op jit(solution)/shard_map/ppermute | solution.py:31
  9.0 11.7 %collective-permute-start.5 = (bf16[256,384]{1,0:T(8,128)(2,1)}, bf16[256,384]{1,0:T(8,128)(2,1)S(1)}, u32[]{:S(2)}, u32[]{:S(2)}) collective-permute-start(bf16[256,384]{1,0:T(8,128)(2,1)} %bitcast.22), channel_id=1, source_target_pairs={{0,1},{1,0},{2,3},{3,2},{4,5},{5,4},{6,7},{7,6},{8,9},{9,8},{10,11... | collective-permute-start | bytes 589832 | tf_op jit(solution)/shard_map/ppermute | solution.py:31
  9.0 0.7 copy-start.6
  14.6 6.5 %collective-permute-start.3 = (bf16[256,384]{1,0:T(8,128)(2,1)S(1)}, bf16[256,384]{1,0:T(8,128)(2,1)S(1)}, u32[]{:S(2)}, u32[]{:S(2)}) collective-permute-start(bf16[256,384]{1,0:T(8,128)(2,1)S(1)} %get-tuple-element.60.refs_2_), channel_id=1, source_target_pairs={{0,2},{1,3},{2,0},{3,1},{4,6},{5,7},{6,4},{7,5},{8,10},{9,11},{10,... | collective-permute-start | bytes 589832 | tf_op jit(solution)/shard_map/ppermute | solution.py:31
  16.4 5.5 %collective-permute-start.1 = (bf16[264,384]{1,0:T(8,128)(2,1)S(1)}, bf16[264,384]{1,0:T(8,128)(2,1)S(1)}, u32[]{:S(2)}, u32[]{:S(2)}) collective-permute-start(bf16[264,384]{1,0:T(8,128)(2,1)S(1)} %get-tuple-element.57), channel_id=1, source_target_pairs={{0,12},{4,16},{8,20},{12,24},{16,28},{1,13},{5,17},{9,21},{13,25},... | collective-permute-start | bytes 608264 | tf_op jit(solution)/shard_map/ppermute | solution.py:27
  18.7 10.0 %collective-permute-start.9 = (bf16[264,384]{1,0:T(8,128)(2,1)S(1)}, bf16[264,384]{1,0:T(8,128)(2,1)S(1)}, u32[]{:S(2)}, u32[]{:S(2)}) collective-permute-start(bf16[264,384]{1,0:T(8,128)(2,1)S(1)} %get-tuple-element.64), channel_id=1, source_target_pairs={{0,4},{4,0},{8,12},{12,8},{16,20},{20,16},{24,28},{28,24},{1,5},{5... | collective-permute-start | bytes 608264 | tf_op jit(solution)/shard_map/ppermute | solution.py:31
  20.7 17.7 %collective-permute-start.7 = (bf16[256,384]{1,0:T(8,128)(2,1)S(1)}, bf16[256,384]{1,0:T(8,128)(2,1)S(1)}, u32[]{:S(2)}, u32[]{:S(2)}) collective-permute-start(bf16[256,384]{1,0:T(8,128)(2,1)S(1)} %collective-permute-done.6.refs_13_), channel_id=1, source_target_pairs={{0,1},{1,0},{2,3},{3,2},{4,5},{5,4},{6,7},{7,6},{8,9},{9,8},{10,11... | collective-permute-start | bytes 589832 | tf_op jit(solution)/shard_map/ppermute | solution.py:31
  20.7 18.3 %collective-permute-start.2 = (bf16[256,384]{1,0:T(8,128)(2,1)S(1)}, bf16[256,384]{1,0:T(8,128)(2,1)S(1)}, u32[]{:S(2)}, u32[]{:S(2)}) collective-permute-start(bf16[256,384]{1,0:T(8,128)(2,1)S(1)} %get-tuple-element.60.refs_2_), channel_id=1, source_target_pairs={{0,1},{1,0},{2,3},{3,2},{4,5},{5,4},{6,7},{7,6},{8,9},{9,8},{10,11... | collective-permute-start | bytes 589832 | tf_op jit(solution)/shard_map/ppermute | solution.py:31
  21.2 17.8 %collective-permute-start.4 = (bf16[256,384]{1,0:T(8,128)(2,1)S(1)}, bf16[256,384]{1,0:T(8,128)(2,1)S(1)}, u32[]{:S(2)}, u32[]{:S(2)}) collective-permute-start(bf16[256,384]{1,0:T(8,128)(2,1)S(1)} %collective-permute-done.3.refs_4_), channel_id=1, source_target_pairs={{0,1},{1,0},{2,3},{3,2},{4,5},{5,4},{6,7},{7,6},{8,9},{9,8},{10,11... | collective-permute-start | bytes 589832 | tf_op jit(solution)/shard_map/ppermute | solution.py:31
  21.9 20.0 %collective-permute-start.8 = (bf16[264,384]{1,0:T(8,128)(2,1)S(1)}, bf16[264,384]{1,0:T(8,128)(2,1)S(1)}, u32[]{:S(2)}, u32[]{:S(2)}) collective-permute-start(bf16[264,384]{1,0:T(8,128)(2,1)S(1)} %get-tuple-element.62), channel_id=1, source_target_pairs={{0,16},{4,20},{8,24},{12,28},{1,17},{5,21},{9,25},{13,29},{2,18},{... | collective-permute-start | bytes 608264 | tf_op jit(solution)/shard_map/ppermute | solution.py:27
  28.7 15.1 %collective-permute-start.10 = (bf16[264,384]{1,0:T(8,128)(2,1)S(1)}, bf16[264,384]{1,0:T(8,128)(2,1)S(1)}, u32[]{:S(2)}, u32[]{:S(2)}) collective-permute-start(bf16[264,384]{1,0:T(8,128)(2,1)S(1)} %collective-permute-done.9), channel_id=1, source_target_pairs={{0,8},{4,4},{8,16},{12,12},{16,24},{20,20},{24,0},{28,28},{1,9},{5... | collective-permute-start | bytes 608264 | tf_op jit(solution)/shard_map/ppermute | solution.py:448
  38.4 6.9 %collective-permute-start.12 = (bf16[256,384]{1,0:T(8,128)(2,1)S(1)}, bf16[256,384]{1,0:T(8,128)(2,1)S(1)}, u32[]{:S(2)}, u32[]{:S(2)}) collective-permute-start(bf16[256,384]{1,0:T(8,128)(2,1)S(1)} %get-tuple-element.67.refs_2_), channel_id=1, source_target_pairs={{0,2},{1,3},{2,0},{3,1},{4,6},{5,7},{6,4},{7,5},{8,10},{9,11},{10,... | collective-permute-start | bytes 589832 | tf_op jit(solution)/shard_map/ppermute | solution.py:31
  42.1 7.8 %collective-permute-start.15 = (bf16[256,384]{1,0:T(8,128)(2,1)S(1)}, bf16[256,384]{1,0:T(8,128)(2,1)S(1)}, u32[]{:S(2)}, u32[]{:S(2)}) collective-permute-start(bf16[256,384]{1,0:T(8,128)(2,1)S(1)} %get-tuple-element.78.refs_2_), channel_id=1, source_target_pairs={{0,2},{1,3},{2,0},{3,1},{4,6},{5,7},{6,4},{7,5},{8,10},{9,11},{10,... | collective-permute-start | bytes 589832 | tf_op jit(solution)/shard_map/ppermute | solution.py:31
  43.7 6.3 %collective-permute-start.11 = (bf16[256,384]{1,0:T(8,128)(2,1)S(1)}, bf16[256,384]{1,0:T(8,128)(2,1)S(1)}, u32[]{:S(2)}, u32[]{:S(2)}) collective-permute-start(bf16[256,384]{1,0:T(8,128)(2,1)S(1)} %get-tuple-element.67.refs_2_), channel_id=1, source_target_pairs={{0,1},{1,0},{2,3},{3,2},{4,5},{5,4},{6,7},{7,6},{8,9},{9,8},{10,11... | collective-permute-start | bytes 589832 | tf_op jit(solution)/shard_map/ppermute | solution.py:31
  44.0 8.9 %collective-permute-start.18 = (bf16[256,384]{1,0:T(8,128)(2,1)S(1)}, bf16[256,384]{1,0:T(8,128)(2,1)S(1)}, u32[]{:S(2)}, u32[]{:S(2)}) collective-permute-start(bf16[256,384]{1,0:T(8,128)(2,1)S(1)} %get-tuple-element.83.refs_2_), channel_id=1, source_target_pairs={{0,2},{1,3},{2,0},{3,1},{4,6},{5,7},{6,4},{7,5},{8,10},{9,11},{10,... | collective-permute-start | bytes 589832 | tf_op jit(solution)/shard_map/ppermute | solution.py:31
  45.3 7.7 %collective-permute-start.13 = (bf16[256,384]{1,0:T(8,128)(2,1)S(1)}, bf16[256,384]{1,0:T(8,128)(2,1)S(1)}, u32[]{:S(2)}, u32[]{:S(2)}) collective-permute-start(bf16[256,384]{1,0:T(8,128)(2,1)S(1)} %collective-permute-done.12.refs_4_), channel_id=1, source_target_pairs={{0,1},{1,0},{2,3},{3,2},{4,5},{5,4},{6,7},{7,6},{8,9},{9,8},{10,11... | collective-permute-start | bytes 589832 | tf_op jit(solution)/shard_map/ppermute | solution.py:31
  45.3 10.2 %collective-permute-start.14 = (bf16[256,384]{1,0:T(8,128)(2,1)S(1)}, bf16[256,384]{1,0:T(8,128)(2,1)S(1)}, u32[]{:S(2)}, u32[]{:S(2)}) collective-permute-start(bf16[256,384]{1,0:T(8,128)(2,1)S(1)} %get-tuple-element.78.refs_2_), channel_id=1, source_target_pairs={{0,1},{1,0},{2,3},{3,2},{4,5},{5,4},{6,7},{7,6},{8,9},{9,8},{10,11... | collective-permute-start | bytes 589832 | tf_op jit(solution)/shard_map/ppermute | solution.py:31
  50.0 5.5 %collective-permute-start.16 = (bf16[256,384]{1,0:T(8,128)(2,1)S(1)}, bf16[256,384]{1,0:T(8,128)(2,1)S(1)}, u32[]{:S(2)}, u32[]{:S(2)}) collective-permute-start(bf16[256,384]{1,0:T(8,128)(2,1)S(1)} %collective-permute-done.15.refs_4_), channel_id=1, source_target_pairs={{0,1},{1,0},{2,3},{3,2},{4,5},{5,4},{6,7},{7,6},{8,9},{9,8},{10,11... | collective-permute-start | bytes 589832 | tf_op jit(solution)/shard_map/ppermute | solution.py:31
  50.0 8.0 %collective-permute-start.17 = (bf16[256,384]{1,0:T(8,128)(2,1)S(1)}, bf16[256,384]{1,0:T(8,128)(2,1)S(1)}, u32[]{:S(2)}, u32[]{:S(2)}) collective-permute-start(bf16[256,384]{1,0:T(8,128)(2,1)S(1)} %get-tuple-element.83.refs_2_), channel_id=1, source_target_pairs={{0,1},{1,0},{2,3},{3,2},{4,5},{5,4},{6,7},{7,6},{8,9},{9,8},{10,11... | collective-permute-start | bytes 589832 | tf_op jit(solution)/shard_map/ppermute | solution.py:31
  53.0 5.1 %collective-permute-start.19 = (bf16[256,384]{1,0:T(8,128)(2,1)S(1)}, bf16[256,384]{1,0:T(8,128)(2,1)S(1)}, u32[]{:S(2)}, u32[]{:S(2)}) collective-permute-start(bf16[256,384]{1,0:T(8,128)(2,1)S(1)} %collective-permute-done.18.refs_4_), channel_id=1, source_target_pairs={{0,1},{1,0},{2,3},{3,2},{4,5},{5,4},{6,7},{7,6},{8,9},{9,8},{10,11... | collective-permute-start | bytes 589832 | tf_op jit(solution)/shard_map/ppermute | solution.py:31
  61.5 11.6 %collective-permute-start.25 = (bf16[768,256]{1,0:T(8,128)(2,1)S(1)}, bf16[768,256]{1,0:T(8,128)(2,1)S(1)}, u32[]{:S(2)}, u32[]{:S(2)}) collective-permute-start(bf16[768,256]{1,0:T(8,128)(2,1)S(1)} %get-tuple-element.96), channel_id=1, source_target_pairs={{0,8},{4,12},{8,0},{12,4},{16,24},{20,28},{24,16},{28,20},{1,9},{5... | collective-permute-start | bytes 1179656 | tf_op jit(solution)/shard_map/ppermute | solution.py:31
  61.9 12.2 %collective-permute-start.22 = (bf16[768,256]{1,0:T(8,128)(2,1)S(1)}, bf16[768,256]{1,0:T(8,128)(2,1)S(1)}, u32[]{:S(2)}, u32[]{:S(2)}) collective-permute-start(bf16[768,256]{1,0:T(8,128)(2,1)S(1)} %get-tuple-element.94), channel_id=1, source_target_pairs={{0,4},{4,0},{8,12},{12,8},{16,20},{20,16},{24,28},{28,24},{1,5},{5... | collective-permute-start | bytes 1179656 | tf_op jit(solution)/shard_map/ppermute | solution.py:31
  63.3 12.7 %collective-permute-start.20 = (bf16[2,1,256,384]{3,2,1,0:T(8,128)(2,1)S(1)}, bf16[2,1,256,384]{3,2,1,0:T(8,128)(2,1)S(1)}, u32[]{:S(2)}, u32[]{:S(2)}) collective-permute-start(bf16[2,1,256,384]{3,2,1,0:T(8,128)(2,1)S(1)} %constant_dynamic-slice_fusion.3), channel_id=1, source_target_pairs={{0,1},{1,0},{2,3},{3,2},{4,5},{5,4},{6,7},{7,6},{8,9},{9,8},{10,11... | collective-permute-start | bytes 1179656 | tf_op jit(solution)/shard_map/ppermute | solution.py:31
  73.3 11.5 %collective-permute-start.26 = (bf16[1,2,192,256]{3,2,1,0:T(8,128)(2,1)S(1)}, bf16[1,2,192,256]{3,2,1,0:T(8,128)(2,1)S(1)}, u32[]{:S(2)}, u32[]{:S(2)}) collective-permute-start(bf16[1,2,192,256]{3,2,1,0:T(8,128)(2,1)S(1)} %constant_dynamic-slice_fusion), channel_id=1, source_target_pairs={{0,16},{4,20},{8,24},{12,28},{16,0},{20,4},{24,8},{28,12},{1,17},{... | collective-permute-start | bytes 589832 | tf_op jit(solution)/shard_map/ppermute | solution.py:31
  74.2 10.7 %collective-permute-start.23 = (bf16[2,1,192,256]{3,2,1,0:T(8,128)(2,1)S(1)}, bf16[2,1,192,256]{3,2,1,0:T(8,128)(2,1)S(1)}, u32[]{:S(2)}, u32[]{:S(2)}) collective-permute-start(bf16[2,1,192,256]{3,2,1,0:T(8,128)(2,1)S(1)} %constant_dynamic-slice_fusion.1), channel_id=1, source_target_pairs={{0,8},{4,12},{8,0},{12,4},{16,24},{20,28},{24,16},{28,20},{1,9},{5... | collective-permute-start | bytes 589832 | tf_op jit(solution)/shard_map/ppermute | solution.py:31
  76.2 9.2 %collective-permute-start.21 = (bf16[1,1,256,384]{3,2,1,0:T(8,128)(2,1)S(1)}, bf16[1,1,256,384]{3,2,1,0:T(8,128)(2,1)S(1)}, u32[]{:S(2)}, u32[]{:S(2)}) collective-permute-start(bf16[1,1,256,384]{3,2,1,0:T(8,128)(2,1)S(1)} %constant_dynamic-slice_fusion.2), channel_id=1, source_target_pairs={{0,2},{1,3},{2,0},{3,1},{4,6},{5,7},{6,4},{7,5},{8,10},{9,11},{10,... | collective-permute-start | bytes 589832 | tf_op jit(solution)/shard_map/ppermute | solution.py:31
  84.8 8.1 %collective-permute-start.27 = (bf16[1,192,256]{2,1,0:T(8,128)(2,1)S(1)}, bf16[1,192,256]{2,1,0:T(8,128)(2,1)S(1)}, u32[]{:S(2)}, u32[]{:S(2)}) collective-permute-start(bf16[1,192,256]{2,1,0:T(8,128)(2,1)S(1)} %dynamic-slice_bitcast_fusion), channel_id=1, source_target_pairs={{0,4},{4,0},{8,12},{12,8},{16,20},{20,16},{24,28},{28,24},{1,5},{5... | collective-permute-start | bytes 294920 | tf_op jit(solution)/shard_map/ppermute | solution.py:31
  85.0 7.2 %collective-permute-start.24 = (bf16[1,192,256]{2,1,0:T(8,128)(2,1)S(1)}, bf16[1,192,256]{2,1,0:T(8,128)(2,1)S(1)}, u32[]{:S(2)}, u32[]{:S(2)}) collective-permute-start(bf16[1,192,256]{2,1,0:T(8,128)(2,1)S(1)} %dynamic-slice_bitcast_fusion.1), channel_id=1, source_target_pairs={{0,16},{4,20},{8,24},{12,28},{16,0},{20,4},{24,8},{28,12},{1,17},{... | collective-permute-start | bytes 294920 | tf_op jit(solution)/shard_map/ppermute | solution.py:31

commit v3 on v2

--- a/solution.py
+++ b/solution.py
@@ -385,6 +385,58 @@
     return total if last else total.astype(bf16)
 
 
+def fold_body(rows, bit, *refs):
+    send_ref, keep_ref = refs[4:]
+    mine = (lax.axis_index("dp") // bit) % 2
+    ours = pl.ds(pl.multiple_of(mine * rows, rows), rows)
+    theirs = pl.ds(pl.multiple_of((1 - mine) * rows, rows), rows)
+    for i in range(2):
+        held, got = refs[2 * i], refs[2 * i + 1]
+        out = pl.ds(i * rows, rows)
+        keep_ref[out, :] = held[ours, :].astype(f32) + got[ours, :].astype(f32)
+        total = held[theirs, :].astype(f32) + got[theirs, :].astype(f32)
+        send_ref[out, :] = total.astype(bf16)
+
+
+def finish_body(keep_ref, got_ref, key_ref, value_ref):
+    rows = key_ref.shape[0]
+    for i, out in enumerate((key_ref, value_ref)):
+        part = pl.ds(i * rows, rows)
+        out[...] = keep_ref[part, :] + got_ref[part, :].astype(f32)
+
+
+def merged_exchange(keeps, sends, rows, inner, bits):
+    low, middle, high = bits
+    shape = jax.ShapeDtypeStruct
+    sides = []
+    for keep, send, first, second in (
+        (keeps[0], sends[0], low, middle),
+        (keeps[1], sends[1], middle, low),
+    ):
+        part = exchange(keep, send, "dp", first, False).reshape(2, 2, rows, inner)
+        keep, send = pick_side(part, "dp", 1, second)
+        got = flip(send.reshape(2 * rows, inner), "dp", second)
+        sides += [keep.reshape(2 * rows, inner), got]
+    send, keep = Chain().call(
+        functools.partial(fold_body, rows, high),
+        [shape((2 * rows, inner), bf16), shape((2 * rows, inner), f32)],
+        [VMEM] * 4,
+        [VMEM] * 2,
+        sides,
+        moved=16 * rows * inner,
+        limit=4,
+    )
+    return Chain().call(
+        finish_body,
+        [shape((rows, inner), f32)] * 2,
+        [VMEM] * 2,
+        [VMEM] * 2,
+        (keep, flip(send, "dp", high)),
+        moved=16 * rows * inner,
+        limit=4,
+    )
+
+
 def powers(size):
     found = []
     while 2 ** len(found) < size:
@@ -415,7 +467,7 @@
     dp = lax.axis_size("dp")
     bits = powers(dp)
     depth = len(bits)
-    turned = bits[1:] + bits[:1]
+    turned = bits[1:2] + bits[:1] + bits[2:]
     rows = model_width // dp
     shape = jax.ShapeDtypeStruct
     chain = Chain()
@@ -541,27 +593,30 @@
         place(p)
     carried = sums
 
-    grads = []
-    for i, order in enumerate((bits, turned)):
-        left = list(reversed(bits))
-        if len(carried) == 4:
-            keep, send = carried[2 * i : 2 * i + 2]
-            left.remove(order[0])
-            dims = (2,) * len(left) + (rows, inner)
-            part = exchange(keep, send, "dp", order[0], depth == 1).reshape(dims)
-            order = order[1:]
-        else:
-            part = carried[i].reshape((2,) * depth + (rows, inner))
-        grads.append([part, left, order])
-    for step in range(max((len(g[2]) for g in grads), default=0)):
-        for g in grads:
-            part, left, order = g
-            bit = order[step]
-            keep, send = pick_side(part, "dp", left.index(bit), bit)
-            part = exchange(keep, send, "dp", bit, step == len(order) - 1)
-            left.remove(bit)
-            g[0] = part.reshape((2,) * len(left) + (rows, inner))
-    key_grad, value_grad = [g[0].astype(f32) for g in grads]
+    if depth == 3 and len(carried) == 4:
+        key_grad, value_grad = merged_exchange(carried[0::2], carried[1::2], rows, inner, bits)
+    else:
+        grads = []
+        for i, order in enumerate((bits, turned)):
+            left = list(reversed(bits))
+            if len(carried) == 4:
+                keep, send = carried[2 * i : 2 * i + 2]
+                left.remove(order[0])
+                dims = (2,) * len(left) + (rows, inner)
+                part = exchange(keep, send, "dp", order[0], depth == 1).reshape(dims)
+                order = order[1:]
+            else:
+                part = carried[i].reshape((2,) * depth + (rows, inner))
+            grads.append([part, left, order])
+        for step in range(max((len(g[2]) for g in grads), default=0)):
+            for g in grads:
+                part, left, order = g
+                bit = order[step]
+                keep, send = pick_side(part, "dp", left.index(bit), bit)
+                part = exchange(keep, send, "dp", bit, step == len(order) - 1)
+                left.remove(bit)
+                g[0] = part.reshape((2,) * len(left) + (rows, inner))
+        key_grad, value_grad = [g[0].astype(f32) for g in grads]
 
     partial_out, base = chain.call(
         functools.partial(out_body, work, parts),

time: 93.9 us -> 92.4 us (0.984)
  waiting for transfers between devices: 36.3 us -> 34.5 us
  other arithmetic: 2.61 us -> 1.09 us
  Pallas kernels: 16 us -> 17.4 us
    ppermute x24 -> x23, waiting for transfers between devices: 30.8 us -> 29 us  [flip(): lax.ppermute(block, axis, [(i, i ^ bit) for i in range(lax.axis_size(axis...]
    reshape x2 -> x0, other arithmetic: 1.4 us -> none  [layer(): g[0] = part.reshape((2,) * len(left) + (rows, inner))]
    pallas_call x11 -> x13, Pallas kernels: 16 us -> 17.4 us  [call(): pl.pallas_call(chained, out_shape=[*outs, jax.ShapeDtypeStruct((8, 128),...]
    ppermute x24 -> x23, starting transfers between devices: 14.1 us -> 14.5 us  [flip(): lax.ppermute(block, axis, [(i, i ^ bit) for i in range(lax.axis_size(axis...]
  transfers between devices with their start and end apart: 28 -> 27, of which waited for: 9 -> 9; matrix products, arithmetic and copies ran while one was open for 2% -> 1% of each run, Pallas kernels for 11% -> 12%
where the time goes in v3:
time: 92.4 us; the launch traced here: 92.1 us
  starting transfers between devices  35.9 us (39%)
  waiting for transfers between devices  34.5 us (37%)
  Pallas kernels  17.4 us (19%)
  local copies, waits for them, and re-layouts  2.3 us (2%)
  other arithmetic  1.09 us (1%)
  between operations  0.94 us (1%)
    ppermute x23, waiting for transfers between devices, flip(): lax.ppermute(block, axis, [(i, i ^ bit) for i in range(lax.axis_size(axis...  29 us
    pallas_call x13, Pallas kernels, call(): pl.pallas_call(chained, out_shape=[*outs, jax.ShapeDtypeStruct((8, 128),...  17.4 us
    ppermute x23, starting transfers between devices, flip(): lax.ppermute(block, axis, [(i, i ^ bit) for i in range(lax.axis_size(axis...  14.5 us
    ppermute x3, starting transfers between devices, from_behind(): return lax.ppermute(block, axis, route)  11.8 us
    ppermute x1, starting transfers between devices, layer(): arrivals.append(lax.ppermute(near, 'dp', route))  9.55 us
    ppermute x3, waiting for transfers between devices, from_behind(): return lax.ppermute(block, axis, route)  5.52 us
    unnamed x18, local copies, waits for them, and re-layouts  2.16 us
  transfers between devices with their start and end apart: 27, of which 9 were waited for; matrix products, arithmetic and copies ran while one was open for 1% of the time, Pallas kernels for 12%

profile of v3, /device:TPU:0, one launch (start us, length us, event | category | flops | bytes accessed | tf_op | source)
XLA Modules:
  0.0 92.1 jit_solution(4602431860312792570)
XLA Ops:
  0.7 0.8 copy-done.7
  1.5 0.7 copy-done.8
  2.1 2.5 %shard_map.121 = (bf16[264,384]{1,0:T(8,128)(2,1)S(1)}, bf16[264,384]{1,0:T(8,128)(2,1)S(1)}, bf16[264,384]{1,0:T(8,128)(2,1)S(1)}, bf16[264,384]{1,0:T(8,128)(2...) custom-call(s32[1,8]{1,0:T(1,128)S(1)} %copy-done.7, s32[2]{0:T(128)S(1)} %copy-done.8, ...), custom_call_target="tpu_custom_call" | custom-call | bytes 3145728 | tf_op jit(solution)/shard_map/pallas_call | solution.py:69
  4.6 2.9 %collective-permute-start = (bf16[264,384]{1,0:T(8,128)(2,1)S(1)}, bf16[264,384]{1,0:T(8,128)(2,1)S(1)}, u32[]{:S(2)}, u32[]{:S(2)}) collective-permute-start(bf16[264,384]{1,0:T(8,128)(2,1)S(1)} %get-tuple-element.59), channel_id=1, source_target_pairs={{0,8},{4,12},{8,16},{12,20},{16,24},{20,28},{24,0},{28,4},{1,9},{5... | collective-permute-start | bytes 608264 | tf_op jit(solution)/shard_map/ppermute | solution.py:27
  7.4 1.5 %collective-permute-start.6 = (bf16[256,384]{1,0:T(8,128)(2,1)}, bf16[256,384]{1,0:T(8,128)(2,1)S(1)}, u32[]{:S(2)}, u32[]{:S(2)}) collective-permute-start(bf16[256,384]{1,0:T(8,128)(2,1)} %bitcast.21), channel_id=1, source_target_pairs={{0,2},{1,3},{2,0},{3,1},{4,6},{5,7},{6,4},{7,5},{8,10},{9,11},{10,... | collective-permute-start | bytes 589832 | tf_op jit(solution)/shard_map/ppermute | solution.py:31
  9.0 0.7 copy-done.6
  9.7 4.8 %collective-permute-done.refs_4_ = bf16[264,384]{1,0:T(8,128)(2,1)S(1)} collective-permute-done((bf16[264,384]{1,0:T(8,128)(2,1)S(1)}, bf16[264,384]{1,0:T(8,128)(2,1)S(1)}, u32[]{:S(2)}, u32[]{:S(2)}) %collective-permute-start) | collective-permute-done | bytes 202784 | tf_op jit(solution)/shard_map/ppermute | solution.py:27
  14.5 0.1 shard_map.123
  14.6 1.8 %collective-permute-start.3 = (bf16[256,384]{1,0:T(8,128)(2,1)S(1)}, bf16[256,384]{1,0:T(8,128)(2,1)S(1)}, u32[]{:S(2)}, u32[]{:S(2)}) collective-permute-start(bf16[256,384]{1,0:T(8,128)(2,1)S(1)} %get-tuple-element.64.refs_2_), channel_id=1, source_target_pairs={{0,2},{1,3},{2,0},{3,1},{4,6},{5,7},{6,4},{7,5},{8,10},{9,11},{10,... | collective-permute-start | bytes 589832 | tf_op jit(solution)/shard_map/ppermute | solution.py:31
  16.4 2.3 %collective-permute-start.1 = (bf16[264,384]{1,0:T(8,128)(2,1)S(1)}, bf16[264,384]{1,0:T(8,128)(2,1)S(1)}, u32[]{:S(2)}, u32[]{:S(2)}) collective-permute-start(bf16[264,384]{1,0:T(8,128)(2,1)S(1)} %get-tuple-element.61), channel_id=1, source_target_pairs={{0,12},{4,16},{8,20},{12,24},{16,28},{1,13},{5,17},{9,21},{13,25},... | collective-permute-start | bytes 608264 | tf_op jit(solution)/shard_map/ppermute | solution.py:27
  18.7 1.9 %collective-permute-start.9 = (bf16[264,384]{1,0:T(8,128)(2,1)S(1)}, bf16[264,384]{1,0:T(8,128)(2,1)S(1)}, u32[]{:S(2)}, u32[]{:S(2)}) collective-permute-start(bf16[264,384]{1,0:T(8,128)(2,1)S(1)} %get-tuple-element.68), channel_id=1, source_target_pairs={{0,4},{4,0},{8,12},{12,8},{16,20},{20,16},{24,28},{28,24},{1,5},{5... | collective-permute-start | bytes 608264 | tf_op jit(solution)/shard_map/ppermute | solution.py:31
  20.6 0.5 collective-permute-start.2
  21.1 0.1 collective-permute-start.4
  21.2 0.7 collective-permute-done.1.refs_5_
  21.9 6.7 %collective-permute-start.8 = (bf16[264,384]{1,0:T(8,128)(2,1)S(1)}, bf16[264,384]{1,0:T(8,128)(2,1)S(1)}, u32[]{:S(2)}, u32[]{:S(2)}) collective-permute-start(bf16[264,384]{1,0:T(8,128)(2,1)S(1)} %get-tuple-element.66), channel_id=1, source_target_pairs={{0,16},{4,20},{8,24},{12,28},{1,17},{5,21},{9,25},{13,29},{2,18},{... | collective-permute-start | bytes 608264 | tf_op jit(solution)/shard_map/ppermute | solution.py:27
  28.6 9.5 %collective-permute-start.10 = (bf16[264,384]{1,0:T(8,128)(2,1)S(1)}, bf16[264,384]{1,0:T(8,128)(2,1)S(1)}, u32[]{:S(2)}, u32[]{:S(2)}) collective-permute-start(bf16[264,384]{1,0:T(8,128)(2,1)S(1)} %collective-permute-done.9), channel_id=1, source_target_pairs={{0,8},{4,4},{8,16},{12,12},{16,24},{20,20},{24,0},{28,28},{1,9},{5... | collective-permute-start | bytes 608264 | tf_op jit(solution)/shard_map/ppermute | solution.py:500
  38.2 0.2 shard_map.124
  38.3 0.6 collective-permute-start.12
  39.0 2.9 %shard_map.125 = (f32[1536,512]{1,0:T(8,128)S(1)}, f32[64,512]{1,0:T(8,128)S(1)}, bf16[64,256]{1,0:T(8,128)(2,1)S(1)}, bf16[256,256]{1,0:T(8,128)(2,1)S(1)}, bf1...) custom-call(f32[8,128]{1,0:T(8,128)S(1)} %get-tuple-element.62.refs_, ...), custom_call_target="tpu_custom_call" | custom-call | flops 1098907648 | tf_op jit(solution)/shard_map/pallas_call | solution.py:69
  41.9 0.2 shard_map.126
  42.1 1.6 %collective-permute-start.15 = (bf16[256,384]{1,0:T(8,128)(2,1)S(1)}, bf16[256,384]{1,0:T(8,128)(2,1)S(1)}, u32[]{:S(2)}, u32[]{:S(2)}) collective-permute-start(bf16[256,384]{1,0:T(8,128)(2,1)S(1)} %get-tuple-element.82.refs_2_), channel_id=1, source_target_pairs={{0,2},{1,3},{2,0},{3,1},{4,6},{5,7},{6,4},{7,5},{8,10},{9,11},{10,... | collective-permute-start | bytes 589832 | tf_op jit(solution)/shard_map/ppermute | solution.py:31
  43.7 0.3 shard_map.127
  44.0 0.6 collective-permute-start.18
  44.5 0.7 collective-permute-done.12.refs_4_
  45.3 0.5 collective-permute-start.14
  45.8 4.2 %collective-permute-done.15.refs_4_ = bf16[256,384]{1,0:T(8,128)(2,1)S(1)} collective-permute-done((bf16[256,384]{1,0:T(8,128)(2,1)S(1)}, bf16[256,384]{1,0:T(8,128)(2,1)S(1)}, u32[]{:S(2)}, u32[]{:S(2)}) %collective-permute-start.15) | collective-permute-done | bytes 196640 | tf_op jit(solution)/shard_map/ppermute | solution.py:31
  49.9 0.5 collective-permute-start.17
  50.5 2.5 %collective-permute-done.18.refs_4_ = bf16[256,384]{1,0:T(8,128)(2,1)S(1)} collective-permute-done((bf16[256,384]{1,0:T(8,128)(2,1)S(1)}, bf16[256,384]{1,0:T(8,128)(2,1)S(1)}, u32[]{:S(2)}, u32[]{:S(2)}) %collective-permute-start.18) | collective-permute-done | bytes 196640 | tf_op jit(solution)/shard_map/ppermute | solution.py:31
  53.0 2.5 %shard_map.128 = (f32[1536,512]{1,0:T(8,128)S(1)}, f32[64,512]{1,0:T(8,128)S(1)}, bf16[64,256]{1,0:T(8,128)(2,1)S(1)}, f32[8,128]{1,0:T(8,128)S(1)}) custom-call(f32[8,128]{1,0:T(8,128)S(1)} %get-tuple-element.69.refs_0_, f32[8,128]{1,0:T(8,128)S(1)} %get-tuple-element.70.refs_1_.refs_2_, ...), custom_call_target="tpu_custom_call", output_to_operand_aliasing={{0}: (8, {}), {1}: (9, {})} | custom-call | flops 1098907648 | tf_op jit(solution)/shard_map/pallas_call | solution.py:69
  55.5 2.5 %shard_map.129 = (f32[1536,512]{1,0:T(8,128)S(1)}, f32[64,512]{1,0:T(8,128)S(1)}, bf16[64,256]{1,0:T(8,128)(2,1)S(1)}, f32[8,128]{1,0:T(8,128)S(1)}) custom-call(f32[8,128]{1,0:T(8,128)S(1)} %get-tuple-element.80.refs_0_, f32[8,128]{1,0:T(8,128)S(1)} %get-tuple-element.81.refs_1_.refs_3_, ...), custom_call_target="tpu_custom_call", output_to_operand_aliasing={{0}: (8, {}), {1}: (9, {})} | custom-call | flops 1098907648 | tf_op jit(solution)/shard_map/pallas_call | solution.py:69
  58.0 3.5 %shard_map.130 = (bf16[768,256]{1,0:T(8,128)(2,1)S(1)}, bf16[768,256]{1,0:T(8,128)(2,1)S(1)}, bf16[768,256]{1,0:T(8,128)(2,1)S(1)}, bf16[768,256]{1,0:T(8,128)(2...) custom-call(f32[8,128]{1,0:T(8,128)S(1)} %get-tuple-element.85.refs_0_, ...), custom_call_target="tpu_custom_call" | custom-call | flops 1098907648 | tf_op jit(solution)/shard_map/pallas_call | solution.py:69
  61.5 0.4 collective-permute-start.24
  61.9 1.4 %shard_map.131 = (bf16[4,256,384]{2,1,0:T(8,128)(2,1)S(1)}, f32[4,64,384]{2,1,0:T(8,128)S(1)}, f32[8,128]{1,0:T(8,128)}) custom-call(f32[8,128]{1,0:T(8,128)S(1)} %get-tuple-element.90.refs_0_, f32[8,128]{1,0:T(8,128)S(1)} %get-tuple-element.63.refs_1_, f32[8,128]{1,0:T(8,128)S(1)} %get-tuple-element.70.refs_1_.refs_2_, ...), custom_call_target="tpu_custom_call" | custom-call | flops 201326592 | tf_op jit(solution)/shard_map/pallas_call | solution.py:69
  63.3 0.5 collective-permute-start.20
  63.8 9.4 %collective-permute-done.24 = bf16[768,256]{1,0:T(8,128)(2,1)S(1)} collective-permute-done((bf16[768,256]{1,0:T(8,128)(2,1)S(1)}, bf16[768,256]{1,0:T(8,128)(2,1)S(1)}, u32[]{:S(2)}, u32[]{:S(2)}) %collective-permute-start.24) | collective-permute-done | bytes 393248 | tf_op jit(solution)/shard_map/ppermute | solution.py:31
  73.1 0.1 add_convert_fusion
  73.3 0.1 collective-permute-start.25
  73.4 0.1 add_convert_fusion.1
  73.5 1.6 %collective-permute-start.23 = (bf16[384,256]{1,0:T(8,128)(2,1)S(1)}, bf16[384,256]{1,0:T(8,128)(2,1)S(1)}, u32[]{:S(2)}, u32[]{:S(2)}) collective-permute-start(bf16[384,256]{1,0:T(8,128)(2,1)S(1)} %bitcast.28), channel_id=1, source_target_pairs={{0,8},{4,12},{8,0},{12,4},{16,24},{20,28},{24,16},{28,20},{1,9},{5... | collective-permute-start | bytes 589832 | tf_op jit(solution)/shard_map/ppermute | solution.py:31
  75.1 0.1 add_convert_fusion.2
  75.2 0.8 collective-permute-start.21
  76.1 3.7 %collective-permute-done.25.refs_3_ = bf16[384,256]{1,0:T(8,128)(2,1)S(1)} collective-permute-done((bf16[384,256]{1,0:T(8,128)(2,1)S(1)}, bf16[384,256]{1,0:T(8,128)(2,1)S(1)}, u32[]{:S(2)}, u32[]{:S(2)}) %collective-permute-start.25) | collective-permute-done | bytes 196640 | tf_op jit(solution)/shard_map/ppermute | solution.py:31
  79.8 0.2 collective-permute-done.23.refs_1_
  80.0 0.6 shard_map.132
  80.6 1.7 %collective-permute-start.26 = (bf16[384,256]{1,0:T(8,128)(2,1)S(1)}, bf16[384,256]{1,0:T(8,128)(2,1)S(1)}, u32[]{:S(2)}, u32[]{:S(2)}) collective-permute-start(bf16[384,256]{1,0:T(8,128)(2,1)S(1)} %get-tuple-element.102), channel_id=1, source_target_pairs={{0,16},{4,20},{8,24},{12,28},{16,0},{20,4},{24,8},{28,12},{1,17},{... | collective-permute-start | bytes 589832 | tf_op jit(solution)/shard_map/ppermute | solution.py:31
  82.3 0.7 add_convert_fusion.3
  83.1 8.3 %collective-permute-done.26.refs_1_ = bf16[384,256]{1,0:T(8,128)(2,1)S(1)} collective-permute-done((bf16[384,256]{1,0:T(8,128)(2,1)S(1)}, bf16[384,256]{1,0:T(8,128)(2,1)S(1)}, u32[]{:S(2)}, u32[]{:S(2)}) %collective-permute-start.26) | collective-permute-done | bytes 196640 | tf_op jit(solution)/shard_map/ppermute | solution.py:31
  91.3 0.8 shard_map.133
  (46 shorter events, 0.3 us)
Async XLA Ops:
  0.6 38.3 %copy-start.4 = (bf16[4,64,384]{2,1,0:T(8,128)(2,1)S(1)}, bf16[4,64,384]{2,1,0:T(8,128)(2,1)}, u32[]{:S(2)}) copy-start(bf16[4,64,384]{2,1,0:T(8,128)(2,1)} %param.19) | copy-start | bytes 589828
  0.6 38.3 %copy-start.3 = (bf16[64,1536]{1,0:T(8,128)(2,1)S(1)}, bf16[64,1536]{1,0:T(8,128)(2,1)}, u32[]{:S(2)}) copy-start(bf16[64,1536]{1,0:T(8,128)(2,1)} %refs_9_.3) | copy-start | bytes 589828
  0.7 38.3 %copy-start.5 = (bf16[64,256]{1,0:T(8,128)(2,1)S(1)}, bf16[64,256]{1,0:T(8,128)(2,1)}, u32[]{:S(2)}) copy-start(bf16[64,256]{1,0:T(8,128)(2,1)} %refs_9_.2) | copy-start | bytes 98308
  0.7 38.3 %copy-start = (bf16[1536,256]{1,0:T(8,128)(2,1)S(1)}, bf16[1536,256]{1,0:T(8,128)(2,1)}, u32[]{:S(2)}) copy-start(bf16[1536,256]{1,0:T(8,128)(2,1)} %refs_6_.7) | copy-start | bytes 2359300
  0.7 38.3 %copy-start.1 = (bf16[1536,256]{1,0:T(8,128)(2,1)S(1)}, bf16[1536,256]{1,0:T(8,128)(2,1)}, u32[]{:S(2)}) copy-start(bf16[1536,256]{1,0:T(8,128)(2,1)} %refs_7_.7) | copy-start | bytes 2359300
  0.7 0.8 copy-start.7
  1.5 0.7 copy-start.8
  2.1 36.8 %copy-start.2 = (bf16[256,1536]{1,0:T(8,128)(2,1)S(1)}, bf16[256,1536]{1,0:T(8,128)(2,1)}, u32[]{:S(2)}) copy-start(bf16[256,1536]{1,0:T(8,128)(2,1)} %refs_10_.3) | copy-start | bytes 2359300
  4.6 9.9 %collective-permute-start = (bf16[264,384]{1,0:T(8,128)(2,1)S(1)}, bf16[264,384]{1,0:T(8,128)(2,1)S(1)}, u32[]{:S(2)}, u32[]{:S(2)}) collective-permute-start(bf16[264,384]{1,0:T(8,128)(2,1)S(1)} %get-tuple-element.59), channel_id=1, source_target_pairs={{0,8},{4,12},{8,16},{12,20},{16,24},{20,28},{24,0},{28,4},{1,9},{5... | collective-permute-start | bytes 608264 | tf_op jit(solution)/shard_map/ppermute | solution.py:27
  7.4 13.2 %collective-permute-start.6 = (bf16[256,384]{1,0:T(8,128)(2,1)}, bf16[256,384]{1,0:T(8,128)(2,1)S(1)}, u32[]{:S(2)}, u32[]{:S(2)}) collective-permute-start(bf16[256,384]{1,0:T(8,128)(2,1)} %bitcast.21), channel_id=1, source_target_pairs={{0,2},{1,3},{2,0},{3,1},{4,6},{5,7},{6,4},{7,5},{8,10},{9,11},{10,... | collective-permute-start | bytes 589832 | tf_op jit(solution)/shard_map/ppermute | solution.py:31
  9.0 11.7 %collective-permute-start.5 = (bf16[256,384]{1,0:T(8,128)(2,1)}, bf16[256,384]{1,0:T(8,128)(2,1)S(1)}, u32[]{:S(2)}, u32[]{:S(2)}) collective-permute-start(bf16[256,384]{1,0:T(8,128)(2,1)} %bitcast.22), channel_id=1, source_target_pairs={{0,1},{1,0},{2,3},{3,2},{4,5},{5,4},{6,7},{7,6},{8,9},{9,8},{10,11... | collective-permute-start | bytes 589832 | tf_op jit(solution)/shard_map/ppermute | solution.py:31
  9.0 0.7 copy-start.6
  14.6 6.5 %collective-permute-start.3 = (bf16[256,384]{1,0:T(8,128)(2,1)S(1)}, bf16[256,384]{1,0:T(8,128)(2,1)S(1)}, u32[]{:S(2)}, u32[]{:S(2)}) collective-permute-start(bf16[256,384]{1,0:T(8,128)(2,1)S(1)} %get-tuple-element.64.refs_2_), channel_id=1, source_target_pairs={{0,2},{1,3},{2,0},{3,1},{4,6},{5,7},{6,4},{7,5},{8,10},{9,11},{10,... | collective-permute-start | bytes 589832 | tf_op jit(solution)/shard_map/ppermute | solution.py:31
  16.4 5.5 %collective-permute-start.1 = (bf16[264,384]{1,0:T(8,128)(2,1)S(1)}, bf16[264,384]{1,0:T(8,128)(2,1)S(1)}, u32[]{:S(2)}, u32[]{:S(2)}) collective-permute-start(bf16[264,384]{1,0:T(8,128)(2,1)S(1)} %get-tuple-element.61), channel_id=1, source_target_pairs={{0,12},{4,16},{8,20},{12,24},{16,28},{1,13},{5,17},{9,21},{13,25},... | collective-permute-start | bytes 608264 | tf_op jit(solution)/shard_map/ppermute | solution.py:27
  18.7 9.9 %collective-permute-start.9 = (bf16[264,384]{1,0:T(8,128)(2,1)S(1)}, bf16[264,384]{1,0:T(8,128)(2,1)S(1)}, u32[]{:S(2)}, u32[]{:S(2)}) collective-permute-start(bf16[264,384]{1,0:T(8,128)(2,1)S(1)} %get-tuple-element.68), channel_id=1, source_target_pairs={{0,4},{4,0},{8,12},{12,8},{16,20},{20,16},{24,28},{28,24},{1,5},{5... | collective-permute-start | bytes 608264 | tf_op jit(solution)/shard_map/ppermute | solution.py:31
  20.6 17.7 %collective-permute-start.7 = (bf16[256,384]{1,0:T(8,128)(2,1)S(1)}, bf16[256,384]{1,0:T(8,128)(2,1)S(1)}, u32[]{:S(2)}, u32[]{:S(2)}) collective-permute-start(bf16[256,384]{1,0:T(8,128)(2,1)S(1)} %collective-permute-done.6.refs_13_), channel_id=1, source_target_pairs={{0,1},{1,0},{2,3},{3,2},{4,5},{5,4},{6,7},{7,6},{8,9},{9,8},{10,11... | collective-permute-start | bytes 589832 | tf_op jit(solution)/shard_map/ppermute | solution.py:31
  20.6 18.3 %collective-permute-start.2 = (bf16[256,384]{1,0:T(8,128)(2,1)S(1)}, bf16[256,384]{1,0:T(8,128)(2,1)S(1)}, u32[]{:S(2)}, u32[]{:S(2)}) collective-permute-start(bf16[256,384]{1,0:T(8,128)(2,1)S(1)} %get-tuple-element.64.refs_2_), channel_id=1, source_target_pairs={{0,1},{1,0},{2,3},{3,2},{4,5},{5,4},{6,7},{7,6},{8,9},{9,8},{10,11... | collective-permute-start | bytes 589832 | tf_op jit(solution)/shard_map/ppermute | solution.py:31
  21.1 17.8 %collective-permute-start.4 = (bf16[256,384]{1,0:T(8,128)(2,1)S(1)}, bf16[256,384]{1,0:T(8,128)(2,1)S(1)}, u32[]{:S(2)}, u32[]{:S(2)}) collective-permute-start(bf16[256,384]{1,0:T(8,128)(2,1)S(1)} %collective-permute-done.3.refs_4_), channel_id=1, source_target_pairs={{0,1},{1,0},{2,3},{3,2},{4,5},{5,4},{6,7},{7,6},{8,9},{9,8},{10,11... | collective-permute-start | bytes 589832 | tf_op jit(solution)/shard_map/ppermute | solution.py:31
  21.9 19.9 %collective-permute-start.8 = (bf16[264,384]{1,0:T(8,128)(2,1)S(1)}, bf16[264,384]{1,0:T(8,128)(2,1)S(1)}, u32[]{:S(2)}, u32[]{:S(2)}) collective-permute-start(bf16[264,384]{1,0:T(8,128)(2,1)S(1)} %get-tuple-element.66), channel_id=1, source_target_pairs={{0,16},{4,20},{8,24},{12,28},{1,17},{5,21},{9,25},{13,29},{2,18},{... | collective-permute-start | bytes 608264 | tf_op jit(solution)/shard_map/ppermute | solution.py:27
  28.6 15.1 %collective-permute-start.10 = (bf16[264,384]{1,0:T(8,128)(2,1)S(1)}, bf16[264,384]{1,0:T(8,128)(2,1)S(1)}, u32[]{:S(2)}, u32[]{:S(2)}) collective-permute-start(bf16[264,384]{1,0:T(8,128)(2,1)S(1)} %collective-permute-done.9), channel_id=1, source_target_pairs={{0,8},{4,4},{8,16},{12,12},{16,24},{20,20},{24,0},{28,28},{1,9},{5... | collective-permute-start | bytes 608264 | tf_op jit(solution)/shard_map/ppermute | solution.py:500
  38.3 6.9 %collective-permute-start.12 = (bf16[256,384]{1,0:T(8,128)(2,1)S(1)}, bf16[256,384]{1,0:T(8,128)(2,1)S(1)}, u32[]{:S(2)}, u32[]{:S(2)}) collective-permute-start(bf16[256,384]{1,0:T(8,128)(2,1)S(1)} %get-tuple-element.71.refs_2_), channel_id=1, source_target_pairs={{0,2},{1,3},{2,0},{3,1},{4,6},{5,7},{6,4},{7,5},{8,10},{9,11},{10,... | collective-permute-start | bytes 589832 | tf_op jit(solution)/shard_map/ppermute | solution.py:31
  42.1 7.8 %collective-permute-start.15 = (bf16[256,384]{1,0:T(8,128)(2,1)S(1)}, bf16[256,384]{1,0:T(8,128)(2,1)S(1)}, u32[]{:S(2)}, u32[]{:S(2)}) collective-permute-start(bf16[256,384]{1,0:T(8,128)(2,1)S(1)} %get-tuple-element.82.refs_2_), channel_id=1, source_target_pairs={{0,2},{1,3},{2,0},{3,1},{4,6},{5,7},{6,4},{7,5},{8,10},{9,11},{10,... | collective-permute-start | bytes 589832 | tf_op jit(solution)/shard_map/ppermute | solution.py:31
  43.7 6.3 %collective-permute-start.11 = (bf16[256,384]{1,0:T(8,128)(2,1)S(1)}, bf16[256,384]{1,0:T(8,128)(2,1)S(1)}, u32[]{:S(2)}, u32[]{:S(2)}) collective-permute-start(bf16[256,384]{1,0:T(8,128)(2,1)S(1)} %get-tuple-element.71.refs_2_), channel_id=1, source_target_pairs={{0,1},{1,0},{2,3},{3,2},{4,5},{5,4},{6,7},{7,6},{8,9},{9,8},{10,11... | collective-permute-start | bytes 589832 | tf_op jit(solution)/shard_map/ppermute | solution.py:31
  44.0 9.0 %collective-permute-start.18 = (bf16[256,384]{1,0:T(8,128)(2,1)S(1)}, bf16[256,384]{1,0:T(8,128)(2,1)S(1)}, u32[]{:S(2)}, u32[]{:S(2)}) collective-permute-start(bf16[256,384]{1,0:T(8,128)(2,1)S(1)} %get-tuple-element.87.refs_2_), channel_id=1, source_target_pairs={{0,2},{1,3},{2,0},{3,1},{4,6},{5,7},{6,4},{7,5},{8,10},{9,11},{10,... | collective-permute-start | bytes 589832 | tf_op jit(solution)/shard_map/ppermute | solution.py:31
  45.3 7.7 %collective-permute-start.13 = (bf16[256,384]{1,0:T(8,128)(2,1)S(1)}, bf16[256,384]{1,0:T(8,128)(2,1)S(1)}, u32[]{:S(2)}, u32[]{:S(2)}) collective-permute-start(bf16[256,384]{1,0:T(8,128)(2,1)S(1)} %collective-permute-done.12.refs_4_), channel_id=1, source_target_pairs={{0,1},{1,0},{2,3},{3,2},{4,5},{5,4},{6,7},{7,6},{8,9},{9,8},{10,11... | collective-permute-start | bytes 589832 | tf_op jit(solution)/shard_map/ppermute | solution.py:31
  45.3 10.2 %collective-permute-start.14 = (bf16[256,384]{1,0:T(8,128)(2,1)S(1)}, bf16[256,384]{1,0:T(8,128)(2,1)S(1)}, u32[]{:S(2)}, u32[]{:S(2)}) collective-permute-start(bf16[256,384]{1,0:T(8,128)(2,1)S(1)} %get-tuple-element.82.refs_2_), channel_id=1, source_target_pairs={{0,1},{1,0},{2,3},{3,2},{4,5},{5,4},{6,7},{7,6},{8,9},{9,8},{10,11... | collective-permute-start | bytes 589832 | tf_op jit(solution)/shard_map/ppermute | solution.py:31
  49.9 5.5 %collective-permute-start.16 = (bf16[256,384]{1,0:T(8,128)(2,1)S(1)}, bf16[256,384]{1,0:T(8,128)(2,1)S(1)}, u32[]{:S(2)}, u32[]{:S(2)}) collective-permute-start(bf16[256,384]{1,0:T(8,128)(2,1)S(1)} %collective-permute-done.15.refs_4_), channel_id=1, source_target_pairs={{0,1},{1,0},{2,3},{3,2},{4,5},{5,4},{6,7},{7,6},{8,9},{9,8},{10,11... | collective-permute-start | bytes 589832 | tf_op jit(solution)/shard_map/ppermute | solution.py:31
  49.9 8.1 %collective-permute-start.17 = (bf16[256,384]{1,0:T(8,128)(2,1)S(1)}, bf16[256,384]{1,0:T(8,128)(2,1)S(1)}, u32[]{:S(2)}, u32[]{:S(2)}) collective-permute-start(bf16[256,384]{1,0:T(8,128)(2,1)S(1)} %get-tuple-element.87.refs_2_), channel_id=1, source_target_pairs={{0,1},{1,0},{2,3},{3,2},{4,5},{5,4},{6,7},{7,6},{8,9},{9,8},{10,11... | collective-permute-start | bytes 589832 | tf_op jit(solution)/shard_map/ppermute | solution.py:31
  52.9 5.1 %collective-permute-start.19 = (bf16[256,384]{1,0:T(8,128)(2,1)S(1)}, bf16[256,384]{1,0:T(8,128)(2,1)S(1)}, u32[]{:S(2)}, u32[]{:S(2)}) collective-permute-start(bf16[256,384]{1,0:T(8,128)(2,1)S(1)} %collective-permute-done.18.refs_4_), channel_id=1, source_target_pairs={{0,1},{1,0},{2,3},{3,2},{4,5},{5,4},{6,7},{7,6},{8,9},{9,8},{10,11... | collective-permute-start | bytes 589832 | tf_op jit(solution)/shard_map/ppermute | solution.py:31
  61.5 11.6 %collective-permute-start.24 = (bf16[768,256]{1,0:T(8,128)(2,1)S(1)}, bf16[768,256]{1,0:T(8,128)(2,1)S(1)}, u32[]{:S(2)}, u32[]{:S(2)}) collective-permute-start(bf16[768,256]{1,0:T(8,128)(2,1)S(1)} %get-tuple-element.100), channel_id=1, source_target_pairs={{0,8},{4,12},{8,0},{12,4},{16,24},{20,28},{24,16},{28,20},{1,9},{5... | collective-permute-start | bytes 1179656 | tf_op jit(solution)/shard_map/ppermute | solution.py:31
  61.9 11.5 %collective-permute-start.22 = (bf16[768,256]{1,0:T(8,128)(2,1)S(1)}, bf16[768,256]{1,0:T(8,128)(2,1)S(1)}, u32[]{:S(2)}, u32[]{:S(2)}) collective-permute-start(bf16[768,256]{1,0:T(8,128)(2,1)S(1)} %get-tuple-element.98), channel_id=1, source_target_pairs={{0,4},{4,0},{8,12},{12,8},{16,20},{20,16},{24,28},{28,24},{1,5},{5... | collective-permute-start | bytes 1179656 | tf_op jit(solution)/shard_map/ppermute | solution.py:31
  63.3 11.8 %collective-permute-start.20 = (bf16[2,1,256,384]{3,2,1,0:T(8,128)(2,1)S(1)}, bf16[2,1,256,384]{3,2,1,0:T(8,128)(2,1)S(1)}, u32[]{:S(2)}, u32[]{:S(2)}) collective-permute-start(bf16[2,1,256,384]{3,2,1,0:T(8,128)(2,1)S(1)} %constant_dynamic-slice_fusion.5), channel_id=1, source_target_pairs={{0,1},{1,0},{2,3},{3,2},{4,5},{5,4},{6,7},{7,6},{8,9},{9,8},{10,11... | collective-permute-start | bytes 1179656 | tf_op jit(solution)/shard_map/ppermute | solution.py:31
  73.3 6.5 %collective-permute-start.25 = (bf16[384,256]{1,0:T(8,128)(2,1)S(1)}, bf16[384,256]{1,0:T(8,128)(2,1)S(1)}, u32[]{:S(2)}, u32[]{:S(2)}) collective-permute-start(bf16[384,256]{1,0:T(8,128)(2,1)S(1)} %bitcast.27), channel_id=1, source_target_pairs={{0,4},{4,0},{8,12},{12,8},{16,20},{20,16},{24,28},{28,24},{1,5},{5... | collective-permute-start | bytes 589832 | tf_op jit(solution)/shard_map/ppermute | solution.py:31
  73.5 6.5 %collective-permute-start.23 = (bf16[384,256]{1,0:T(8,128)(2,1)S(1)}, bf16[384,256]{1,0:T(8,128)(2,1)S(1)}, u32[]{:S(2)}, u32[]{:S(2)}) collective-permute-start(bf16[384,256]{1,0:T(8,128)(2,1)S(1)} %bitcast.28), channel_id=1, source_target_pairs={{0,8},{4,12},{8,0},{12,4},{16,24},{20,28},{24,16},{28,20},{1,9},{5... | collective-permute-start | bytes 589832 | tf_op jit(solution)/shard_map/ppermute | solution.py:31
  75.2 7.1 %collective-permute-start.21 = (bf16[1,1,256,384]{3,2,1,0:T(8,128)(2,1)S(1)}, bf16[1,1,256,384]{3,2,1,0:T(8,128)(2,1)S(1)}, u32[]{:S(2)}, u32[]{:S(2)}) collective-permute-start(bf16[1,1,256,384]{3,2,1,0:T(8,128)(2,1)S(1)} %constant_dynamic-slice_fusion.4), channel_id=1, source_target_pairs={{0,2},{1,3},{2,0},{3,1},{4,6},{5,7},{6,4},{7,5},{8,10},{9,11},{10,... | collective-permute-start | bytes 589832 | tf_op jit(solution)/shard_map/ppermute | solution.py:31
  80.6 10.7 %collective-permute-start.26 = (bf16[384,256]{1,0:T(8,128)(2,1)S(1)}, bf16[384,256]{1,0:T(8,128)(2,1)S(1)}, u32[]{:S(2)}, u32[]{:S(2)}) collective-permute-start(bf16[384,256]{1,0:T(8,128)(2,1)S(1)} %get-tuple-element.102), channel_id=1, source_target_pairs={{0,16},{4,20},{8,24},{12,28},{16,0},{20,4},{24,8},{28,12},{1,17},{... | collective-permute-start | bytes 589832 | tf_op jit(solution)/shard_map/ppermute | solution.py:31
